TPU v7x, 8 devices: a whole 2x2x1 slice. The times are simulated.
8 devices in a mesh: graph: 8 (over z, y, x, core).
Axes of the slice: x: 2, y: 2, z: 1, core: 2. Of those that a mesh axis runs over, the one named last changes fastest.
Arguments:
- node_feats: bfloat16 [16384, 200], P('graph')
- w_one: float32 [200, 512], replicated
- w_two: float32 [512, 107], replicated
- send_idx: int32 [16, 1024], P('graph')
- edge_src: int32 [65536], P('graph')
- edge_dst: int32 [65536], P('graph')
- edge_w: float32 [65536], P('graph')
- labels: int32 [16384], P('graph')
- label_mask: int32 [16384], P('graph')
Outputs:
- output 1: float32 [], replicated
- output 2: float32 [200, 512], replicated
- output 3: float32 [512, 107], replicated
All inputs are finite; a program needn't handle non-finite values.
Results may differ from a plain program's by a relative error of at most 0.001.
Values are sent between devices in bfloat16 or wider.
A program may use at most 1 GiB of HBM per device.

v0:
```python
import jax
import jax.numpy as jnp
from jax import lax
from jax.sharding import PartitionSpec as P

GRAPH_AXIS = "graph"
CONTRACT_ROWS = (((0,), (0,)), ((), ()))
CONTRACT_COLS = (((1,), (1,)), ((), ()))


def solution(mesh):
    num_dev = mesh.shape[GRAPH_AXIS]
    to_next = [(dev_id, (dev_id + 1) % num_dev) for dev_id in range(num_dev)]
    to_prev = [(dev_id, (dev_id - 1) % num_dev) for dev_id in range(num_dev)]

    def halo_extend(node_table, send_rows):
        from_prev = lax.ppermute(node_table[send_rows[1]], GRAPH_AXIS, to_next)
        from_next = lax.ppermute(node_table[send_rows[0]], GRAPH_AXIS, to_prev)
        return jnp.concatenate([node_table, from_prev, from_next], axis=0)

    def aggregate(ext_table, edge_src, edge_dst, edge_w, rows_loc):
        return jax.ops.segment_sum(edge_w[:, None] * ext_table[edge_src], edge_dst, num_segments=rows_loc)

    def scatter_back(grad_rows, send_rows, edge_src, edge_dst, edge_w):
        rows_loc = grad_rows.shape[0]
        halo_rows = send_rows.shape[1]
        ext_grad = jax.ops.segment_sum(edge_w[:, None] * grad_rows[edge_dst], edge_src, num_segments=rows_loc + 2 * halo_rows)
        back_prev = lax.ppermute(ext_grad[rows_loc:rows_loc + halo_rows], GRAPH_AXIS, to_prev)
        back_next = lax.ppermute(ext_grad[rows_loc + halo_rows:], GRAPH_AXIS, to_next)
        row_ids = jnp.concatenate([send_rows[1], send_rows[0]])
        return ext_grad[:rows_loc].at[row_ids].add(jnp.concatenate([back_prev, back_next], axis=0))

    def device_step(node_feats, w_one, w_two, send_rows, edge_src, edge_dst, edge_w, labels, label_mask):
        rows_loc = node_feats.shape[0]
        w_one_b = w_one.astype(jnp.bfloat16)
        w_two_b = w_two.astype(jnp.bfloat16)
        tab_one = jnp.dot(node_feats, w_one_b, preferred_element_type=jnp.float32).astype(jnp.bfloat16)
        pre_one = aggregate(halo_extend(tab_one, send_rows), edge_src, edge_dst, edge_w, rows_loc)
        hidden = jnp.maximum(pre_one, 0.0).astype(jnp.bfloat16)
        tab_two = jnp.dot(hidden, w_two_b, preferred_element_type=jnp.float32).astype(jnp.bfloat16)
        logits = aggregate(halo_extend(tab_two, send_rows), edge_src, edge_dst, edge_w, rows_loc)
        mask_f = label_mask.astype(jnp.float32)
        label_count = jnp.maximum(lax.psum(jnp.sum(mask_f), GRAPH_AXIS), 1.0)
        log_norm = jax.nn.logsumexp(logits, axis=1)
        one_hot = (labels[:, None] == jnp.arange(logits.shape[1])[None, :]).astype(jnp.float32)
        picked = jnp.sum(logits * one_hot, axis=1)
        mean_loss = lax.psum(jnp.sum(mask_f * (log_norm - picked)), GRAPH_AXIS) / label_count
        d_logits = (jnp.exp(logits - log_norm[:, None]) - one_hot) * (mask_f / label_count)[:, None]
        d_tab_two = scatter_back(d_logits, send_rows, edge_src, edge_dst, edge_w).astype(jnp.bfloat16)
        grad_two = lax.psum(lax.dot_general(hidden, d_tab_two, CONTRACT_ROWS, preferred_element_type=jnp.float32), GRAPH_AXIS)
        d_hidden = lax.dot_general(d_tab_two, w_two_b, CONTRACT_COLS, preferred_element_type=jnp.float32)
        d_pre = jnp.where(pre_one > 0.0, d_hidden, 0.0)
        d_tab_one = scatter_back(d_pre, send_rows, edge_src, edge_dst, edge_w).astype(jnp.bfloat16)
        grad_one = lax.psum(lax.dot_general(node_feats, d_tab_one, CONTRACT_ROWS, preferred_element_type=jnp.float32), GRAPH_AXIS)
        return mean_loss, grad_one, grad_two

    row_spec = P(GRAPH_AXIS)
    return jax.shard_map(device_step, mesh=mesh, in_specs=(row_spec, P(), P(), row_spec, row_spec, row_spec, row_spec, row_spec, row_spec), out_specs=(P(), P(), P()), check_vma=False)
```

profile of v0, /device:TPU:0, one launch (start us, length us, event | category | flops | bytes accessed | tf_op | source)
XLA Modules:
  0.0 654.6 jit_solution(110695086110357597)
XLA Ops:
  10.1 5.1 gather_fusion
  16.1 5.1 gather_fusion.1
  24.1 10.9 %collective-permute-done = bf16[1024,512]{1,0:T(8,128)(2,1)} collective-permute-done((bf16[1024,512]{1,0:T(8,128)(2,1)}, bf16[1024,512]{1,0:T(8,128)(2,1)}, u32[]{:S(2)}, u32[]{:S(2)}) %collective-permute-start) | collective-permute-done | bytes 1048608 | tf_op jit(solution)/shard_map/ppermute | solution.py:17
  35.0 6.5 collective-permute-done.1
  41.5 9.3 %pad_maximum_fusion = bf16[4096,512]{1,0:T(8,128)(2,1)} fusion(bf16[1024,512]{1,0:T(8,128)(2,1)S(1)} %collective-permute-done.1, bf16[1024,512]{1,0:T(8,128)(2,1)} %collective-permute-done, bf16[2048,512]{1,0:T(8,128)(2,1)S(1)} %convolution_convert_fusion), kind=kLoop, calls=%fused_computation.21 | loop fusion | flops 12582912 | bytes 8388608 | tf_op jit(solution)/shard_map/concatenate | solution.py:19
  50.8 111.4 %scatter_custom_fusion = f32[2048,512]{1,0:T(8,128)} fusion(s32[8192]{0:T(1024)S(1)} %copy-done.9, f32[8192]{0:T(1024)S(1)} %copy-done.5, f32[]{:T(128)} %constant.6.clone.1, bf16[4096,512]{1,0:T(8,128)(2,1)} %pad_maximum_fusion, s32[8192]{0:T(1024)S(1)} %fusion.37), kind=kCustom, calls=%fused_computation.16 | custom fusion | flops 12582912 | bytes 8454148 | tf_op jit(solution)/shard_map/scatter-add | solution.py:22
  162.2 3.0 convolution_convert_fusion.1
  165.5 3.2 gather_fusion.3
  168.7 3.2 gather_fusion.2
  172.3 2.9 collective-permute-start.3
  175.2 6.0 collective-permute-done.3
  184.2 73.0 %scatter_custom_fusion.1 = f32[2048,107]{1,0:T(8,128)S(1)} fusion(s32[8192]{0:T(1024)S(1)} %copy-done.9, f32[8192]{0:T(1024)S(1)} %copy-done.5, f32[]{:T(128)} %constant.6.clone.1, bf16[4096,107]{1,0:T(8,128)(2,1)S(1)} %copy.21, s32[8192]{0:T(1024)S(1)} %fusion.37), kind=kCustom, calls=%fused_computation.29 | custom fusion | flops 2629632 | bytes 1990660 | tf_op jit(solution)/shard_map/scatter-add | solution.py:22
  259.5 22.6 %all-reduce = (f32[]{:T(128)}, f32[]{:T(128)}) all-reduce(f32[]{:T(128)} %get-tuple-element.6, f32[]{:T(128)} %get-tuple-element.5), channel_id=1, replica_groups=mesh['graph'=8] {'graph'}, use_global_device_ids=true, to_apply=%region_6.0 | all-reduce | flops 2 | bytes 16 | tf_op jit(solution)/shard_map/psum | solution.py:47
  285.2 94.5 %scatter_custom_fusion.2 = f32[4096,107]{1,0:T(8,128)S(1)} fusion(s32[8192]{0:T(1024)S(1)} %copy-done.10, f32[8192]{0:T(1024)S(1)} %copy-done.5, f32[]{:T(128)} %constant.6.clone.1, f32[2048,107]{1,0:T(8,128)} %subtract_multiply_fusion, s32[8192]{0:T(1024)S(1)} %fusion.38), kind=kCustom, calls=%fused_computation.26 | custom fusion | flops 1753088 | bytes 2695172 | tf_op jit(solution)/shard_map/scatter-add | solution.py:27
  382.4 10.3 %collective-permute-done.4 = f32[1024,107]{1,0:T(8,128)S(1)} collective-permute-done((f32[1024,107]{1,0:T(8,128)S(1)}, f32[1024,107]{1,0:T(8,128)S(1)}, u32[]{:S(2)}, u32[]{:S(2)}) %collective-permute-start.4) | collective-permute-done | bytes 438304 | tf_op jit(solution)/shard_map/ppermute | solution.py:28
  392.7 3.5 collective-permute-done.5
  397.0 12.8 %scatter_custom_fusion.3 = f32[2048,107]{1,0:T(8,128)S(1)} fusion(f32[2048,107]{1,0:T(8,128)S(1)} %slice.54, s32[2048]{0:T(1024)S(1)} %bitcast.17, f32[1024,107]{1,0:T(8,128)} %copy-done.7, f32[]{:T(128)} %constant.10.clone.1, f32[1024,107]{1,0:T(8,128)} %copy-done.6), kind=kCustom, calls=%fused_computation.42 | custom fusion | flops 438272 | bytes 1753092 | tf_op jit(solution)/shard_map/scatter-add | solution.py:31
  409.7 4.8 compare_select_fusion
  414.6 111.6 %scatter_custom_fusion.4 = f32[4096,512]{1,0:T(8,128)} fusion(s32[8192]{0:T(1024)S(1)} %copy-done.10, f32[8192]{0:T(1024)S(1)} %copy-done.5, f32[]{:T(128)} %constant.6.clone.1, f32[2048,512]{1,0:T(8,128)} %compare_select_fusion, s32[8192]{0:T(1024)S(1)} %fusion.38), kind=kCustom, calls=%fused_computation.14 | custom fusion | flops 8388608 | bytes 12648452 | tf_op jit(solution)/shard_map/scatter-add | solution.py:27
  534.4 40.5 %collective-permute-done.6 = f32[1024,512]{1,0:T(8,128)} collective-permute-done((f32[1024,512]{1,0:T(8,128)S(1)}, f32[1024,512]{1,0:T(8,128)}, u32[]{:S(2)}, u32[]{:S(2)}) %collective-permute-start.6) | collective-permute-done | bytes 2097184 | tf_op jit(solution)/shard_map/ppermute | solution.py:28
  574.9 3.1 collective-permute-done.7
  578.0 17.9 %scatter_custom_fusion.5 = f32[2048,512]{1,0:T(8,128)} fusion(f32[2048,512]{1,0:T(8,128)} %slice.57, s32[2048]{0:T(1024)S(1)} %bitcast.18, f32[1024,512]{1,0:T(8,128)} %collective-permute-done.7, f32[]{:T(128)} %constant.10.clone.1, f32[1024,512]{1,0:T(8,128)} %collective-permute-done.6), kind=kCustom, calls=%fused_computation.22 | custom fusion | flops 2097152 | bytes 8389120 | tf_op jit(solution)/shard_map/scatter-add | solution.py:31
  595.9 3.5 fusion.22
  600.0 42.8 %all-reduce.4.cloned.1.call-done = (f32[200,512]{1,0:T(8,128)}, f32[512,107]{0,1:T(8,128)}) async-done(((f32[200,512]{1,0:T(8,128)}, f32[512,107]{0,1:T(8,128)}), (f32[200,512]{1,0:T(8,128)}, f32[512,107]{0,1:T(8,128)})) %all-reduce.4.cloned.1.call-update) | async-done | bytes 628752 | tf_op jit(solution)/shard_map/psum | solution.py:54
  (62 shorter events, 30.1 us)
Async XLA Ops:
  7.2 1.2 copy-start
  7.2 635.6 %all-reduce.4.cloned.1.call-start = ((), (), s32[]{:S(2)}) async-start(), calls=%async_computation | async-start | bytes 1277952 | tf_op jit(solution)/shard_map/psum | solution.py:54
  15.2 19.8 %collective-permute-start = (bf16[1024,512]{1,0:T(8,128)(2,1)}, bf16[1024,512]{1,0:T(8,128)(2,1)}, u32[]{:S(2)}, u32[]{:S(2)}) collective-permute-start(bf16[1024,512]{1,0:T(8,128)(2,1)} %gather_fusion), channel_id=1, source_target_pairs={{0,1},{1,2},{2,3},{3,4},{4,5},{5,6},{6,7},{7,0}} | collective-permute-start | bytes 3145736 | tf_op jit(solution)/shard_map/ppermute | solution.py:17
  16.0 8.0 %copy-start.10 = (s32[8192]{0:T(1024)S(1)}, s32[8192]{0:T(1024)}, u32[]{:S(2)}) copy-start(s32[8192]{0:T(1024)} %param.13) | copy-start | bytes 98308
  21.1 20.4 %collective-permute-start.1 = (bf16[1024,512]{1,0:T(8,128)(2,1)}, bf16[1024,512]{1,0:T(8,128)(2,1)S(1)}, u32[]{:S(2)}, u32[]{:S(2)}) collective-permute-start(bf16[1024,512]{1,0:T(8,128)(2,1)} %gather_fusion.1), channel_id=1, source_target_pairs={{0,7},{1,0},{2,1},{3,2},{4,3},{5,4},{6,5},{7,6}} | collective-permute-start | bytes 3145736 | tf_op jit(solution)/shard_map/ppermute | solution.py:18
  24.0 26.7 %copy-start.5 = (f32[8192]{0:T(1024)S(1)}, f32[8192]{0:T(1024)}, u32[]{:S(2)}) copy-start(f32[8192]{0:T(1024)} %param.15) | copy-start | bytes 98308
  24.0 26.7 %copy-start.9 = (s32[8192]{0:T(1024)S(1)}, s32[8192]{0:T(1024)}, u32[]{:S(2)}) copy-start(s32[8192]{0:T(1024)} %param.14) | copy-start | bytes 98308
  50.8 111.4 %copy-start.4 = (f32[512,107]{0,1:T(8,128)S(1)}, f32[512,107]{0,1:T(8,128)}, u32[]{:S(2)}) copy-start(f32[512,107]{0,1:T(8,128)} %param.11) | copy-start | bytes 657412
  171.9 85.7 %copy-start.8 = (s32[2048]{0:T(1024)S(1)}, s32[2048]{0:T(1024)}, u32[]{:S(2)}) copy-start(s32[2048]{0:T(1024)} %param.16) | copy-start | bytes 24580
  172.3 86.6 %copy-start.12 = (s32[2048]{0:T(1024)S(1)}, s32[2048]{0:T(1024)}, u32[]{:S(2)}) copy-start(s32[2048]{0:T(1024)} %param.17) | copy-start | bytes 24580
  172.3 8.9 %collective-permute-start.3 = (bf16[1024,107]{0,1:T(8,128)(2,1)S(1)}, bf16[1024,107]{0,1:T(8,128)(2,1)S(1)}, u32[]{:S(2)}, u32[]{:S(2)}) collective-permute-start(bf16[1024,107]{0,1:T(8,128)(2,1)S(1)} %copy.20), channel_id=1, source_target_pairs={{0,7},{1,0},{2,1},{3,2},{4,3},{5,4},{6,5},{7,6}} | collective-permute-start | bytes 657416 | tf_op jit(solution)/shard_map/ppermute | solution.py:18
  175.2 6.3 collective-permute-start.2
  257.6 123.4 %copy-start.11 = (s32[2,1024]{1,0:T(2,128)S(1)}, s32[2,1024]{1,0:T(2,128)}, u32[]{:S(2)}) copy-start(s32[2,1024]{1,0:T(2,128)} %param.12) | copy-start | bytes 24580
  379.7 1.4 copy-start.3
  379.8 12.9 %collective-permute-start.4 = (f32[1024,107]{1,0:T(8,128)S(1)}, f32[1024,107]{1,0:T(8,128)S(1)}, u32[]{:S(2)}, u32[]{:S(2)}) collective-permute-start(f32[1024,107]{1,0:T(8,128)S(1)} %get-tuple-element.14), channel_id=1, source_target_pairs={{0,7},{1,0},{2,1},{3,2},{4,3},{5,4},{6,5},{7,6}} | collective-permute-start | bytes 1314824 | tf_op jit(solution)/shard_map/ppermute | solution.py:28
  381.0 15.2 %collective-permute-start.5 = (f32[1024,107]{1,0:T(8,128)S(1)}, f32[1024,107]{1,0:T(8,128)S(1)}, u32[]{:S(2)}, u32[]{:S(2)}) collective-permute-start(f32[1024,107]{1,0:T(8,128)S(1)} %get-tuple-element.15), channel_id=1, source_target_pairs={{0,1},{1,2},{2,3},{3,4},{4,5},{5,6},{6,7},{7,0}} | collective-permute-start | bytes 1314824 | tf_op jit(solution)/shard_map/ppermute | solution.py:29
  392.7 3.5 copy-start.6
  396.2 0.8 copy-start.7
  526.2 4.6 copy-start.2
  529.0 45.9 %collective-permute-start.6 = (f32[1024,512]{1,0:T(8,128)S(1)}, f32[1024,512]{1,0:T(8,128)}, u32[]{:S(2)}, u32[]{:S(2)}) collective-permute-start(f32[1024,512]{1,0:T(8,128)S(1)} %get-tuple-element.12), channel_id=1, source_target_pairs={{0,7},{1,0},{2,1},{3,2},{4,3},{5,4},{6,5},{7,6}} | collective-permute-start | bytes 6291464 | tf_op jit(solution)/shard_map/ppermute | solution.py:28
  529.3 4.0 copy-start.1
  529.3 48.7 %collective-permute-start.7 = (f32[1024,512]{1,0:T(8,128)S(1)}, f32[1024,512]{1,0:T(8,128)}, u32[]{:S(2)}, u32[]{:S(2)}) collective-permute-start(f32[1024,512]{1,0:T(8,128)S(1)} %get-tuple-element.13), channel_id=1, source_target_pairs={{0,1},{1,2},{2,3},{3,4},{4,5},{5,6},{6,7},{7,0}} | collective-permute-start | bytes 6291464 | tf_op jit(solution)/shard_map/ppermute | solution.py:29
Sparse Core Ops, SparseCore 0:
  599.5 43.1 all-reduce.3
where the time goes:
time: 665 us; the launch traced here: 655 us
  other arithmetic  437 us (66%)
  waiting for transfers between devices  124 us (19%)
  local copies, waits for them, and re-layouts  31.3 us (5%)
  blocking collectives  22.6 us (3%)
  between operations  17.1 us (3%)
  matrix products  14.3 us (2%)
  starting transfers between devices  8.46 us (1%)
    scatter-add x2, other arithmetic, scatter_back(): jax.ops.segment_sum(edge_w[:, None] * grad_rows[edge_dst], edge_src, num_...  206 us
    scatter-add x2, other arithmetic, aggregate(): jax.ops.segment_sum(edge_w[:, None] * ext_table[edge_src], edge_dst, num_...  184 us
    ppermute x2, waiting for transfers between devices, scatter_back(): lax.ppermute(ext_grad[rows_loc:rows_loc + halo_rows], GRAPH_AXIS, to_prev)  50.8 us
    psum x1, waiting for transfers between devices, device_step(): lax.psum(lax.dot_general(node_feats, d_tab_one, CONTRACT_ROWS, preferred_...  42.8 us
    scatter-add x2, other arithmetic, scatter_back(): ext_grad[:rows_loc].at[row_ids]  30.6 us
    psum x1, blocking collectives, device_step(): lax.psum(jnp.sum(mask_f * (log_norm - picked)), GRAPH_AXIS) / label_count  22.6 us
  transfers between devices with their start and end apart: 9, of which 9 were waited for; matrix products, arithmetic and copies ran while one was open for 2% of the time, Pallas kernels for 0%

commit v1 on v0

v1 whole, which is shorter than its diff:
```python
import functools

import jax
import jax.numpy as jnp
from jax import lax
from jax.experimental import pallas as pl
from jax.experimental.pallas import tpu as pltpu
from jax.sharding import PartitionSpec as P

GRAPH_AXIS = "graph"
CONTRACT_ROWS = (((0,), (0,)), ((), ()))
MESH = pl.DeviceIdType.MESH
F32 = jnp.float32
BF16 = jnp.bfloat16
LANES = 128
CHUNK = 256
SLOT = 384
VMEM_LIMIT = 64000000

SMEM_SPEC = pl.BlockSpec(memory_space=pltpu.SMEM)
VMEM_SPEC = pl.BlockSpec(memory_space=pltpu.VMEM)


def params(**kw):
    return pltpu.CompilerParams(vmem_limit_bytes=VMEM_LIMIT, **kw)


def zero_rows(refs):
    rows = refs[0].shape[0]

    def body(i, _):
        for ref in refs:
            ref[pl.ds(i * 64, 64), :] = jnp.zeros((64, LANES), F32)
        return 0

    lax.fori_loop(0, rows // 64, body, 0)


def sum_rows(out, refs):
    rows = refs[0].shape[0]

    def body(i, _):
        total = refs[0][pl.ds(i * 64, 64), :]
        for ref in refs[1:]:
            total = total + ref[pl.ds(i * 64, 64), :]
        out[pl.ds(i * 64, 64), :] = total
        return 0

    lax.fori_loop(0, rows // 64, body, 0)


def edge_pass(from_ref, to_ref, w_ref, cnt_ref, table, accs, width, unroll, back):
    n_acc = len(accs)
    shift = unroll.bit_length() - 1

    def row(r, _):
        blocks = lax.shift_right_logical(cnt_ref[r] + (unroll - 1), shift)

        def body(j, _):
            off = r * SLOT + (SLOT - unroll - j * unroll if back else j * unroll)
            vals = [table[pl.ds(pl.multiple_of(from_ref[off + u], width), width), :] * w_ref[off + u] for u in range(unroll)]
            for g in range(unroll // n_acc):
                rows = [pl.multiple_of(to_ref[off + g * n_acc + k], width) for k in range(n_acc)]
                old = [accs[k][pl.ds(rows[k], width), :] for k in range(n_acc)]
                for k in range(n_acc):
                    accs[k][pl.ds(rows[k], width), :] = old[k] + vals[g * n_acc + k]
            return 0

        lax.fori_loop(0, blocks, body, 0)
        return 0

    lax.fori_loop(0, cnt_ref.shape[0], row, 0)


def scatter_pass(ids_ref, table, accs, width, unroll):
    n_acc = len(accs)

    def body(j, _):
        off = j * unroll
        for g in range(unroll // n_acc):
            rows = [pl.multiple_of(ids_ref[off + g * n_acc + k], width) for k in range(n_acc)]
            vals = [table[pl.ds(pl.multiple_of((off + g * n_acc + k) * width, width), width), :] for k in range(n_acc)]
            old = [accs[k][pl.ds(rows[k], width), :] for k in range(n_acc)]
            for k in range(n_acc):
                accs[k][pl.ds(rows[k], width), :] = old[k] + vals[k]
        return 0

    lax.fori_loop(0, ids_ref.shape[0] // unroll, body, 0)


def gather_pass(ids_ref, table, out, width, unroll=8):
    def body(j, _):
        for u in range(unroll):
            i = j * unroll + u
            out[pl.ds(pl.multiple_of(i * width, width), width), :] = table[pl.ds(pl.multiple_of(ids_ref[i], width), width), :]
        return 0

    lax.fori_loop(0, ids_ref.shape[0] // unroll, body, 0)


def spread(table, start, block):
    tiles = block.shape[1] // LANES
    for c in range(tiles):
        table[pl.ds(start * tiles + c, block.shape[0], tiles), :] = block[:, c * LANES:(c + 1) * LANES]


def unspread(table, start, rows, tiles):
    return jnp.concatenate([table[pl.ds(start * tiles + c, rows, tiles), :] for c in range(tiles)], axis=1)


def halo_rows_kernel(ids2, x, to_next, to_prev, table, picked):
    rows = x.shape[0]

    def put(i, _):
        spread(table, i * 256, x[pl.ds(i * 256, 256), :].astype(F32))
        return 0

    lax.fori_loop(0, rows // 256, put, 0)
    gather_pass(ids2, table, picked, 2)
    half = to_next.shape[0]

    def take(i, _):
        to_next[pl.ds(i * 256, 256), :] = unspread(picked, i * 256, 256, 2).astype(BF16)
        to_prev[pl.ds(i * 256, 256), :] = unspread(picked, half + i * 256, 256, 2).astype(BF16)
        return 0

    lax.fori_loop(0, half // 256, take, 0)


def one_own_kernel(s4, d4, w, cnt, x, w1, y, table, *accs):
    zero_rows(accs)

    def put(i, _):
        t = jnp.dot(x[pl.ds(i * 256, 256), :], w1[...], preferred_element_type=F32)
        spread(table, i * 256, t.astype(BF16).astype(F32))
        return 0

    lax.fori_loop(0, x.shape[0] // 256, put, 0)
    edge_pass(s4, d4, w, cnt, table, accs, 4, 16, False)
    sum_rows(y, accs)


def one_halo_kernel(s4, d4, w, cnt, ids, y_own, x_prev, x_next, w1, w2, hid, t2, to_next, to_prev, table, picked, *accs):
    zero_rows(accs)
    half = x_prev.shape[0]

    def put(i, _):
        t = jnp.dot(x_prev[pl.ds(i * 256, 256), :], w1[...], preferred_element_type=F32)
        spread(table, i * 256, t.astype(BF16).astype(F32))
        t = jnp.dot(x_next[pl.ds(i * 256, 256), :], w1[...], preferred_element_type=F32)
        spread(table, half + i * 256, t.astype(BF16).astype(F32))
        return 0

    lax.fori_loop(0, half // 256, put, 0)
    edge_pass(s4, d4, w, cnt, table, accs, 4, 8, True)
    sum_rows(accs[0], (y_own,) + accs)

    def act(i, _):
        h = jnp.maximum(unspread(accs[0], i * 256, 256, 4), 0.0).astype(BF16)
        hid[pl.ds(i * 256, 256), :] = h
        t = jnp.dot(h, w2[...], preferred_element_type=F32)
        t2[pl.ds(i * 256, 256), :] = t.astype(BF16).astype(F32)
        return 0

    lax.fori_loop(0, hid.shape[0] // 256, act, 0)
    gather_pass(ids, t2, picked, 1)

    def take(i, _):
        to_next[pl.ds(i * 256, 256), :] = picked[pl.ds(i * 256, 256), :].astype(BF16)
        to_prev[pl.ds(i * 256, 256), :] = picked[pl.ds(half + i * 256, 256), :].astype(BF16)
        return 0

    lax.fori_loop(0, half // 256, take, 0)


def narrow_own_kernel(frm, to, w, cnt, table, out, *accs):
    zero_rows(accs)
    edge_pass(frm, to, w, cnt, table, accs, 1, 16, False)
    sum_rows(out, accs)


def wide_own_kernel(frm, to, w, cnt, table, out, *accs):
    zero_rows(accs)
    edge_pass(frm, to, w, cnt, table, accs, 4, 16, False)
    sum_rows(out, accs)


def logits_kernel(classes, s, d, w, cnt, z_own, t_prev, t_next, labels, count, dz, back_prev, back_next, loss, table, *accs):
    zero_rows(accs)
    half = t_prev.shape[0]

    def put(i, _):
        table[pl.ds(i * 256, 256), :] = t_prev[pl.ds(i * 256, 256), :].astype(F32)
        table[pl.ds(half + i * 256, 256), :] = t_next[pl.ds(i * 256, 256), :].astype(F32)
        return 0

    lax.fori_loop(0, half // 256, put, 0)
    edge_pass(s, d, w, cnt, table, accs, 1, 8, True)
    scale = 1.0 / count[0:1, :]
    denom = count[0:1, :]
    loss[...] = jnp.zeros_like(loss)

    def soft(i, _):
        at = pl.ds(i * 64, 64)
        z = z_own[at, :]
        for acc in accs:
            z = z + acc[at, :]
        lane = lax.broadcasted_iota(jnp.int32, z.shape, 1)
        lab = labels[at, :]
        hot = lab == lane
        keep = lab >= 0
        zm = jnp.where(lane < classes, z, -jnp.inf)
        top = jnp.max(zm, axis=1, keepdims=True)
        ex = jnp.exp(zm - top)
        log_norm = jnp.log(jnp.sum(ex, axis=1, keepdims=True)) + top
        hot_f = jnp.where(hot, 1.0, 0.0)
        term = jnp.where(hot, log_norm - z, 0.0)
        part = term[0:8]
        for b in range(1, 8):
            part = part + term[b * 8:b * 8 + 8]
        loss[...] += part
        mask_f = jnp.where(keep, 1.0, 0.0)
        dz[at, :] = jnp.where(lane < classes, (jnp.exp(zm - log_norm) - hot_f) * (mask_f / denom), 0.0)
        return 0

    lax.fori_loop(0, dz.shape[0] // 64, soft, 0)
    zero_rows(accs)
    edge_pass(d, s, w, cnt, dz, accs, 1, 8, True)

    def fin(i, _):
        at = pl.ds(i * 64, 64)
        bt = pl.ds(half + i * 64, 64)
        a, b = accs[0][at, :], accs[0][bt, :]
        for acc in accs[1:]:
            a, b = a + acc[at, :], b + acc[bt, :]
        back_prev[at, :] = a
        back_next[at, :] = b
        return 0

    lax.fori_loop(0, half // 64, fin, 0)


def hidden_grad_kernel(s4, d4, w, cnt, ids, own, ret_next, ret_prev, hid, w2t, dt2, dy, back_prev, back_next, *accs):
    n_loc, half = own.shape[0], ret_next.shape[0]
    narrow = tuple(acc.at[pl.ds(0, n_loc)] for acc in accs)
    zero_rows(narrow)
    scatter_pass(ids.at[pl.ds(0, half)], ret_next, narrow, 1, 8)
    scatter_pass(ids.at[pl.ds(half, half)], ret_prev, narrow, 1, 8)

    def fold(i, _):
        at = pl.ds(i * 256, 256)
        total = own[at, :]
        for acc in narrow:
            total = total + acc[at, :]
        dt = total.astype(BF16)
        dt2[at, :] = dt
        dh = jnp.dot(dt, w2t[...], preferred_element_type=F32)
        spread(dy, i * 256, jnp.where(hid[at, :].astype(F32) > 0.0, dh, 0.0))
        return 0

    lax.fori_loop(0, n_loc // 256, fold, 0)
    zero_rows(accs)
    edge_pass(d4, s4, w, cnt, dy, accs, 4, 8, True)
    quad = 4 * half

    def fin(i, _):
        at = pl.ds(i * 64, 64)
        bt = pl.ds(quad + i * 64, 64)
        a, b = accs[0][at, :], accs[0][bt, :]
        for acc in accs[1:]:
            a, b = a + acc[at, :], b + acc[bt, :]
        back_prev[at, :] = a
        back_next[at, :] = b
        return 0

    lax.fori_loop(0, quad // 64, fin, 0)


def table_grad_kernel(ids4, own, ret_next, ret_prev, dt1, *accs):
    half = ids4.shape[0] // 2
    zero_rows(accs)
    scatter_pass(ids4.at[pl.ds(0, half)], ret_next, accs, 4, 8)
    scatter_pass(ids4.at[pl.ds(half, half)], ret_prev, accs, 4, 8)

    def fold(i, _):
        total = unspread(own, i * 128, 128, 4)
        for acc in accs:
            total = total + unspread(acc, i * 128, 128, 4)
        dt1[pl.ds(i * 128, 128), :] = total.astype(BF16)
        return 0

    lax.fori_loop(0, dt1.shape[0] // 128, fold, 0)


def enter(me, num_dev):
    barrier = pltpu.get_barrier_semaphore()
    for step in range(1, num_dev):
        pl.semaphore_signal(barrier, inc=1, device_id=(lax.rem(me + step, num_dev),), device_id_type=MESH)
    pl.semaphore_wait(barrier, num_dev - 1)


def push(src, dst, send_sem, recv_sem, dev):
    copy = pltpu.make_async_remote_copy(src_ref=src, dst_ref=dst, send_sem=send_sem, recv_sem=recv_sem, device_id=(dev,), device_id_type=MESH)
    copy.start()
    return copy


def count_kernel(num_dev, part, out, slots, send_sem, recv_sem):
    me = lax.axis_index(GRAPH_AXIS)
    enter(me, num_dev)
    copies = []
    for step in range(1, num_dev):
        copies.append(push(part, slots.at[step - 1], send_sem.at[step - 1], recv_sem.at[step - 1], lax.rem(me + step, num_dev)))
    for copy in copies:
        copy.wait()
    total = part[...]
    for step in range(num_dev - 1):
        total = total + slots[step]
    out[...] = total


def reduce_kernel(num_dev, g1, g2, loss, o1, o2, lo, r1, r2, s1, s2, q1, q2, lslots, sem_s, sem_r, lsem_s, lsem_r):
    me = lax.axis_index(GRAPH_AXIS)
    core = lax.rem(me, 2)
    chip = me // 2
    mate = me + 1 - 2 * core
    h1, h2 = g1.shape[0] // 2, g2.shape[0] // 2
    e1, e2 = h1 // 4, h2 // 4
    enter(me, num_dev)
    other = 1 - core
    pair = [
        push(g1.at[pl.ds(pl.multiple_of(other * h1, h1), h1)], r1, sem_s.at[0], sem_r.at[0], mate),
        push(g2.at[pl.ds(pl.multiple_of(other * h2, h2), h2)], r2, sem_s.at[1], sem_r.at[1], mate),
    ]
    scalar = []
    for step in range(1, num_dev):
        scalar.append(push(loss, lslots.at[step - 1], lsem_s.at[step - 1], lsem_r.at[step - 1], lax.rem(me + step, num_dev)))
    for copy in pair:
        copy.wait()
    s1[...] = g1[pl.ds(pl.multiple_of(core * h1, h1), h1), :] + r1[...]
    s2[...] = g2[pl.ds(pl.multiple_of(core * h2, h2), h2), :] + r2[...]
    spreads = []
    for step in range(1, 4):
        far = lax.rem(chip + step, 4)
        dev = far * 2 + core
        k = 2 * step
        spreads.append(push(s1.at[pl.ds(pl.multiple_of(far * e1, e1), e1)], q1.at[step - 1], sem_s.at[k], sem_r.at[k], dev))
        spreads.append(push(s2.at[pl.ds(pl.multiple_of(far * e2, e2), e2)], q2.at[step - 1], sem_s.at[k + 1], sem_r.at[k + 1], dev))
    for copy in spreads:
        copy.wait()
    mine1 = pl.ds(pl.multiple_of(core * h1 + chip * e1, e1), e1)
    mine2 = pl.ds(pl.multiple_of(core * h2 + chip * e2, e2), e2)
    t1 = s1[pl.ds(pl.multiple_of(chip * e1, e1), e1), :]
    t2 = s2[pl.ds(pl.multiple_of(chip * e2, e2), e2), :]
    for step in range(3):
        t1 = t1 + q1[step]
        t2 = t2 + q2[step]
    o1[mine1, :] = t1
    o2[mine2, :] = t2
    gathers = []
    for step in range(1, 4):
        dev = lax.rem(chip + step, 4) * 2 + core
        k = 6 + 2 * step
        gathers.append((push(o1.at[mine1], o1.at[mine1], sem_s.at[k], sem_r.at[k], dev), push(o2.at[mine2], o2.at[mine2], sem_s.at[k + 1], sem_r.at[k + 1], dev)))
    tails = [push(o1.at[mine1], o1.at[mine1], sem_s.at[14], sem_r.at[14], mate), push(o2.at[mine2], o2.at[mine2], sem_s.at[15], sem_r.at[15], mate)]
    for step in range(1, 4):
        near = lax.rem(chip + 4 - step, 4)
        at1 = pl.ds(pl.multiple_of(core * h1 + near * e1, e1), e1)
        at2 = pl.ds(pl.multiple_of(core * h2 + near * e2, e2), e2)
        for copy in gathers[step - 1]:
            copy.wait()
        k = 14 + 2 * step
        tails.append(push(o1.at[at1], o1.at[at1], sem_s.at[k], sem_r.at[k], mate))
        tails.append(push(o2.at[at2], o2.at[at2], sem_s.at[k + 1], sem_r.at[k + 1], mate))
    for copy in scalar:
        copy.wait()
    total = loss[...]
    for step in range(num_dev - 1):
        total = total + lslots[step]
    lo[...] = total
    for copy in tails:
        copy.wait()


def solution(mesh):
    num_dev = mesh.shape[GRAPH_AXIS]
    to_next = [(dev_id, (dev_id + 1) % num_dev) for dev_id in range(num_dev)]
    to_prev = [(dev_id, (dev_id - 1) % num_dev) for dev_id in range(num_dev)]

    def shift_next(a):
        return lax.ppermute(a, GRAPH_AXIS, to_next)

    def shift_prev(a):
        return lax.ppermute(a, GRAPH_AXIS, to_prev)

    def compact(edge_src, edge_dst, edge_w, n_loc):
        rows = edge_src.shape[0] // CHUNK
        src, dst, w = (a.reshape(rows, CHUNK) for a in (edge_src, edge_dst, edge_w))
        live = w != 0.0
        own = live & (src < n_loc)
        hal = live & (src >= n_loc)
        tri = (jnp.arange(CHUNK)[:, None] < jnp.arange(CHUNK)[None, :]).astype(BF16)
        both = jnp.concatenate([own, hal], axis=0).astype(BF16)
        rank = jnp.dot(both, tri, preferred_element_type=F32).astype(jnp.int32)
        place = jnp.where(own, rank[:rows], jnp.where(hal, SLOT - 1 - rank[rows:], SLOT))
        hit = place[:, :, None] == jnp.arange(SLOT)[None, None, :]
        code = jnp.where(src < n_loc, src, src - n_loc) + dst * n_loc
        code = jnp.sum(jnp.where(hit, code[:, :, None], 0), axis=1).reshape(-1)
        wc = jnp.sum(jnp.where(hit, w[:, :, None], 0.0), axis=1).reshape(-1)
        s, d = code % n_loc, code // n_loc
        counts = jnp.sum(both.astype(F32), axis=1).astype(jnp.int32)
        return s, d, s * 4, d * 4, wc, counts[:rows], counts[rows:]

    def device_step(node_feats, w_one, w_two, send_rows, edge_src, edge_dst, edge_w, labels, label_mask):
        n_loc, f_in = node_feats.shape
        halo = send_rows.shape[1]
        f_hid, classes = w_two.shape
        quad = 4 * n_loc
        sds = jax.ShapeDtypeStruct
        x = jnp.pad(node_feats, ((0, 0), (0, 256 - f_in)))
        w1 = jnp.pad(w_one.astype(BF16), ((0, 256 - f_in), (0, 0)))
        w2 = jnp.pad(w_two.astype(BF16), ((0, 0), (0, LANES - classes)))
        ids = jnp.concatenate([send_rows[1], send_rows[0]])
        x_next, x_prev = pl.pallas_call(
            halo_rows_kernel,
            out_shape=[sds((halo, 256), BF16)] * 2,
            in_specs=[SMEM_SPEC, VMEM_SPEC],
            out_specs=[VMEM_SPEC] * 2,
            scratch_shapes=[pltpu.VMEM((2 * n_loc, LANES), F32), pltpu.VMEM((4 * halo, LANES), F32)],
            compiler_params=params(),
            name="halo_rows",
        )(ids * 2, x)
        xh_prev = shift_next(x_next)
        xh_next = shift_prev(x_prev)
        mask_count = jnp.sum(label_mask.astype(F32))
        count = pl.pallas_call(
            functools.partial(count_kernel, num_dev),
            out_shape=sds((8, LANES), F32),
            in_specs=[VMEM_SPEC],
            out_specs=VMEM_SPEC,
            scratch_shapes=[pltpu.VMEM((num_dev - 1, 8, LANES), F32), pltpu.SemaphoreType.DMA((num_dev - 1,)), pltpu.SemaphoreType.DMA((num_dev - 1,))],
            compiler_params=params(collective_id=0, has_side_effects=True),
            name="count",
        )(jnp.broadcast_to(mask_count, (8, LANES)))
        count = jnp.maximum(count, 1.0)
        s, d, s4, d4, wc, n_own, n_hal = compact(edge_src, edge_dst, edge_w, n_loc)
        wide4 = [pltpu.VMEM((quad, LANES), F32)] * 4
        thin4 = [pltpu.VMEM((n_loc, LANES), F32)] * 4
        y_own = pl.pallas_call(
            one_own_kernel,
            out_shape=sds((quad, LANES), F32),
            in_specs=[SMEM_SPEC] * 4 + [VMEM_SPEC] * 2,
            out_specs=VMEM_SPEC,
            scratch_shapes=[pltpu.VMEM((quad, LANES), F32)] + wide4,
            compiler_params=params(),
            cost_estimate=pl.CostEstimate(flops=200000000000, bytes_accessed=8000000, transcendentals=0),
            name="one_own",
        )(s4, d4, wc, n_own, x, w1)
        hid, t2, t_next, t_prev = pl.pallas_call(
            one_halo_kernel,
            out_shape=[sds((n_loc, f_hid), BF16), sds((n_loc, LANES), F32), sds((halo, LANES), BF16), sds((halo, LANES), BF16)],
            in_specs=[SMEM_SPEC] * 5 + [VMEM_SPEC] * 5,
            out_specs=[VMEM_SPEC] * 4,
            scratch_shapes=[pltpu.VMEM((4 * 2 * halo, LANES), F32), pltpu.VMEM((2 * halo, LANES), F32)] + wide4,
            compiler_params=params(),
            name="one_halo",
        )(s4, d4, wc, n_hal, ids, y_own, xh_prev, xh_next, w1, w2)
        th_prev = shift_next(t_next)
        th_next = shift_prev(t_prev)
        narrow_own = functools.partial(
            pl.pallas_call,
            narrow_own_kernel,
            out_shape=sds((n_loc, LANES), F32),
            in_specs=[SMEM_SPEC] * 4 + [VMEM_SPEC],
            out_specs=VMEM_SPEC,
            scratch_shapes=thin4,
            compiler_params=params(),
            cost_estimate=pl.CostEstimate(flops=200000000000, bytes_accessed=8000000, transcendentals=0),
        )
        z_own = narrow_own(name="two_own")(s, d, wc, n_own, t2)
        marks = jnp.broadcast_to(jnp.where(label_mask == 1, labels, -1)[:, None], (n_loc, LANES))
        dz, bz_prev, bz_next, loss = pl.pallas_call(
            functools.partial(logits_kernel, classes),
            out_shape=[sds((n_loc, LANES), F32), sds((halo, LANES), F32), sds((halo, LANES), F32), sds((8, LANES), F32)],
            in_specs=[SMEM_SPEC] * 4 + [VMEM_SPEC] * 5,
            out_specs=[VMEM_SPEC] * 4,
            scratch_shapes=[pltpu.VMEM((2 * halo, LANES), F32)] + thin4,
            compiler_params=params(),
            name="logits",
        )(s, d, wc, n_hal, z_own, th_prev, th_next, marks, count)
        rz_next = shift_prev(bz_prev)
        rz_prev = shift_next(bz_next)
        dt2_own = narrow_own(name="two_back_own")(d, s, wc, n_own, dz)
        dt2, dy, by_prev, by_next = pl.pallas_call(
            hidden_grad_kernel,
            out_shape=[sds((n_loc, LANES), BF16), sds((quad, LANES), F32), sds((4 * halo, LANES), F32), sds((4 * halo, LANES), F32)],
            in_specs=[SMEM_SPEC] * 5 + [VMEM_SPEC] * 5,
            out_specs=[VMEM_SPEC] * 4,
            scratch_shapes=wide4,
            compiler_params=params(),
            name="hidden_grad",
        )(s4, d4, wc, n_hal, ids, dt2_own, rz_next, rz_prev, hid, w2.T)
        ry_next = shift_prev(by_prev)
        ry_prev = shift_next(by_next)
        dt1_own = pl.pallas_call(
            wide_own_kernel,
            out_shape=sds((quad, LANES), F32),
            in_specs=[SMEM_SPEC] * 4 + [VMEM_SPEC],
            out_specs=VMEM_SPEC,
            scratch_shapes=wide4,
            compiler_params=params(),
            cost_estimate=pl.CostEstimate(flops=200000000000, bytes_accessed=8000000, transcendentals=0),
            name="one_back_own",
        )(d4, s4, wc, n_own, dy)
        grad_two = lax.dot_general(hid, dt2, CONTRACT_ROWS, preferred_element_type=F32)
        dt1 = pl.pallas_call(
            table_grad_kernel,
            out_shape=sds((n_loc, f_hid), BF16),
            in_specs=[SMEM_SPEC] + [VMEM_SPEC] * 3,
            out_specs=VMEM_SPEC,
            scratch_shapes=wide4,
            compiler_params=params(),
            name="table_grad",
        )(ids * 4, dt1_own, ry_next, ry_prev)
        grad_one = lax.dot_general(x, dt1, CONTRACT_ROWS, preferred_element_type=F32)
        grad_one, grad_two, loss = pl.pallas_call(
            functools.partial(reduce_kernel, num_dev),
            out_shape=[sds((256, f_hid), F32), sds((f_hid, LANES), F32), sds((8, LANES), F32)],
            in_specs=[VMEM_SPEC] * 3,
            out_specs=[VMEM_SPEC] * 3,
            scratch_shapes=[
                pltpu.VMEM((128, f_hid), F32), pltpu.VMEM((f_hid // 2, LANES), F32),
                pltpu.VMEM((128, f_hid), F32), pltpu.VMEM((f_hid // 2, LANES), F32),
                pltpu.VMEM((3, 32, f_hid), F32), pltpu.VMEM((3, f_hid // 8, LANES), F32),
                pltpu.VMEM((num_dev - 1, 8, LANES), F32),
                pltpu.SemaphoreType.DMA((22,)), pltpu.SemaphoreType.DMA((22,)),
                pltpu.SemaphoreType.DMA((num_dev - 1,)), pltpu.SemaphoreType.DMA((num_dev - 1,)),
            ],
            compiler_params=params(collective_id=1, has_side_effects=True),
            name="reduce",
        )(grad_one, grad_two, loss)
        mean_loss = jnp.sum(loss) / count[0, 0]
        return mean_loss, grad_one[:f_in], grad_two[:, :classes]

    row_spec = P(GRAPH_AXIS)
    return jax.shard_map(device_step, mesh=mesh, in_specs=(row_spec, P(), P(), row_spec, row_spec, row_spec, row_spec, row_spec, row_spec), out_specs=(P(), P(), P()), check_vma=False)
```

time: 665 us -> 258 us (0.39); the launches traced: 655 us -> 262 us
  other arithmetic: 437 us -> 9.73 us
  Pallas kernels: 0 us -> 185 us
  waiting for transfers between devices: 124 us -> 19.9 us
  blocking collectives: 22.6 us -> 0 us
  local copies, waits for them, and re-layouts: 31.3 us -> 14 us
  starting transfers between devices: 8.46 us -> 25.3 us
  between operations: 17.1 us -> 3.25 us
  matrix products: 14.3 us -> 4.74 us
    scatter-add x6 -> x0, other arithmetic: 421 us -> none  [the longest x2 206 us: scatter_back(): jax.ops.segment_sum(edge_w[:, None] * grad_rows[edge_dst], edge_src, num_...]
    pallas_call x0 -> x11, Pallas kernels: none -> 185 us  [the longest x1 25.3 us: device_step(): pl.pallas_call(one_own_kernel, out_shape=sds((quad, LANES), F32), in_spec...]
    ppermute x8, waiting for transfers between devices: 81.1 us -> 19.9 us  [the longest x4 13.5 us: shift_prev(): return lax.ppermute(a, GRAPH_AXIS, to_prev)]
    psum x1 -> x0, waiting for transfers between devices: 42.8 us -> none  [device_step(): lax.psum(lax.dot_general(node_feats, d_tab_one, CONTRACT_ROWS, preferred_...]
    psum x1 -> x0, blocking collectives: 22.6 us -> none  [device_step(): lax.psum(jnp.sum(mask_f * (log_norm - picked)), GRAPH_AXIS) / label_count]
    gather x6 -> x0, local copies, waits for them, and re-layouts: 16.9 us -> none  [the longest x3 8.46 us: halo_extend(): from_prev = lax.ppermute(node_table[send_rows[1]], GRAPH_AXIS, to_next)]
    ppermute x8, starting transfers between devices: 8.42 us -> 25.3 us  [the longest x4 24.4 us: shift_prev(): return lax.ppermute(a, GRAPH_AXIS, to_prev)]
    concatenate x2 -> x0, other arithmetic: 10.3 us -> none  [halo_extend(): return jnp.concatenate([node_table, from_prev, from_next], axis=0)]
  transfers between devices with their start and end apart: 9 -> 8, of which waited for: 9 -> 2; matrix products, arithmetic and copies ran while one was open for 2% -> 6% of each run, Pallas kernels for 0% -> 39%
where the time goes in v1:
time: 258 us; the launch traced here: 262 us
  Pallas kernels  185 us (72%)
  starting transfers between devices  25.3 us (10%)
  waiting for transfers between devices  19.9 us (8%)
  local copies, waits for them, and re-layouts  14 us (5%)
  other arithmetic  9.73 us (4%)
  matrix products  4.74 us (2%)
  between operations  3.25 us (1%)
    pallas_call x1, Pallas kernels, device_step(): pl.pallas_call(one_own_kernel, out_shape=sds((quad, LANES), F32), in_spec...  25.3 us
    ppermute x4, starting transfers between devices, shift_prev(): return lax.ppermute(a, GRAPH_AXIS, to_prev)  24.4 us
    pallas_call x1, Pallas kernels, device_step(): pl.pallas_call(wide_own_kernel, out_shape=sds((quad, LANES), F32), in_spe...  23.5 us
    pallas_call x1, Pallas kernels, device_step(): z_own = narrow_own(name='two_own')(s, d, wc, n_own, t2)  20.4 us
    pallas_call x1, Pallas kernels, device_step(): dt2_own = narrow_own(name='two_back_own')(d, s, wc, n_own, dz)  20.3 us
    pallas_call x1, Pallas kernels, device_step(): pl.pallas_call(functools.partial(reduce_kernel, num_dev), out_shape=[sds(...  18.7 us
    pallas_call x1, Pallas kernels, device_step(): pl.pallas_call(hidden_grad_kernel, out_shape=[sds((n_loc, LANES), BF16),...  16.6 us
    pallas_call x1, Pallas kernels, device_step(): pl.pallas_call(one_halo_kernel, out_shape=[sds((n_loc, f_hid), BF16), sds...  16.3 us
  transfers between devices with their start and end apart: 8, of which 2 were waited for; matrix products, arithmetic and copies ran while one was open for 6% of the time, Pallas kernels for 39%

profile of v1, /device:TPU:0, one launch (start us, length us, event | category | flops | bytes accessed | tf_op | source)
XLA Modules:
  0.0 262.1 jit_solution(252060337255612834)
XLA Ops:
  1.5 1.5 copy.15
  5.1 5.5 %halo_rows.1 = (bf16[1024,256]{1,0:T(8,128)(2,1)}, bf16[1024,256]{1,0:T(8,128)(2,1)}) custom-call(s32[2048]{0:T(1024)} %get-tuple-element.51.ids2, bf16[2048,256]{1,0:T(8,128)(2,1)} %pad.12.x), custom_call_target="tpu_custom_call" | custom-call | tf_op jit(solution)/shard_map/halo_rows/pallas_call | solution.py:424
  11.4 2.9 %collective-permute-start.1 = (bf16[1024,256]{1,0:T(8,128)(2,1)}, bf16[1024,256]{1,0:T(8,128)(2,1)}, u32[]{:S(2)}, u32[]{:S(2)}) collective-permute-start(bf16[1024,256]{1,0:T(8,128)(2,1)} %get-tuple-element.21), channel_id=1, source_target_pairs={{0,7},{1,0},{2,1},{3,2},{4,3},{5,4},{6,5},{7,6}} | collective-permute-start | bytes 1572872 | tf_op jit(solution)/shard_map/ppermute | solution.py:394
  16.5 12.1 %count.1 = f32[8,128]{1,0:T(8,128)} custom-call(f32[8,128]{1,0:T(8,128)} %broadcast_in_dim.53.part), custom_call_target="tpu_custom_call" | custom-call | tf_op jit(solution)/shard_map/count/pallas_call | solution.py:436
  29.3 2.8 %select_reduce_fusion = f32[32,384]{1,0:T(8,128)S(1)} fusion(f32[32,256]{1,0:T(8,128)S(1)} %reshape.43, s32[32,256]{1,0:T(8,128)S(1)} %get-tuple-element.59), kind=kLoop, calls=%fused_computation | loop fusion | flops 9424896 | bytes 114688 | tf_op jit(solution)/shard_map/reduce_sum | solution.py:409
  32.1 2.8 %select_reduce_fusion.1 = s32[32,384]{1,0:T(8,128)S(1)} fusion(s32[32,256]{1,0:T(8,128)S(1)} %get-tuple-element.58, s32[32,256]{1,0:T(8,128)S(1)} %get-tuple-element.59), kind=kLoop, calls=%fused_computation.1 | loop fusion | flops 9424896 | bytes 114688 | tf_op jit(solution)/shard_map/reduce_sum | solution.py:408
  37.1 25.3 %one_own.1.y_own = f32[8192,128]{1,0:T(8,128)} custom-call(s32[12288]{0:T(1024)} %get-tuple-element.43.s4.to, s32[12288]{0:T(1024)} %get-tuple-element.49.d4.frm, f32[12288]{0:T(1024)} %reshape.46.w, s32[32]{0:T(128)} %get-tuple-element.57.cnt, bf16[2048,256]{1,0:T(8,128)(2,1)} %pad.12.x, bf16[256,512]{1,0:T(8,128)(2,1)} %pad.13.w1), custom_call_target="tpu_custom_call" | custom-call | flops 199999995904 | bytes 8000000 | tf_op jit(solution)/shard_map/one_own/pallas_call | solution.py:449
  65.1 16.3 %one_halo.1 = (bf16[2048,512]{1,0:T(8,128)(2,1)}, f32[2048,128]{1,0:T(8,128)}, bf16[1024,128]{1,0:T(8,128)(2,1)}, bf16[1024,128]{1,0:T(8,128)(2,1)}) custom-call(s32[12288]{0:T(1024)} %get-tuple-element.43.s4.to, s32[12288]{0:T(1024)} %get-tuple-element.49.d4.frm, f32[12288]{0:T(1024)} %reshape.46.w, s32[32]{0:T(128)} %get-tuple-element.56.cnt, ...), custom_call_target="tpu_custom_call" | custom-call | tf_op jit(solution)/shard_map/one_halo/pallas_call | solution.py:459
  81.4 6.0 %collective-permute-start.3 = (bf16[1024,128]{1,0:T(8,128)(2,1)}, bf16[1024,128]{1,0:T(8,128)(2,1)}, u32[]{:S(2)}, u32[]{:S(2)}) collective-permute-start(bf16[1024,128]{1,0:T(8,128)(2,1)} %get-tuple-element.24), channel_id=1, source_target_pairs={{0,7},{1,0},{2,1},{3,2},{4,3},{5,4},{6,5},{7,6}} | collective-permute-start | bytes 786440 | tf_op jit(solution)/shard_map/ppermute | solution.py:394
  87.4 20.4 %two_own.1.z_own = f32[2048,128]{1,0:T(8,128)} custom-call(s32[12288]{0:T(1024)} %get-tuple-element.44.frm.s.to, s32[12288]{0:T(1024)} %get-tuple-element.50.to.d.frm, f32[12288]{0:T(1024)} %reshape.46.w, s32[32]{0:T(128)} %get-tuple-element.57.cnt, f32[2048,128]{1,0:T(8,128)} %get-tuple-element.22.table), custom_call_target="tpu_custom_call" | custom-call | flops 199999995904 | bytes 8000000 | tf_op jit(solution)/shard_map/two_own/pallas_call | solution.py:480
  109.2 16.0 %logits.1 = (f32[2048,128]{1,0:T(8,128)}, f32[1024,128]{1,0:T(8,128)}, f32[1024,128]{1,0:T(8,128)}, f32[8,128]{1,0:T(8,128)}) custom-call(s32[12288]{0:T(1024)} %get-tuple-element.44.frm.s.to, s32[12288]{0:T(1024)} %get-tuple-element.50.to.d.frm, f32[12288]{0:T(1024)} %reshape.46.w, s32[32]{0:T(128)} %get-tuple-element.56.cnt, f32[2048,128]{1,0:T(8,128)} %two_own.1.z_own, ...), custom_call_target="tpu_custom_call" | custom-call | tf_op jit(solution)/shard_map/logits/pallas_call | solution.py:482
  125.2 8.1 %collective-permute-start.4 = (f32[1024,128]{1,0:T(8,128)}, f32[1024,128]{1,0:T(8,128)}, u32[]{:S(2)}, u32[]{:S(2)}) collective-permute-start(f32[1024,128]{1,0:T(8,128)} %get-tuple-element.26), channel_id=1, source_target_pairs={{0,7},{1,0},{2,1},{3,2},{4,3},{5,4},{6,5},{7,6}} | collective-permute-start | bytes 1572872 | tf_op jit(solution)/shard_map/ppermute | solution.py:394
  133.3 20.3 %two_back_own.1.own = f32[2048,128]{1,0:T(8,128)} custom-call(s32[12288]{0:T(1024)} %get-tuple-element.50.to.d.frm, s32[12288]{0:T(1024)} %get-tuple-element.44.frm.s.to, f32[12288]{0:T(1024)} %reshape.46.w, s32[32]{0:T(128)} %get-tuple-element.57.cnt, f32[2048,128]{1,0:T(8,128)} %get-tuple-element.25.table), custom_call_target="tpu_custom_call" | custom-call | flops 199999995904 | bytes 8000000 | tf_op jit(solution)/shard_map/two_back_own/pallas_call | solution.py:493
  153.7 16.6 %hidden_grad.1 = (bf16[2048,128]{1,0:T(8,128)(2,1)}, f32[8192,128]{1,0:T(8,128)}, f32[4096,128]{1,0:T(8,128)}, f32[4096,128]{1,0:T(8,128)}) custom-call(s32[12288]{0:T(1024)} %get-tuple-element.43.s4.to, s32[12288]{0:T(1024)} %get-tuple-element.49.d4.frm, f32[12288]{0:T(1024)} %reshape.46.w, s32[32]{0:T(128)} %get-tuple-element.56.cnt, ...), custom_call_target="tpu_custom_call" | custom-call | tf_op jit(solution)/shard_map/hidden_grad/pallas_call | solution.py:494
  170.3 7.4 %collective-permute-start.6 = (f32[4096,128]{1,0:T(8,128)}, f32[4096,128]{1,0:T(8,128)}, u32[]{:S(2)}, u32[]{:S(2)}) collective-permute-start(f32[4096,128]{1,0:T(8,128)} %get-tuple-element.30), channel_id=1, source_target_pairs={{0,7},{1,0},{2,1},{3,2},{4,3},{5,4},{6,5},{7,6}} | collective-permute-start | bytes 6291464 | tf_op jit(solution)/shard_map/ppermute | solution.py:394
  177.7 23.5 %one_back_own.1.own = f32[8192,128]{1,0:T(8,128)} custom-call(s32[12288]{0:T(1024)} %get-tuple-element.49.d4.frm, s32[12288]{0:T(1024)} %get-tuple-element.43.s4.to, f32[12288]{0:T(1024)} %reshape.46.w, s32[32]{0:T(128)} %get-tuple-element.57.cnt, f32[8192,128]{1,0:T(8,128)} %get-tuple-element.29.table), custom_call_target="tpu_custom_call" | custom-call | flops 199999995904 | bytes 8000000 | tf_op jit(solution)/shard_map/one_back_own/pallas_call | solution.py:505
  201.2 1.5 fusion.11.g2
  202.6 13.5 %collective-permute-done.6.ret_next = f32[4096,128]{1,0:T(8,128)} collective-permute-done((f32[4096,128]{1,0:T(8,128)}, f32[4096,128]{1,0:T(8,128)}, u32[]{:S(2)}, u32[]{:S(2)}) %collective-permute-start.6) | collective-permute-done | bytes 2097184 | tf_op jit(solution)/shard_map/ppermute | solution.py:394
  216.1 6.5 %collective-permute-done.7.ret_prev = f32[4096,128]{1,0:T(8,128)} collective-permute-done((f32[4096,128]{1,0:T(8,128)}, f32[4096,128]{1,0:T(8,128)}, u32[]{:S(2)}, u32[]{:S(2)}) %collective-permute-start.7) | collective-permute-done | bytes 2097184 | tf_op jit(solution)/shard_map/ppermute | solution.py:391
  222.5 10.5 %table_grad.1 = bf16[2048,512]{1,0:T(8,128)(2,1)} custom-call(s32[2048]{0:T(1024)} %get-tuple-element.52.ids4, f32[8192,128]{1,0:T(8,128)} %one_back_own.1.own, f32[4096,128]{1,0:T(8,128)} %collective-permute-done.6.ret_next, f32[4096,128]{1,0:T(8,128)} %collective-permute-done.7.ret_prev), custom_call_target="tpu_custom_call" | custom-call | tf_op jit(solution)/shard_map/table_grad/pallas_call | solution.py:516
  233.0 3.1 %fusion.6.g1 = f32[256,512]{1,0:T(8,128)} fusion(bf16[2048,512]{1,0:T(8,128)(2,1)} %table_grad.1, bf16[2048,200]{1,0:T(8,128)(2,1)S(1)} %copy-done.2), kind=kOutput, calls=%fused_computation.34 | convolution fusion | flops 536870912 | bytes 3440640 | tf_op jit(solution)/shard_map/dot_general | solution.py:525
  236.1 18.7 %reduce.1 = (f32[256,512]{1,0:T(8,128)}, f32[512,128]{1,0:T(8,128)}, f32[8,128]{1,0:T(8,128)}) custom-call(f32[256,512]{1,0:T(8,128)} %fusion.6.g1, f32[512,128]{1,0:T(8,128)} %fusion.11.g2, f32[8,128]{1,0:T(8,128)} %get-tuple-element.33.loss), custom_call_target="tpu_custom_call" | custom-call | tf_op jit(solution)/shard_map/reduce/pallas_call | solution.py:526
  254.8 1.8 copy.17
  256.6 1.8 slice.34
  (70 shorter events, 14.0 us)
Async XLA Ops:
  0.6 13.7 %copy-start.9 = (s32[8192]{0:T(1024)S(1)}, s32[8192]{0:T(1024)}, u32[]{:S(2)}) copy-start(s32[8192]{0:T(1024)} %param.13) | copy-start | bytes 98308
  0.6 13.7 %copy-start.10 = (f32[8192]{0:T(1024)S(1)}, f32[8192]{0:T(1024)}, u32[]{:S(2)}) copy-start(f32[8192]{0:T(1024)} %param.15) | copy-start | bytes 98308
  0.7 14.0 %copy-start.7 = (s32[2048]{0:T(1024)S(1)}, s32[2048]{0:T(1024)}, u32[]{:S(2)}) copy-start(s32[2048]{0:T(1024)} %param.17) | copy-start | bytes 24580
  0.7 28.6 %copy-start.11 = (s32[8192]{0:T(1024)S(1)}, s32[8192]{0:T(1024)}, u32[]{:S(2)}) copy-start(s32[8192]{0:T(1024)} %param.14) | copy-start | bytes 98308
  1.5 34.8 %copy-start.4 = (f32[200,512]{1,0:T(8,128)S(1)}, f32[200,512]{1,0:T(8,128)}, u32[]{:S(2)}) copy-start(f32[200,512]{1,0:T(8,128)} %param.10) | copy-start | bytes 1228804
  3.0 1.0 copy-start.1
  10.6 54.5 %collective-permute-start = (bf16[1024,256]{1,0:T(8,128)(2,1)}, bf16[1024,256]{1,0:T(8,128)(2,1)}, u32[]{:S(2)}, u32[]{:S(2)}) collective-permute-start(bf16[1024,256]{1,0:T(8,128)(2,1)} %get-tuple-element.20), channel_id=1, source_target_pairs={{0,1},{1,2},{2,3},{3,4},{4,5},{5,6},{6,7},{7,0}} | collective-permute-start | bytes 1572872 | tf_op jit(solution)/shard_map/ppermute | solution.py:391
  11.4 53.6 %collective-permute-start.1 = (bf16[1024,256]{1,0:T(8,128)(2,1)}, bf16[1024,256]{1,0:T(8,128)(2,1)}, u32[]{:S(2)}, u32[]{:S(2)}) collective-permute-start(bf16[1024,256]{1,0:T(8,128)(2,1)} %get-tuple-element.21), channel_id=1, source_target_pairs={{0,7},{1,0},{2,1},{3,2},{4,3},{5,4},{6,5},{7,6}} | collective-permute-start | bytes 1572872 | tf_op jit(solution)/shard_map/ppermute | solution.py:394
  37.1 25.3 %copy-start.13 = (f32[8,128]{1,0:T(8,128)S(1)}, f32[8,128]{1,0:T(8,128)}, u32[]{:S(2)}) copy-start(f32[8,128]{1,0:T(8,128)} %count.1) | copy-start | bytes 12292
  37.1 25.9 %copy-start.5 = (f32[512,107]{0,1:T(8,128)S(1)}, f32[512,107]{0,1:T(8,128)}, u32[]{:S(2)}) copy-start(f32[512,107]{0,1:T(8,128)} %param.11) | copy-start | bytes 657412
  37.1 27.4 %copy-start.8 = (s32[2048]{0:T(1024)S(1)}, s32[2048]{0:T(1024)}, u32[]{:S(2)}) copy-start(s32[2048]{0:T(1024)} %param.17) | copy-start | bytes 24580
  37.1 27.4 %copy-start.14 = (s32[2048]{0:T(1024)S(1)}, s32[2048]{0:T(1024)}, u32[]{:S(2)}) copy-start(s32[2048]{0:T(1024)} %param.16) | copy-start | bytes 24580
  62.4 0.6 copy-start.12
  81.4 26.5 %collective-permute-start.2 = (bf16[1024,128]{1,0:T(8,128)(2,1)}, bf16[1024,128]{1,0:T(8,128)(2,1)}, u32[]{:S(2)}, u32[]{:S(2)}) collective-permute-start(bf16[1024,128]{1,0:T(8,128)(2,1)} %get-tuple-element.23), channel_id=1, source_target_pairs={{0,1},{1,2},{2,3},{3,4},{4,5},{5,6},{6,7},{7,0}} | collective-permute-start | bytes 786440 | tf_op jit(solution)/shard_map/ppermute | solution.py:391
  81.4 26.5 %collective-permute-start.3 = (bf16[1024,128]{1,0:T(8,128)(2,1)}, bf16[1024,128]{1,0:T(8,128)(2,1)}, u32[]{:S(2)}, u32[]{:S(2)}) collective-permute-start(bf16[1024,128]{1,0:T(8,128)(2,1)} %get-tuple-element.24), channel_id=1, source_target_pairs={{0,7},{1,0},{2,1},{3,2},{4,3},{5,4},{6,5},{7,6}} | collective-permute-start | bytes 786440 | tf_op jit(solution)/shard_map/ppermute | solution.py:394
  87.4 20.5 %copy-start.6 = (s32[2048]{0:T(1024)S(1)}, s32[2048]{0:T(1024)}, u32[]{:S(2)}) copy-start(s32[2048]{0:T(1024)} %compare_select_fusion) | copy-start | bytes 24580
  125.2 28.4 %collective-permute-start.4 = (f32[1024,128]{1,0:T(8,128)}, f32[1024,128]{1,0:T(8,128)}, u32[]{:S(2)}, u32[]{:S(2)}) collective-permute-start(f32[1024,128]{1,0:T(8,128)} %get-tuple-element.26), channel_id=1, source_target_pairs={{0,7},{1,0},{2,1},{3,2},{4,3},{5,4},{6,5},{7,6}} | collective-permute-start | bytes 1572872 | tf_op jit(solution)/shard_map/ppermute | solution.py:394
  133.3 20.3 %collective-permute-start.5 = (f32[1024,128]{1,0:T(8,128)}, f32[1024,128]{1,0:T(8,128)}, u32[]{:S(2)}, u32[]{:S(2)}) collective-permute-start(f32[1024,128]{1,0:T(8,128)} %get-tuple-element.27), channel_id=1, source_target_pairs={{0,1},{1,2},{2,3},{3,4},{4,5},{5,6},{6,7},{7,0}} | collective-permute-start | bytes 1572872 | tf_op jit(solution)/shard_map/ppermute | solution.py:391
  170.3 45.8 %collective-permute-start.6 = (f32[4096,128]{1,0:T(8,128)}, f32[4096,128]{1,0:T(8,128)}, u32[]{:S(2)}, u32[]{:S(2)}) collective-permute-start(f32[4096,128]{1,0:T(8,128)} %get-tuple-element.30), channel_id=1, source_target_pairs={{0,7},{1,0},{2,1},{3,2},{4,3},{5,4},{6,5},{7,6}} | collective-permute-start | bytes 6291464 | tf_op jit(solution)/shard_map/ppermute | solution.py:394
  177.7 44.9 %collective-permute-start.7 = (f32[4096,128]{1,0:T(8,128)}, f32[4096,128]{1,0:T(8,128)}, u32[]{:S(2)}, u32[]{:S(2)}) collective-permute-start(f32[4096,128]{1,0:T(8,128)} %get-tuple-element.31), channel_id=1, source_target_pairs={{0,1},{1,2},{2,3},{3,4},{4,5},{5,6},{6,7},{7,0}} | collective-permute-start | bytes 6291464 | tf_op jit(solution)/shard_map/ppermute | solution.py:391
  177.7 23.5 %copy-start = (bf16[2048,512]{1,0:T(8,128)(2,1)S(1)}, bf16[2048,512]{1,0:T(8,128)(2,1)}, u32[]{:S(2)}) copy-start(bf16[2048,512]{1,0:T(8,128)(2,1)} %get-tuple-element.28.hid) | copy-start | bytes 6291460
  177.7 23.5 %copy-start.3 = (bf16[2048,128]{1,0:T(8,128)(2,1)S(1)}, bf16[2048,128]{1,0:T(8,128)(2,1)}, u32[]{:S(2)}) copy-start(bf16[2048,128]{1,0:T(8,128)(2,1)} %get-tuple-element.32) | copy-start | bytes 1572868
  222.5 10.5 %copy-start.2 = (bf16[2048,200]{1,0:T(8,128)(2,1)S(1)}, bf16[2048,200]{1,0:T(8,128)(2,1)}, u32[]{:S(2)}) copy-start(bf16[2048,200]{1,0:T(8,128)(2,1)} %copy-done.1) | copy-start | bytes 2457604

commit v2 on v1

--- a/solution.py
+++ b/solution.py
@@ -6,6 +6,7 @@
 from jax.experimental import pallas as pl
 from jax.experimental.pallas import tpu as pltpu
 from jax.sharding import PartitionSpec as P
+
 
 GRAPH_AXIS = "graph"
 CONTRACT_ROWS = (((0,), (0,)), ((), ()))
@@ -15,14 +16,13 @@
 LANES = 128
 CHUNK = 256
 SLOT = 384
-VMEM_LIMIT = 64000000
 
 SMEM_SPEC = pl.BlockSpec(memory_space=pltpu.SMEM)
 VMEM_SPEC = pl.BlockSpec(memory_space=pltpu.VMEM)
 
 
-def params(**kw):
-    return pltpu.CompilerParams(vmem_limit_bytes=VMEM_LIMIT, **kw)
+def params(mib, **kw):
+    return pltpu.CompilerParams(vmem_limit_bytes=mib * 2**20, **kw)
 
 
 def zero_rows(refs):
@@ -58,12 +58,12 @@
 
         def body(j, _):
             off = r * SLOT + (SLOT - unroll - j * unroll if back else j * unroll)
-            vals = [table[pl.ds(pl.multiple_of(from_ref[off + u], width), width), :] * w_ref[off + u] for u in range(unroll)]
-            for g in range(unroll // n_acc):
-                rows = [pl.multiple_of(to_ref[off + g * n_acc + k], width) for k in range(n_acc)]
-                old = [accs[k][pl.ds(rows[k], width), :] for k in range(n_acc)]
-                for k in range(n_acc):
-                    accs[k][pl.ds(rows[k], width), :] = old[k] + vals[g * n_acc + k]
+            frm, to, wgt = (ref.at[pl.ds(off, unroll)] for ref in (from_ref, to_ref, w_ref))
+            for u in range(unroll):
+                acc = accs[u % n_acc]
+                val = table[pl.ds(pl.multiple_of(frm[u], width), width), :] * wgt[u]
+                at = pl.ds(pl.multiple_of(to[u], width), width)
+                acc[at, :] = acc[at, :] + val
             return 0
 
         lax.fori_loop(0, blocks, body, 0)
@@ -108,6 +108,38 @@
     return jnp.concatenate([table[pl.ds(start * tiles + c, rows, tiles), :] for c in range(tiles)], axis=1)
 
 
+def enter(me, num_dev):
+    barrier = pltpu.get_barrier_semaphore()
+    for step in range(1, num_dev):
+        pl.semaphore_signal(barrier, inc=1, device_id=(lax.rem(me + step, num_dev),), device_id_type=MESH)
+    pl.semaphore_wait(barrier, num_dev - 1)
+
+
+def push(src, dst, send_sem, recv_sem, dev):
+    copy = pltpu.make_async_remote_copy(src_ref=src, dst_ref=dst, send_sem=send_sem, recv_sem=recv_sem, device_id=(dev,), device_id_type=MESH)
+    copy.start()
+    return copy
+
+
+def lists_kernel(num_dev, part, code, wgt, count, code_prev, code_next, w_prev, w_next, slots, send_sem, recv_sem, lsend, lrecv):
+    me = lax.axis_index(GRAPH_AXIS)
+    succ, pred = lax.rem(me + 1, num_dev), lax.rem(me + num_dev - 1, num_dev)
+    enter(me, num_dev)
+    copies = []
+    for step in range(1, num_dev):
+        copies.append(push(part, slots.at[step - 1], send_sem.at[step - 1], recv_sem.at[step - 1], lax.rem(me + step, num_dev)))
+    copies.append(push(code, code_prev, lsend.at[0], lrecv.at[0], succ))
+    copies.append(push(code, code_next, lsend.at[1], lrecv.at[1], pred))
+    copies.append(push(wgt, w_prev, lsend.at[2], lrecv.at[2], succ))
+    copies.append(push(wgt, w_next, lsend.at[3], lrecv.at[3], pred))
+    for copy in copies:
+        copy.wait()
+    total = part[...]
+    for step in range(num_dev - 1):
+        total = total + slots[step]
+    count[...] = jnp.maximum(total, 1.0)
+
+
 def halo_rows_kernel(ids2, x, to_next, to_prev, table, picked):
     rows = x.shape[0]
 
@@ -136,11 +168,11 @@
         return 0
 
     lax.fori_loop(0, x.shape[0] // 256, put, 0)
-    edge_pass(s4, d4, w, cnt, table, accs, 4, 16, False)
+    edge_pass(s4, d4, w, cnt, table, accs, 4, 32, False)
     sum_rows(y, accs)
 
 
-def one_halo_kernel(s4, d4, w, cnt, ids, y_own, x_prev, x_next, w1, w2, hid, t2, to_next, to_prev, table, picked, *accs):
+def one_halo_kernel(s4, d4, w, cnt, ids, y_own, x_prev, x_next, w1, w2, hid_a, hid_b, t2, to_next, to_prev, table, picked, *accs):
     zero_rows(accs)
     half = x_prev.shape[0]
 
@@ -157,12 +189,14 @@
 
     def act(i, _):
         h = jnp.maximum(unspread(accs[0], i * 256, 256, 4), 0.0).astype(BF16)
-        hid[pl.ds(i * 256, 256), :] = h
+        cut = hid_a.shape[1]
+        hid_a[pl.ds(i * 256, 256), :] = h[:, :cut]
+        hid_b[pl.ds(i * 256, 256), :] = h[:, cut:]
         t = jnp.dot(h, w2[...], preferred_element_type=F32)
         t2[pl.ds(i * 256, 256), :] = t.astype(BF16).astype(F32)
         return 0
 
-    lax.fori_loop(0, hid.shape[0] // 256, act, 0)
+    lax.fori_loop(0, t2.shape[0] // 256, act, 0)
     gather_pass(ids, t2, picked, 1)
 
     def take(i, _):
@@ -175,13 +209,13 @@
 
 def narrow_own_kernel(frm, to, w, cnt, table, out, *accs):
     zero_rows(accs)
-    edge_pass(frm, to, w, cnt, table, accs, 1, 16, False)
+    edge_pass(frm, to, w, cnt, table, accs, 1, 32, False)
     sum_rows(out, accs)
 
 
 def wide_own_kernel(frm, to, w, cnt, table, out, *accs):
     zero_rows(accs)
-    edge_pass(frm, to, w, cnt, table, accs, 4, 16, False)
+    edge_pass(frm, to, w, cnt, table, accs, 4, 32, False)
     sum_rows(out, accs)
 
 
@@ -196,7 +230,6 @@
 
     lax.fori_loop(0, half // 256, put, 0)
     edge_pass(s, d, w, cnt, table, accs, 1, 8, True)
-    scale = 1.0 / count[0:1, :]
     denom = count[0:1, :]
     loss[...] = jnp.zeros_like(loss)
 
@@ -240,47 +273,77 @@
     lax.fori_loop(0, half // 64, fin, 0)
 
 
-def hidden_grad_kernel(s4, d4, w, cnt, ids, own, ret_next, ret_prev, hid, w2t, dt2, dy, back_prev, back_next, *accs):
+def masked(grad, hid_a, hid_b):
+    cut = hid_a.shape[1]
+    lo = jnp.where(hid_a.astype(F32) > 0.0, grad[:, :cut], 0.0)
+    hi = jnp.where(hid_b.astype(F32) > 0.0, grad[:, cut:], 0.0)
+    return jnp.concatenate([lo, hi], axis=1)
+
+
+def hidden_grad_kernel(ids, own, ret_next, ret_prev, hid_a, hid_b, w2t, dt2, dy, *accs):
     n_loc, half = own.shape[0], ret_next.shape[0]
-    narrow = tuple(acc.at[pl.ds(0, n_loc)] for acc in accs)
-    zero_rows(narrow)
-    scatter_pass(ids.at[pl.ds(0, half)], ret_next, narrow, 1, 8)
-    scatter_pass(ids.at[pl.ds(half, half)], ret_prev, narrow, 1, 8)
+    zero_rows(accs)
+    scatter_pass(ids.at[pl.ds(0, half)], ret_next, accs, 1, 8)
+    scatter_pass(ids.at[pl.ds(half, half)], ret_prev, accs, 1, 8)
 
     def fold(i, _):
         at = pl.ds(i * 256, 256)
         total = own[at, :]
-        for acc in narrow:
+        for acc in accs:
             total = total + acc[at, :]
         dt = total.astype(BF16)
         dt2[at, :] = dt
         dh = jnp.dot(dt, w2t[...], preferred_element_type=F32)
-        spread(dy, i * 256, jnp.where(hid[at, :].astype(F32) > 0.0, dh, 0.0))
+        spread(dy, i * 256, masked(dh, hid_a[at, :], hid_b[at, :]))
         return 0
 
     lax.fori_loop(0, n_loc // 256, fold, 0)
-    zero_rows(accs)
-    edge_pass(d4, s4, w, cnt, dy, accs, 4, 8, True)
-    quad = 4 * half
-
-    def fin(i, _):
-        at = pl.ds(i * 64, 64)
-        bt = pl.ds(quad + i * 64, 64)
-        a, b = accs[0][at, :], accs[0][bt, :]
-        for acc in accs[1:]:
-            a, b = a + acc[at, :], b + acc[bt, :]
-        back_prev[at, :] = a
-        back_next[at, :] = b
-        return 0
-
-    lax.fori_loop(0, quad // 64, fin, 0)
-
-
-def table_grad_kernel(ids4, own, ret_next, ret_prev, dt1, *accs):
-    half = ids4.shape[0] // 2
-    zero_rows(accs)
-    scatter_pass(ids4.at[pl.ds(0, half)], ret_next, accs, 4, 8)
-    scatter_pass(ids4.at[pl.ds(half, half)], ret_prev, accs, 4, 8)
+
+
+def peer_pass(ids4, code_ref, w_ref, rows, far, table, accs):
+    n_acc = len(accs)
+    tally = rows * SLOT
+    n_loc = ids4.shape[0]
+    shift = n_loc.bit_length() - 1
+
+    def row(r, _):
+        first = SLOT - 8 - (code_ref[tally + 2 * rows + r] if far else 0)
+        edges = code_ref[tally + far * rows + r]
+
+        def body(j, _):
+            off = r * SLOT + first - j * 8
+            codes, wgt = (ref.at[pl.ds(off, 8)] for ref in (code_ref, w_ref))
+            for u in range(8):
+                acc = accs[u % n_acc]
+                code = codes[u]
+                frm = lax.shift_right_logical(code, shift) * 4
+                val = table[pl.ds(pl.multiple_of(frm, 4), 4), :] * wgt[u]
+                at = pl.ds(pl.multiple_of(ids4[code & (n_loc - 1)], 4), 4)
+                acc[at, :] = acc[at, :] + val
+            return 0
+
+        lax.fori_loop(0, lax.shift_right_logical(edges + 7, 3), body, 0)
+        return 0
+
+    lax.fori_loop(0, rows, row, 0)
+
+
+def table_grad_kernel(rows, ids4, cn, wn, cp, wp, own, tn, han, hbn, tp, hap, hbp, w2t, dt1, table, *accs):
+    zero_rows(accs)
+
+    def fill(dt, hid_a, hid_b):
+        def put(i, _):
+            at = pl.ds(i * 256, 256)
+            dh = jnp.dot(dt[at, :], w2t[...], preferred_element_type=F32)
+            spread(table, i * 256, masked(dh, hid_a[at, :], hid_b[at, :]))
+            return 0
+
+        lax.fori_loop(0, dt.shape[0] // 256, put, 0)
+
+    fill(tn, han, hbn)
+    peer_pass(ids4, cn, wn, rows, 0, table, accs)
+    fill(tp, hap, hbp)
+    peer_pass(ids4, cp, wp, rows, 1, table, accs)
 
     def fold(i, _):
         total = unspread(own, i * 128, 128, 4)
@@ -290,33 +353,6 @@
         return 0
 
     lax.fori_loop(0, dt1.shape[0] // 128, fold, 0)
-
-
-def enter(me, num_dev):
-    barrier = pltpu.get_barrier_semaphore()
-    for step in range(1, num_dev):
-        pl.semaphore_signal(barrier, inc=1, device_id=(lax.rem(me + step, num_dev),), device_id_type=MESH)
-    pl.semaphore_wait(barrier, num_dev - 1)
-
-
-def push(src, dst, send_sem, recv_sem, dev):
-    copy = pltpu.make_async_remote_copy(src_ref=src, dst_ref=dst, send_sem=send_sem, recv_sem=recv_sem, device_id=(dev,), device_id_type=MESH)
-    copy.start()
-    return copy
-
-
-def count_kernel(num_dev, part, out, slots, send_sem, recv_sem):
-    me = lax.axis_index(GRAPH_AXIS)
-    enter(me, num_dev)
-    copies = []
-    for step in range(1, num_dev):
-        copies.append(push(part, slots.at[step - 1], send_sem.at[step - 1], recv_sem.at[step - 1], lax.rem(me + step, num_dev)))
-    for copy in copies:
-        copy.wait()
-    total = part[...]
-    for step in range(num_dev - 1):
-        total = total + slots[step]
-    out[...] = total
 
 
 def reduce_kernel(num_dev, g1, g2, loss, o1, o2, lo, r1, r2, s1, s2, q1, q2, lslots, sem_s, sem_r, lsem_s, lsem_r):
@@ -393,23 +429,28 @@
     def shift_prev(a):
         return lax.ppermute(a, GRAPH_AXIS, to_prev)
 
-    def compact(edge_src, edge_dst, edge_w, n_loc):
+    def compact(edge_src, edge_dst, edge_w, n_loc, halo):
         rows = edge_src.shape[0] // CHUNK
         src, dst, w = (a.reshape(rows, CHUNK) for a in (edge_src, edge_dst, edge_w))
         live = w != 0.0
         own = live & (src < n_loc)
-        hal = live & (src >= n_loc)
+        far = live & (src >= n_loc + halo)
+        near = live & (src >= n_loc) & (src < n_loc + halo)
         tri = (jnp.arange(CHUNK)[:, None] < jnp.arange(CHUNK)[None, :]).astype(BF16)
-        both = jnp.concatenate([own, hal], axis=0).astype(BF16)
-        rank = jnp.dot(both, tri, preferred_element_type=F32).astype(jnp.int32)
-        place = jnp.where(own, rank[:rows], jnp.where(hal, SLOT - 1 - rank[rows:], SLOT))
+        sets = jnp.concatenate([own, near, far], axis=0).astype(BF16)
+        rank = jnp.dot(sets, tri, preferred_element_type=F32).astype(jnp.int32)
+        counts = jnp.sum(sets.astype(F32), axis=1).astype(jnp.int32)
+        n_own, n_near, n_far = counts[:rows], counts[rows:2 * rows], counts[2 * rows:]
+        skip = (n_near + 7) // 8 * 8
+        place = jnp.where(far, SLOT - 1 - skip[:, None] - rank[2 * rows:], SLOT)
+        place = jnp.where(near, SLOT - 1 - rank[rows:2 * rows], place)
+        place = jnp.where(own, rank[:rows], place)
         hit = place[:, :, None] == jnp.arange(SLOT)[None, None, :]
         code = jnp.where(src < n_loc, src, src - n_loc) + dst * n_loc
-        code = jnp.sum(jnp.where(hit, code[:, :, None], 0), axis=1).reshape(-1)
-        wc = jnp.sum(jnp.where(hit, w[:, :, None], 0.0), axis=1).reshape(-1)
-        s, d = code % n_loc, code // n_loc
-        counts = jnp.sum(both.astype(F32), axis=1).astype(jnp.int32)
-        return s, d, s * 4, d * 4, wc, counts[:rows], counts[rows:]
+        code = jnp.sum(jnp.where(hit, code[:, :, None], 0), axis=1)
+        wc = jnp.sum(jnp.where(hit, w[:, :, None], 0.0), axis=1)
+        n_hal = jnp.where(n_far > 0, skip + n_far, n_near)
+        return code, wc, n_own, n_hal, n_near, n_far, skip
 
     def device_step(node_feats, w_one, w_two, send_rows, edge_src, edge_dst, edge_w, labels, label_mask):
         n_loc, f_in = node_feats.shape
@@ -421,29 +462,36 @@
         w1 = jnp.pad(w_one.astype(BF16), ((0, 256 - f_in), (0, 0)))
         w2 = jnp.pad(w_two.astype(BF16), ((0, 0), (0, LANES - classes)))
         ids = jnp.concatenate([send_rows[1], send_rows[0]])
+        mask_count = jnp.sum(label_mask.astype(F32))
+        code, wc, n_own, n_hal, n_near, n_far, skip = compact(edge_src, edge_dst, edge_w, n_loc, halo)
+        rows = n_own.shape[0]
+        slots = code.size // LANES
+        code, wc = code.reshape(-1), wc.reshape(-1)
+        tally = jnp.concatenate([n_near, n_far, skip, jnp.zeros((8 * LANES - 3 * rows,), jnp.int32)])
+        lists = jnp.concatenate([code, tally]).reshape(slots + 8, LANES)
+        count, code_prev, code_next, w_prev, w_next = pl.pallas_call(
+            functools.partial(lists_kernel, num_dev),
+            out_shape=[sds((8, LANES), F32)] + [sds((slots + 8, LANES), jnp.int32)] * 2 + [sds((slots, LANES), F32)] * 2,
+            in_specs=[VMEM_SPEC] * 3,
+            out_specs=[VMEM_SPEC] * 5,
+            scratch_shapes=[pltpu.VMEM((num_dev - 1, 8, LANES), F32)] + [pltpu.SemaphoreType.DMA((n,)) for n in (num_dev - 1, num_dev - 1, 4, 4)],
+            compiler_params=params(1, collective_id=0, has_side_effects=True),
+            name="lists",
+        )(jnp.broadcast_to(mask_count, (8, LANES)), lists, wc.reshape(slots, LANES))
+        s, d = code % n_loc, code // n_loc
+        s4, d4 = s * 4, d * 4
+        count, x_src = lax.optimization_barrier((count, x))
         x_next, x_prev = pl.pallas_call(
             halo_rows_kernel,
             out_shape=[sds((halo, 256), BF16)] * 2,
             in_specs=[SMEM_SPEC, VMEM_SPEC],
             out_specs=[VMEM_SPEC] * 2,
             scratch_shapes=[pltpu.VMEM((2 * n_loc, LANES), F32), pltpu.VMEM((4 * halo, LANES), F32)],
-            compiler_params=params(),
+            compiler_params=params(12),
             name="halo_rows",
-        )(ids * 2, x)
+        )(ids * 2, x_src)
         xh_prev = shift_next(x_next)
         xh_next = shift_prev(x_prev)
-        mask_count = jnp.sum(label_mask.astype(F32))
-        count = pl.pallas_call(
-            functools.partial(count_kernel, num_dev),
-            out_shape=sds((8, LANES), F32),
-            in_specs=[VMEM_SPEC],
-            out_specs=VMEM_SPEC,
-            scratch_shapes=[pltpu.VMEM((num_dev - 1, 8, LANES), F32), pltpu.SemaphoreType.DMA((num_dev - 1,)), pltpu.SemaphoreType.DMA((num_dev - 1,))],
-            compiler_params=params(collective_id=0, has_side_effects=True),
-            name="count",
-        )(jnp.broadcast_to(mask_count, (8, LANES)))
-        count = jnp.maximum(count, 1.0)
-        s, d, s4, d4, wc, n_own, n_hal = compact(edge_src, edge_dst, edge_w, n_loc)
         wide4 = [pltpu.VMEM((quad, LANES), F32)] * 4
         thin4 = [pltpu.VMEM((n_loc, LANES), F32)] * 4
         y_own = pl.pallas_call(
@@ -452,21 +500,22 @@
             in_specs=[SMEM_SPEC] * 4 + [VMEM_SPEC] * 2,
             out_specs=VMEM_SPEC,
             scratch_shapes=[pltpu.VMEM((quad, LANES), F32)] + wide4,
-            compiler_params=params(),
+            compiler_params=params(28),
             cost_estimate=pl.CostEstimate(flops=200000000000, bytes_accessed=8000000, transcendentals=0),
             name="one_own",
         )(s4, d4, wc, n_own, x, w1)
-        hid, t2, t_next, t_prev = pl.pallas_call(
+        hid_a, hid_b, t2, t_next, t_prev = pl.pallas_call(
             one_halo_kernel,
-            out_shape=[sds((n_loc, f_hid), BF16), sds((n_loc, LANES), F32), sds((halo, LANES), BF16), sds((halo, LANES), BF16)],
+            out_shape=[sds((n_loc, f_hid // 2), BF16)] * 2 + [sds((n_loc, LANES), F32), sds((halo, LANES), BF16), sds((halo, LANES), BF16)],
             in_specs=[SMEM_SPEC] * 5 + [VMEM_SPEC] * 5,
-            out_specs=[VMEM_SPEC] * 4,
+            out_specs=[VMEM_SPEC] * 5,
             scratch_shapes=[pltpu.VMEM((4 * 2 * halo, LANES), F32), pltpu.VMEM((2 * halo, LANES), F32)] + wide4,
-            compiler_params=params(),
+            compiler_params=params(30),
             name="one_halo",
         )(s4, d4, wc, n_hal, ids, y_own, xh_prev, xh_next, w1, w2)
         th_prev = shift_next(t_next)
         th_next = shift_prev(t_prev)
+        ha_prev, ha_next = shift_next(hid_a), shift_prev(hid_a)
         narrow_own = functools.partial(
             pl.pallas_call,
             narrow_own_kernel,
@@ -474,7 +523,7 @@
             in_specs=[SMEM_SPEC] * 4 + [VMEM_SPEC],
             out_specs=VMEM_SPEC,
             scratch_shapes=thin4,
-            compiler_params=params(),
+            compiler_params=params(10),
             cost_estimate=pl.CostEstimate(flops=200000000000, bytes_accessed=8000000, transcendentals=0),
         )
         z_own = narrow_own(name="two_own")(s, d, wc, n_own, t2)
@@ -485,43 +534,45 @@
             in_specs=[SMEM_SPEC] * 4 + [VMEM_SPEC] * 5,
             out_specs=[VMEM_SPEC] * 4,
             scratch_shapes=[pltpu.VMEM((2 * halo, LANES), F32)] + thin4,
-            compiler_params=params(),
+            compiler_params=params(12),
             name="logits",
         )(s, d, wc, n_hal, z_own, th_prev, th_next, marks, count)
         rz_next = shift_prev(bz_prev)
         rz_prev = shift_next(bz_next)
+        late_b, _ = lax.optimization_barrier((hid_b, bz_prev))
+        hb_prev, hb_next = shift_next(late_b), shift_prev(late_b)
         dt2_own = narrow_own(name="two_back_own")(d, s, wc, n_own, dz)
-        dt2, dy, by_prev, by_next = pl.pallas_call(
+        w2t = w2.T
+        dt2, dy = pl.pallas_call(
             hidden_grad_kernel,
-            out_shape=[sds((n_loc, LANES), BF16), sds((quad, LANES), F32), sds((4 * halo, LANES), F32), sds((4 * halo, LANES), F32)],
-            in_specs=[SMEM_SPEC] * 5 + [VMEM_SPEC] * 5,
-            out_specs=[VMEM_SPEC] * 4,
-            scratch_shapes=wide4,
-            compiler_params=params(),
+            out_shape=[sds((n_loc, LANES), BF16), sds((quad, LANES), F32)],
+            in_specs=[SMEM_SPEC] + [VMEM_SPEC] * 6,
+            out_specs=[VMEM_SPEC] * 2,
+            scratch_shapes=thin4,
+            compiler_params=params(16),
             name="hidden_grad",
-        )(s4, d4, wc, n_hal, ids, dt2_own, rz_next, rz_prev, hid, w2.T)
-        ry_next = shift_prev(by_prev)
-        ry_prev = shift_next(by_next)
+        )(ids, dt2_own, rz_next, rz_prev, hid_a, hid_b, w2t)
+        dt_prev, dt_next = shift_next(dt2), shift_prev(dt2)
         dt1_own = pl.pallas_call(
             wide_own_kernel,
             out_shape=sds((quad, LANES), F32),
             in_specs=[SMEM_SPEC] * 4 + [VMEM_SPEC],
             out_specs=VMEM_SPEC,
             scratch_shapes=wide4,
-            compiler_params=params(),
+            compiler_params=params(28),
             cost_estimate=pl.CostEstimate(flops=200000000000, bytes_accessed=8000000, transcendentals=0),
             name="one_back_own",
         )(d4, s4, wc, n_own, dy)
-        grad_two = lax.dot_general(hid, dt2, CONTRACT_ROWS, preferred_element_type=F32)
+        grad_two = jnp.concatenate([lax.dot_general(h, dt2, CONTRACT_ROWS, preferred_element_type=F32) for h in (hid_a, hid_b)])
         dt1 = pl.pallas_call(
-            table_grad_kernel,
+            functools.partial(table_grad_kernel, rows),
             out_shape=sds((n_loc, f_hid), BF16),
-            in_specs=[SMEM_SPEC] + [VMEM_SPEC] * 3,
+            in_specs=[SMEM_SPEC] * 5 + [VMEM_SPEC] * 8,
             out_specs=VMEM_SPEC,
-            scratch_shapes=wide4,
-            compiler_params=params(),
+            scratch_shapes=[pltpu.VMEM((quad, LANES), F32)] + wide4,
+            compiler_params=params(40),
             name="table_grad",
-        )(ids * 4, dt1_own, ry_next, ry_prev)
+        )(ids * 4, code_next.reshape(-1), w_next.reshape(-1), code_prev.reshape(-1), w_prev.reshape(-1), dt1_own, dt_next, ha_next, hb_next, dt_prev, ha_prev, hb_prev, w2t)
         grad_one = lax.dot_general(x, dt1, CONTRACT_ROWS, preferred_element_type=F32)
         grad_one, grad_two, loss = pl.pallas_call(
             functools.partial(reduce_kernel, num_dev),
@@ -536,7 +587,7 @@
                 pltpu.SemaphoreType.DMA((22,)), pltpu.SemaphoreType.DMA((22,)),
                 pltpu.SemaphoreType.DMA((num_dev - 1,)), pltpu.SemaphoreType.DMA((num_dev - 1,)),
             ],
-            compiler_params=params(collective_id=1, has_side_effects=True),
+            compiler_params=params(8, collective_id=1, has_side_effects=True),
             name="reduce",
         )(grad_one, grad_two, loss)
         mean_loss = jnp.sum(loss) / count[0, 0]

time: 258 us -> 213 us (0.83); the launches traced: 262 us -> 212 us
  Pallas kernels: 185 us -> 148 us
  starting transfers between devices: 25.3 us -> 15.3 us
  local copies, waits for them, and re-layouts: 14 us -> 10.9 us
    ppermute x4 -> x6, starting transfers between devices: 24.4 us -> 14.8 us  [shift_prev(): return lax.ppermute(a, GRAPH_AXIS, to_prev)]
    pallas_call x1, Pallas kernels: 16.6 us -> 7.26 us  [device_step(): pl.pallas_call(hidden_grad_kernel, out_shape=[sds((n_loc, LANES), BF16),...]
    pallas_call x1, Pallas kernels: 23.5 us -> 15.5 us  [device_step(): pl.pallas_call(wide_own_kernel, out_shape=sds((quad, LANES), F32), in_spe...]
    pallas_call x1, Pallas kernels: 25.3 us -> 17.4 us  [device_step(): pl.pallas_call(one_own_kernel, out_shape=sds((quad, LANES), F32), in_spec...]
    ppermute x4 -> x6, waiting for transfers between devices: 6.47 us -> 14 us  [shift_next(): return lax.ppermute(a, GRAPH_AXIS, to_next)]
    pallas_call x1, Pallas kernels: 20.4 us -> 13.6 us  [device_step(): z_own = narrow_own(name='two_own')(s, d, wc, n_own, t2)]
    pallas_call x1, Pallas kernels: 20.3 us -> 13.6 us  [device_step(): dt2_own = narrow_own(name='two_back_own')(d, s, wc, n_own, dz)]
    ppermute x4 -> x6, waiting for transfers between devices: 13.5 us -> 7.54 us  [shift_prev(): return lax.ppermute(a, GRAPH_AXIS, to_prev)]
  transfers between devices with their start and end apart: 8 -> 12, of which waited for: 2 -> 3; matrix products, arithmetic and copies ran while one was open for 6% -> 2% of each run, Pallas kernels for 39% -> 40%
where the time goes in v2:
time: 213 us; the launch traced here: 212 us
  Pallas kernels  148 us (69%)
  waiting for transfers between devices  21.5 us (10%)
  starting transfers between devices  15.3 us (7%)
  local copies, waits for them, and re-layouts  10.9 us (5%)
  other arithmetic  9.41 us (4%)
  matrix products  4.3 us (2%)
  between operations  3.49 us (2%)
    pallas_call x1, Pallas kernels, device_step(): pl.pallas_call(functools.partial(reduce_kernel, num_dev), out_shape=[sds(...  19.2 us
    pallas_call x1, Pallas kernels, device_step(): pl.pallas_call(functools.partial(logits_kernel, classes), out_shape=[sds(...  17.6 us
    pallas_call x1, Pallas kernels, device_step(): pl.pallas_call(one_own_kernel, out_shape=sds((quad, LANES), F32), in_spec...  17.4 us
    pallas_call x1, Pallas kernels, device_step(): pl.pallas_call(one_halo_kernel, out_shape=[sds((n_loc, f_hid // 2), BF16)...  16.7 us
    pallas_call x1, Pallas kernels, device_step(): pl.pallas_call(wide_own_kernel, out_shape=sds((quad, LANES), F32), in_spe...  15.5 us
    ppermute x6, starting transfers between devices, shift_prev(): return lax.ppermute(a, GRAPH_AXIS, to_prev)  14.8 us
    ppermute x6, waiting for transfers between devices, shift_next(): return lax.ppermute(a, GRAPH_AXIS, to_next)  14 us
    pallas_call x1, Pallas kernels, device_step(): pl.pallas_call(functools.partial(table_grad_kernel, rows), out_shape=sds(...  13.8 us
  transfers between devices with their start and end apart: 12, of which 3 were waited for; matrix products, arithmetic and copies ran while one was open for 2% of the time, Pallas kernels for 40%

profile of v2, /device:TPU:0, one launch (start us, length us, event | category | flops | bytes accessed | tf_op | source)
XLA Modules:
  0.0 212.4 jit_solution(8107708008190274081)
XLA Ops:
  3.6 2.8 %select_reduce_fusion = f32[32,384]{1,0:T(8,128)S(1)} fusion(f32[32,256]{1,0:T(8,128)S(1)} %reshape.60, s32[32,256]{1,0:T(8,128)S(1)} %get-tuple-element.76), kind=kLoop, calls=%fused_computation | loop fusion | flops 9424896 | bytes 114688 | tf_op jit(solution)/shard_map/reduce_sum | solution.py:451
  6.4 2.8 %select_reduce_fusion.1 = s32[32,384]{1,0:T(8,128)S(1)} fusion(s32[32,256]{1,0:T(8,128)S(1)} %get-tuple-element.75, s32[32,256]{1,0:T(8,128)S(1)} %get-tuple-element.76), kind=kLoop, calls=%fused_computation.1 | loop fusion | flops 9424896 | bytes 114688 | tf_op jit(solution)/shard_map/reduce_sum | solution.py:450
  13.0 8.0 %lists.1 = (f32[8,128]{1,0:T(8,128)S(1)}, s32[104,128]{1,0:T(8,128)S(1)}, s32[104,128]{1,0:T(8,128)S(1)}, f32[96,128]{1,0:T(8,128)S(1)}, f32[96,128]{1,0:T(8,128)S(1)}) custom-call(f32[8,128]{1,0:T(8,128)S(1)} %broadcast_in_dim.50.part, s32[104,128]{1,0:T(8,128)S(1)} %bitcast.17, f32[96,128]{1,0:T(8,128)S(1)} %reshape_reshape.3.wgt), custom_call_target="tpu_custom_call" | custom-call | tf_op jit(solution)/shard_map/lists/pallas_call | solution.py:472
  21.1 4.9 %halo_rows.1 = (bf16[1024,256]{1,0:T(8,128)(2,1)}, bf16[1024,256]{1,0:T(8,128)(2,1)}) custom-call(s32[2048]{0:T(1024)S(1)} %get-tuple-element.69.ids2, bf16[2048,256]{1,0:T(8,128)(2,1)S(1)} %pad.12.x), custom_call_target="tpu_custom_call" | custom-call | tf_op jit(solution)/shard_map/halo_rows/pallas_call | solution.py:484
  26.4 2.2 %collective-permute-start.1 = (bf16[1024,256]{1,0:T(8,128)(2,1)}, bf16[1024,256]{1,0:T(8,128)(2,1)}, u32[]{:S(2)}, u32[]{:S(2)}) collective-permute-start(bf16[1024,256]{1,0:T(8,128)(2,1)} %get-tuple-element.34), channel_id=1, source_target_pairs={{0,7},{1,0},{2,1},{3,2},{4,3},{5,4},{6,5},{7,6}} | collective-permute-start | bytes 1572872 | tf_op jit(solution)/shard_map/ppermute | solution.py:430
  28.8 17.4 %one_own.1.y_own = f32[8192,128]{1,0:T(8,128)S(1)} custom-call(s32[12288]{0:T(1024)S(1)} %get-tuple-element.59.s4.to, s32[12288]{0:T(1024)S(1)} %get-tuple-element.65.d4.frm, f32[12288]{0:T(1024)S(1)} %reshape.68.w, s32[32]{0:T(128)S(1)} %get-tuple-element.74.cnt, bf16[2048,256]{1,0:T(8,128)(2,1)S(1)} %pad.12.x, bf16[256,512]{1,0:T(8,128)(2,1)S(1)} %pad.13.w1), custom_call_target="tpu_custom_call" | custom-call | flops 199999995904 | bytes 8000000 | tf_op jit(solution)/shard_map/one_own/pallas_call | solution.py:497
  46.2 1.9 copy-done
  49.5 2.2 %copy-done.1 = f32[8192,128]{1,0:T(8,128)S(1)} copy-done((f32[8192,128]{1,0:T(8,128)S(1)}, f32[8192,128]{1,0:T(8,128)}, u32[]{:S(2)}) %copy-start.1) | copy-done | bytes 4194328
  51.7 16.7 %one_halo.1 = (bf16[2048,256]{1,0:T(8,128)(2,1)}, bf16[2048,256]{1,0:T(8,128)(2,1)}, f32[2048,128]{1,0:T(8,128)S(1)}, bf16[1024,128]{1,0:T(8,128)(2,1)}, bf16[1024,128]{1,0:T(8,128)(2,1)}) custom-call(s32[12288]{0:T(1024)S(1)} %get-tuple-element.59.s4.to, s32[12288]{0:T(1024)S(1)} %get-tuple-element.65.d4.frm, f32[12288]{0:T(1024)S(1)} %reshape.68.w, ...), custom_call_target="tpu_custom_call" | custom-call | tf_op jit(solution)/shard_map/one_halo/pallas_call | solution.py:507
  68.4 2.6 %collective-permute-start.7 = (bf16[2048,256]{1,0:T(8,128)(2,1)}, bf16[2048,256]{1,0:T(8,128)(2,1)}, u32[]{:S(2)}, u32[]{:S(2)}) collective-permute-start(bf16[2048,256]{1,0:T(8,128)(2,1)} %get-tuple-element.42.hid_a), channel_id=1, source_target_pairs={{0,7},{1,0},{2,1},{3,2},{4,3},{5,4},{6,5},{7,6}} | collective-permute-start | bytes 3145736 | tf_op jit(solution)/shard_map/ppermute | solution.py:430
  71.1 2.6 %collective-permute-start.3 = (bf16[1024,128]{1,0:T(8,128)(2,1)}, bf16[1024,128]{1,0:T(8,128)(2,1)}, u32[]{:S(2)}, u32[]{:S(2)}) collective-permute-start(bf16[1024,128]{1,0:T(8,128)(2,1)} %get-tuple-element.37), channel_id=1, source_target_pairs={{0,7},{1,0},{2,1},{3,2},{4,3},{5,4},{6,5},{7,6}} | collective-permute-start | bytes 786440 | tf_op jit(solution)/shard_map/ppermute | solution.py:430
  73.7 13.6 %two_own.1.z_own = f32[2048,128]{1,0:T(8,128)S(1)} custom-call(s32[12288]{0:T(1024)S(1)} %get-tuple-element.60.frm.s.to, s32[12288]{0:T(1024)S(1)} %get-tuple-element.66.to.d.frm, f32[12288]{0:T(1024)S(1)} %reshape.68.w, s32[32]{0:T(128)S(1)} %get-tuple-element.74.cnt, f32[2048,128]{1,0:T(8,128)S(1)} %get-tuple-element.35.table), custom_call_target="tpu_custom_call" | custom-call | flops 199999995904 | bytes 8000000 | tf_op jit(solution)/shard_map/two_own/pallas_call | solution.py:529
  87.3 11.9 %collective-permute-done.2.t_prev = bf16[1024,128]{1,0:T(8,128)(2,1)} collective-permute-done((bf16[1024,128]{1,0:T(8,128)(2,1)}, bf16[1024,128]{1,0:T(8,128)(2,1)}, u32[]{:S(2)}, u32[]{:S(2)}) %collective-permute-start.2) | collective-permute-done | bytes 262176 | tf_op jit(solution)/shard_map/ppermute | solution.py:427
  99.5 17.6 %logits.1 = (f32[2048,128]{1,0:T(8,128)S(1)}, f32[1024,128]{1,0:T(8,128)}, f32[1024,128]{1,0:T(8,128)}, f32[8,128]{1,0:T(8,128)S(1)}) custom-call(s32[12288]{0:T(1024)S(1)} %get-tuple-element.60.frm.s.to, s32[12288]{0:T(1024)S(1)} %get-tuple-element.66.to.d.frm, f32[12288]{0:T(1024)S(1)} %reshape.68.w, s32[32]{0:T(128)S(1)} %get-tuple-element.57.cnt, ...), custom_call_target="tpu_custom_call" | custom-call | tf_op jit(solution)/shard_map/logits/pallas_call | solution.py:531
  117.0 2.8 %collective-permute-start.4 = (f32[1024,128]{1,0:T(8,128)}, f32[1024,128]{1,0:T(8,128)}, u32[]{:S(2)}, u32[]{:S(2)}) collective-permute-start(f32[1024,128]{1,0:T(8,128)} %get-tuple-element.40), channel_id=1, source_target_pairs={{0,7},{1,0},{2,1},{3,2},{4,3},{5,4},{6,5},{7,6}} | collective-permute-start | bytes 1572872 | tf_op jit(solution)/shard_map/ppermute | solution.py:430
  119.8 13.6 %two_back_own.1.own = f32[2048,128]{1,0:T(8,128)S(1)} custom-call(s32[12288]{0:T(1024)S(1)} %get-tuple-element.66.to.d.frm, s32[12288]{0:T(1024)S(1)} %get-tuple-element.60.frm.s.to, f32[12288]{0:T(1024)S(1)} %reshape.68.w, s32[32]{0:T(128)S(1)} %get-tuple-element.74.cnt, f32[2048,128]{1,0:T(8,128)S(1)} %get-tuple-element.39.table), custom_call_target="tpu_custom_call" | custom-call | flops 199999995904 | bytes 8000000 | tf_op jit(solution)/shard_map/two_back_own/pallas_call | solution.py:544
  133.5 3.3 %collective-permute-start.8 = (bf16[2048,256]{1,0:T(8,128)(2,1)}, bf16[2048,256]{1,0:T(8,128)(2,1)}, u32[]{:S(2)}, u32[]{:S(2)}) collective-permute-start(bf16[2048,256]{1,0:T(8,128)(2,1)} %get-tuple-element.46.hid_b), channel_id=1, source_target_pairs={{0,7},{1,0},{2,1},{3,2},{4,3},{5,4},{6,5},{7,6}} | collective-permute-start | bytes 3145736 | tf_op jit(solution)/shard_map/ppermute | solution.py:430
  136.8 7.3 %hidden_grad.1 = (bf16[2048,128]{1,0:T(8,128)(2,1)S(1)}, f32[8192,128]{1,0:T(8,128)S(1)}) custom-call(s32[2048]{0:T(1024)S(1)} %get-tuple-element.71.ids, f32[2048,128]{1,0:T(8,128)S(1)} %two_back_own.1.own, f32[1024,128]{1,0:T(8,128)} %collective-permute-done.4.ret_next, f32[1024,128]{1,0:T(8,128)} %collective-permute-done.5.ret_prev, ...), custom_call_target="tpu_custom_call" | custom-call | tf_op jit(solution)/shard_map/hidden_grad/pallas_call | solution.py:546
  144.1 15.5 %one_back_own.1.own = f32[8192,128]{1,0:T(8,128)S(1)} custom-call(s32[12288]{0:T(1024)S(1)} %get-tuple-element.65.d4.frm, s32[12288]{0:T(1024)S(1)} %get-tuple-element.59.s4.to, f32[12288]{0:T(1024)S(1)} %reshape.68.w, s32[32]{0:T(128)S(1)} %get-tuple-element.74.cnt, f32[8192,128]{1,0:T(8,128)S(1)} %get-tuple-element.44.table), custom_call_target="tpu_custom_call" | custom-call | flops 199999995904 | bytes 8000000 | tf_op jit(solution)/shard_map/one_back_own/pallas_call | solution.py:556
  160.8 1.7 fusion.12
  164.3 7.5 %collective-permute-done.6.tn = bf16[2048,128]{1,0:T(8,128)(2,1)S(1)} collective-permute-done((bf16[2048,128]{1,0:T(8,128)(2,1)S(1)}, bf16[2048,128]{1,0:T(8,128)(2,1)S(1)}, u32[]{:S(2)}, u32[]{:S(2)}) %collective-permute-start.6) | collective-permute-done | bytes 524320 | tf_op jit(solution)/shard_map/ppermute | solution.py:430
  171.8 2.1 %collective-permute-done.9.tp = bf16[2048,128]{1,0:T(8,128)(2,1)S(1)} collective-permute-done((bf16[2048,128]{1,0:T(8,128)(2,1)S(1)}, bf16[2048,128]{1,0:T(8,128)(2,1)S(1)}, u32[]{:S(2)}, u32[]{:S(2)}) %collective-permute-start.9) | collective-permute-done | bytes 524320 | tf_op jit(solution)/shard_map/ppermute | solution.py:427
  174.0 13.8 %table_grad.1 = bf16[2048,512]{1,0:T(8,128)(2,1)S(1)} custom-call(s32[2048]{0:T(1024)S(1)} %get-tuple-element.70.ids4, s32[13312]{0:T(1024)S(1)} %bitcast.19, f32[12288]{0:T(1024)S(1)} %bitcast.21, s32[13312]{0:T(1024)S(1)} %bitcast.18, f32[12288]{0:T(1024)S(1)} %bitcast.20, f32[8192,128]{1,0:T(8,128)S(1)} %one_back_own.1.own, ...), custom_call_target="tpu_custom_call" | custom-call | tf_op jit(solution)/shard_map/table_grad/pallas_call | solution.py:567
  188.5 19.2 %reduce.1 = (f32[256,512]{1,0:T(8,128)S(1)}, f32[512,128]{1,0:T(8,128)S(1)}, f32[8,128]{1,0:T(8,128)S(1)}) custom-call(f32[256,512]{1,0:T(8,128)S(1)} %fusion.7.g1, f32[512,128]{1,0:T(8,128)S(1)} %pad_maximum_fusion.g2, f32[8,128]{1,0:T(8,128)S(1)} %get-tuple-element.47.loss), custom_call_target="tpu_custom_call" | custom-call | tf_op jit(solution)/shard_map/reduce/pallas_call | solution.py:577
  (78 shorter events, 14.8 us)
Async XLA Ops:
  0.6 20.4 %copy-start.11 = (s32[2,1024]{1,0:T(2,128)S(1)}, s32[2,1024]{1,0:T(2,128)}, u32[]{:S(2)}) copy-start(s32[2,1024]{1,0:T(2,128)} %param.12) | copy-start | bytes 24580
  0.6 28.0 %copy-start.6 = (f32[200,512]{1,0:T(8,128)S(1)}, f32[200,512]{1,0:T(8,128)}, u32[]{:S(2)}) copy-start(f32[200,512]{1,0:T(8,128)} %param.10) | copy-start | bytes 1228804
  10.7 35.4 %copy-start.4 = (bf16[2048,200]{1,0:T(8,128)(2,1)}, bf16[2048,200]{1,0:T(8,128)(2,1)S(1)}, u32[]{:S(2)}) copy-start(bf16[2048,200]{1,0:T(8,128)(2,1)S(1)} %copy.15) | copy-start | bytes 2457604
  26.0 23.6 %collective-permute-start = (bf16[1024,256]{1,0:T(8,128)(2,1)}, bf16[1024,256]{1,0:T(8,128)(2,1)}, u32[]{:S(2)}, u32[]{:S(2)}) collective-permute-start(bf16[1024,256]{1,0:T(8,128)(2,1)} %get-tuple-element.33), channel_id=1, source_target_pairs={{0,1},{1,2},{2,3},{3,4},{4,5},{5,6},{6,7},{7,0}} | collective-permute-start | bytes 1572872 | tf_op jit(solution)/shard_map/ppermute | solution.py:427
  26.4 23.1 %collective-permute-start.1 = (bf16[1024,256]{1,0:T(8,128)(2,1)}, bf16[1024,256]{1,0:T(8,128)(2,1)}, u32[]{:S(2)}, u32[]{:S(2)}) collective-permute-start(bf16[1024,256]{1,0:T(8,128)(2,1)} %get-tuple-element.34), channel_id=1, source_target_pairs={{0,7},{1,0},{2,1},{3,2},{4,3},{5,4},{6,5},{7,6}} | collective-permute-start | bytes 1572872 | tf_op jit(solution)/shard_map/ppermute | solution.py:430
  28.7 19.4 %copy-start.7 = (f32[512,107]{0,1:T(8,128)S(1)}, f32[512,107]{0,1:T(8,128)}, u32[]{:S(2)}) copy-start(f32[512,107]{0,1:T(8,128)} %param.11) | copy-start | bytes 657412
  28.8 20.1 %copy-start.9 = (s32[2048]{0:T(1024)S(1)}, s32[2048]{0:T(1024)}, u32[]{:S(2)}) copy-start(s32[2048]{0:T(1024)} %param.17) | copy-start | bytes 24580
  28.8 20.1 %copy-start.10 = (s32[2048]{0:T(1024)S(1)}, s32[2048]{0:T(1024)}, u32[]{:S(2)}) copy-start(s32[2048]{0:T(1024)} %param.16) | copy-start | bytes 24580
  46.2 1.9 copy-start
  48.9 87.9 %copy-start.2 = (bf16[128,512]{1,0:T(8,128)(2,1)}, bf16[128,512]{1,0:T(8,128)(2,1)S(1)}, u32[]{:S(2)}) copy-start(bf16[128,512]{1,0:T(8,128)(2,1)S(1)} %pad_bitcast_fusion.w2t) | copy-start | bytes 393220
  49.5 2.2 %copy-start.1 = (f32[8192,128]{1,0:T(8,128)S(1)}, f32[8192,128]{1,0:T(8,128)}, u32[]{:S(2)}) copy-start(f32[8192,128]{1,0:T(8,128)} %copy-done) | copy-start | bytes 12582916
  68.4 92.4 %collective-permute-start.10 = (bf16[2048,256]{1,0:T(8,128)(2,1)}, bf16[2048,256]{1,0:T(8,128)(2,1)}, u32[]{:S(2)}, u32[]{:S(2)}) collective-permute-start(bf16[2048,256]{1,0:T(8,128)(2,1)} %get-tuple-element.42.hid_a), channel_id=1, source_target_pairs={{0,1},{1,2},{2,3},{3,4},{4,5},{5,6},{6,7},{7,0}} | collective-permute-start | bytes 3145736 | tf_op jit(solution)/shard_map/ppermute | solution.py:427
  68.4 95.8 %collective-permute-start.7 = (bf16[2048,256]{1,0:T(8,128)(2,1)}, bf16[2048,256]{1,0:T(8,128)(2,1)}, u32[]{:S(2)}, u32[]{:S(2)}) collective-permute-start(bf16[2048,256]{1,0:T(8,128)(2,1)} %get-tuple-element.42.hid_a), channel_id=1, source_target_pairs={{0,7},{1,0},{2,1},{3,2},{4,3},{5,4},{6,5},{7,6}} | collective-permute-start | bytes 3145736 | tf_op jit(solution)/shard_map/ppermute | solution.py:430
  71.1 28.1 %collective-permute-start.2 = (bf16[1024,128]{1,0:T(8,128)(2,1)}, bf16[1024,128]{1,0:T(8,128)(2,1)}, u32[]{:S(2)}, u32[]{:S(2)}) collective-permute-start(bf16[1024,128]{1,0:T(8,128)(2,1)} %get-tuple-element.36), channel_id=1, source_target_pairs={{0,1},{1,2},{2,3},{3,4},{4,5},{5,6},{6,7},{7,0}} | collective-permute-start | bytes 786440 | tf_op jit(solution)/shard_map/ppermute | solution.py:427
  71.1 28.1 %collective-permute-start.3 = (bf16[1024,128]{1,0:T(8,128)(2,1)}, bf16[1024,128]{1,0:T(8,128)(2,1)}, u32[]{:S(2)}, u32[]{:S(2)}) collective-permute-start(bf16[1024,128]{1,0:T(8,128)(2,1)} %get-tuple-element.37), channel_id=1, source_target_pairs={{0,7},{1,0},{2,1},{3,2},{4,3},{5,4},{6,5},{7,6}} | collective-permute-start | bytes 786440 | tf_op jit(solution)/shard_map/ppermute | solution.py:430
  73.7 25.4 %copy-start.8 = (s32[2048]{0:T(1024)S(1)}, s32[2048]{0:T(1024)}, u32[]{:S(2)}) copy-start(s32[2048]{0:T(1024)} %compare_select_fusion) | copy-start | bytes 24580
  117.0 16.4 %collective-permute-start.4 = (f32[1024,128]{1,0:T(8,128)}, f32[1024,128]{1,0:T(8,128)}, u32[]{:S(2)}, u32[]{:S(2)}) collective-permute-start(f32[1024,128]{1,0:T(8,128)} %get-tuple-element.40), channel_id=1, source_target_pairs={{0,7},{1,0},{2,1},{3,2},{4,3},{5,4},{6,5},{7,6}} | collective-permute-start | bytes 1572872 | tf_op jit(solution)/shard_map/ppermute | solution.py:430
  119.8 17.0 %collective-permute-start.5 = (f32[1024,128]{1,0:T(8,128)}, f32[1024,128]{1,0:T(8,128)}, u32[]{:S(2)}, u32[]{:S(2)}) collective-permute-start(f32[1024,128]{1,0:T(8,128)} %get-tuple-element.41), channel_id=1, source_target_pairs={{0,1},{1,2},{2,3},{3,4},{4,5},{5,6},{6,7},{7,0}} | collective-permute-start | bytes 1572872 | tf_op jit(solution)/shard_map/ppermute | solution.py:427
  133.4 30.9 %collective-permute-start.11 = (bf16[2048,256]{1,0:T(8,128)(2,1)}, bf16[2048,256]{1,0:T(8,128)(2,1)}, u32[]{:S(2)}, u32[]{:S(2)}) collective-permute-start(bf16[2048,256]{1,0:T(8,128)(2,1)} %get-tuple-element.46.hid_b), channel_id=1, source_target_pairs={{0,1},{1,2},{2,3},{3,4},{4,5},{5,6},{6,7},{7,0}} | collective-permute-start | bytes 3145736 | tf_op jit(solution)/shard_map/ppermute | solution.py:427
  133.5 30.8 %collective-permute-start.8 = (bf16[2048,256]{1,0:T(8,128)(2,1)}, bf16[2048,256]{1,0:T(8,128)(2,1)}, u32[]{:S(2)}, u32[]{:S(2)}) collective-permute-start(bf16[2048,256]{1,0:T(8,128)(2,1)} %get-tuple-element.46.hid_b), channel_id=1, source_target_pairs={{0,7},{1,0},{2,1},{3,2},{4,3},{5,4},{6,5},{7,6}} | collective-permute-start | bytes 3145736 | tf_op jit(solution)/shard_map/ppermute | solution.py:430
  144.1 29.9 %copy-start.3 = (bf16[128,512]{1,0:T(8,128)(2,1)S(1)}, bf16[128,512]{1,0:T(8,128)(2,1)}, u32[]{:S(2)}) copy-start(bf16[128,512]{1,0:T(8,128)(2,1)} %copy-done.2) | copy-start | bytes 393220
  159.7 12.2 %collective-permute-start.6 = (bf16[2048,128]{1,0:T(8,128)(2,1)S(1)}, bf16[2048,128]{1,0:T(8,128)(2,1)S(1)}, u32[]{:S(2)}, u32[]{:S(2)}) collective-permute-start(bf16[2048,128]{1,0:T(8,128)(2,1)S(1)} %get-tuple-element.45), channel_id=1, source_target_pairs={{0,7},{1,0},{2,1},{3,2},{4,3},{5,4},{6,5},{7,6}} | collective-permute-start | bytes 1572872 | tf_op jit(solution)/shard_map/ppermute | solution.py:430
  160.8 13.1 %collective-permute-start.9 = (bf16[2048,128]{1,0:T(8,128)(2,1)S(1)}, bf16[2048,128]{1,0:T(8,128)(2,1)S(1)}, u32[]{:S(2)}, u32[]{:S(2)}) collective-permute-start(bf16[2048,128]{1,0:T(8,128)(2,1)S(1)} %get-tuple-element.45), channel_id=1, source_target_pairs={{0,1},{1,2},{2,3},{3,4},{4,5},{5,6},{6,7},{7,0}} | collective-permute-start | bytes 1572872 | tf_op jit(solution)/shard_map/ppermute | solution.py:427
  174.0 13.8 %copy-start.5 = (bf16[2048,200]{1,0:T(8,128)(2,1)S(1)}, bf16[2048,200]{1,0:T(8,128)(2,1)}, u32[]{:S(2)}) copy-start(bf16[2048,200]{1,0:T(8,128)(2,1)} %copy-done.4) | copy-start | bytes 2457604

commit v3 on v2

--- a/solution.py
+++ b/solution.py
@@ -10,6 +10,7 @@
 
 GRAPH_AXIS = "graph"
 CONTRACT_ROWS = (((0,), (0,)), ((), ()))
+CONTRACT_COLS = (((1,), (1,)), ((), ()))
 MESH = pl.DeviceIdType.MESH
 F32 = jnp.float32
 BF16 = jnp.bfloat16
@@ -58,12 +59,12 @@
 
         def body(j, _):
             off = r * SLOT + (SLOT - unroll - j * unroll if back else j * unroll)
-            frm, to, wgt = (ref.at[pl.ds(off, unroll)] for ref in (from_ref, to_ref, w_ref))
-            for u in range(unroll):
-                acc = accs[u % n_acc]
-                val = table[pl.ds(pl.multiple_of(frm[u], width), width), :] * wgt[u]
-                at = pl.ds(pl.multiple_of(to[u], width), width)
-                acc[at, :] = acc[at, :] + val
+            vals = [table[pl.ds(pl.multiple_of(from_ref[off + u], width), width), :] * w_ref[off + u] for u in range(unroll)]
+            for g in range(unroll // n_acc):
+                rows = [pl.multiple_of(to_ref[off + g * n_acc + k], width) for k in range(n_acc)]
+                old = [accs[k][pl.ds(rows[k], width), :] for k in range(n_acc)]
+                for k in range(n_acc):
+                    accs[k][pl.ds(rows[k], width), :] = old[k] + vals[g * n_acc + k]
             return 0
 
         lax.fori_loop(0, blocks, body, 0)
@@ -121,7 +122,9 @@
     return copy
 
 
-def lists_kernel(num_dev, part, code, wgt, count, code_prev, code_next, w_prev, w_next, slots, send_sem, recv_sem, lsend, lrecv):
+def lists_kernel(num_dev, mask, code, wgt, count, code_prev, code_next, w_prev, w_next, part, slots, send_sem, recv_sem, lsend, lrecv):
+    ones = jnp.sum(jnp.sum(mask[...].astype(F32), axis=1, keepdims=True), axis=0, keepdims=True)
+    part[...] = jnp.broadcast_to(ones, part.shape)
     me = lax.axis_index(GRAPH_AXIS)
     succ, pred = lax.rem(me + 1, num_dev), lax.rem(me + num_dev - 1, num_dev)
     enter(me, num_dev)
@@ -144,7 +147,9 @@
     rows = x.shape[0]
 
     def put(i, _):
-        spread(table, i * 256, x[pl.ds(i * 256, 256), :].astype(F32))
+        block = x[pl.ds(i * 256, 256), :].astype(F32)
+        pad = jnp.zeros((256, 2 * LANES - block.shape[1]), F32)
+        spread(table, i * 256, jnp.concatenate([block, pad], axis=1))
         return 0
 
     lax.fori_loop(0, rows // 256, put, 0)
@@ -168,23 +173,23 @@
         return 0
 
     lax.fori_loop(0, x.shape[0] // 256, put, 0)
-    edge_pass(s4, d4, w, cnt, table, accs, 4, 32, False)
+    edge_pass(s4, d4, w, cnt, table, accs, 4, 16, False)
     sum_rows(y, accs)
 
 
-def one_halo_kernel(s4, d4, w, cnt, ids, y_own, x_prev, x_next, w1, w2, hid_a, hid_b, t2, to_next, to_prev, table, picked, *accs):
+def one_halo_kernel(s4, d4, w, cnt, ids, y_own, x_prev, x_next, w1, w2t, hid_a, hid_b, t2, to_next, to_prev, table, picked, *accs):
     zero_rows(accs)
     half = x_prev.shape[0]
 
     def put(i, _):
-        t = jnp.dot(x_prev[pl.ds(i * 256, 256), :], w1[...], preferred_element_type=F32)
+        t = jnp.dot(x_prev[pl.ds(i * 256, 256), :w1.shape[0]], w1[...], preferred_element_type=F32)
         spread(table, i * 256, t.astype(BF16).astype(F32))
-        t = jnp.dot(x_next[pl.ds(i * 256, 256), :], w1[...], preferred_element_type=F32)
+        t = jnp.dot(x_next[pl.ds(i * 256, 256), :w1.shape[0]], w1[...], preferred_element_type=F32)
         spread(table, half + i * 256, t.astype(BF16).astype(F32))
         return 0
 
     lax.fori_loop(0, half // 256, put, 0)
-    edge_pass(s4, d4, w, cnt, table, accs, 4, 8, True)
+    edge_pass(s4, d4, w, cnt, table, accs, 4, 16, True)
     sum_rows(accs[0], (y_own,) + accs)
 
     def act(i, _):
@@ -192,7 +197,7 @@
         cut = hid_a.shape[1]
         hid_a[pl.ds(i * 256, 256), :] = h[:, :cut]
         hid_b[pl.ds(i * 256, 256), :] = h[:, cut:]
-        t = jnp.dot(h, w2[...], preferred_element_type=F32)
+        t = lax.dot_general(h, w2t[...], CONTRACT_COLS, preferred_element_type=F32)
         t2[pl.ds(i * 256, 256), :] = t.astype(BF16).astype(F32)
         return 0
 
@@ -209,13 +214,13 @@
 
 def narrow_own_kernel(frm, to, w, cnt, table, out, *accs):
     zero_rows(accs)
-    edge_pass(frm, to, w, cnt, table, accs, 1, 32, False)
+    edge_pass(frm, to, w, cnt, table, accs, 1, 16, False)
     sum_rows(out, accs)
 
 
 def wide_own_kernel(frm, to, w, cnt, table, out, *accs):
     zero_rows(accs)
-    edge_pass(frm, to, w, cnt, table, accs, 4, 32, False)
+    edge_pass(frm, to, w, cnt, table, accs, 4, 16, False)
     sum_rows(out, accs)
 
 
@@ -229,7 +234,7 @@
         return 0
 
     lax.fori_loop(0, half // 256, put, 0)
-    edge_pass(s, d, w, cnt, table, accs, 1, 8, True)
+    edge_pass(s, d, w, cnt, table, accs, 1, 16, True)
     denom = count[0:1, :]
     loss[...] = jnp.zeros_like(loss)
 
@@ -258,7 +263,7 @@
 
     lax.fori_loop(0, dz.shape[0] // 64, soft, 0)
     zero_rows(accs)
-    edge_pass(d, s, w, cnt, dz, accs, 1, 8, True)
+    edge_pass(d, s, w, cnt, dz, accs, 1, 16, True)
 
     def fin(i, _):
         at = pl.ds(i * 64, 64)
@@ -280,11 +285,12 @@
     return jnp.concatenate([lo, hi], axis=1)
 
 
-def hidden_grad_kernel(ids, own, ret_next, ret_prev, hid_a, hid_b, w2t, dt2, dy, *accs):
+def hidden_grad_kernel(ids, own, ret_next, ret_prev, hid_a, hid_b, w2t, dt2, dy, g2, *accs):
     n_loc, half = own.shape[0], ret_next.shape[0]
     zero_rows(accs)
     scatter_pass(ids.at[pl.ds(0, half)], ret_next, accs, 1, 8)
     scatter_pass(ids.at[pl.ds(half, half)], ret_prev, accs, 1, 8)
+    g2[...] = jnp.zeros_like(g2)
 
     def fold(i, _):
         at = pl.ds(i * 256, 256)
@@ -293,6 +299,9 @@
             total = total + acc[at, :]
         dt = total.astype(BF16)
         dt2[at, :] = dt
+        cut = hid_a.shape[1]
+        g2[:cut, :] += lax.dot_general(hid_a[at, :], dt, CONTRACT_ROWS, preferred_element_type=F32)
+        g2[cut:, :] += lax.dot_general(hid_b[at, :], dt, CONTRACT_ROWS, preferred_element_type=F32)
         dh = jnp.dot(dt, w2t[...], preferred_element_type=F32)
         spread(dy, i * 256, masked(dh, hid_a[at, :], hid_b[at, :]))
         return 0
@@ -307,13 +316,13 @@
     shift = n_loc.bit_length() - 1
 
     def row(r, _):
-        first = SLOT - 8 - (code_ref[tally + 2 * rows + r] if far else 0)
+        first = SLOT - 16 - (code_ref[tally + 2 * rows + r] if far else 0)
         edges = code_ref[tally + far * rows + r]
 
         def body(j, _):
-            off = r * SLOT + first - j * 8
-            codes, wgt = (ref.at[pl.ds(off, 8)] for ref in (code_ref, w_ref))
-            for u in range(8):
+            off = r * SLOT + first - j * 16
+            codes, wgt = (ref.at[pl.ds(off, 16)] for ref in (code_ref, w_ref))
+            for u in range(16):
                 acc = accs[u % n_acc]
                 code = codes[u]
                 frm = lax.shift_right_logical(code, shift) * 4
@@ -322,14 +331,15 @@
                 acc[at, :] = acc[at, :] + val
             return 0
 
-        lax.fori_loop(0, lax.shift_right_logical(edges + 7, 3), body, 0)
+        lax.fori_loop(0, lax.shift_right_logical(edges + 15, 4), body, 0)
         return 0
 
     lax.fori_loop(0, rows, row, 0)
 
 
-def table_grad_kernel(rows, ids4, cn, wn, cp, wp, own, tn, han, hbn, tp, hap, hbp, w2t, dt1, table, *accs):
-    zero_rows(accs)
+def table_grad_kernel(rows, ids4, cn, wn, cp, wp, own, tn, han, hbn, tp, hap, hbp, w2t, x, g1, table, *accs):
+    zero_rows(accs)
+    g1[...] = jnp.zeros_like(g1)
 
     def fill(dt, hid_a, hid_b):
         def put(i, _):
@@ -346,13 +356,13 @@
     peer_pass(ids4, cp, wp, rows, 1, table, accs)
 
     def fold(i, _):
-        total = unspread(own, i * 128, 128, 4)
+        total = unspread(own, i * 256, 256, 4)
         for acc in accs:
-            total = total + unspread(acc, i * 128, 128, 4)
-        dt1[pl.ds(i * 128, 128), :] = total.astype(BF16)
-        return 0
-
-    lax.fori_loop(0, dt1.shape[0] // 128, fold, 0)
+            total = total + unspread(acc, i * 256, 256, 4)
+        g1[:x.shape[1], :] += lax.dot_general(x[pl.ds(i * 256, 256), :], total.astype(BF16), CONTRACT_ROWS, preferred_element_type=F32)
+        return 0
+
+    lax.fori_loop(0, x.shape[0] // 256, fold, 0)
 
 
 def reduce_kernel(num_dev, g1, g2, loss, o1, o2, lo, r1, r2, s1, s2, q1, q2, lslots, sem_s, sem_r, lsem_s, lsem_r):
@@ -441,14 +451,14 @@
         rank = jnp.dot(sets, tri, preferred_element_type=F32).astype(jnp.int32)
         counts = jnp.sum(sets.astype(F32), axis=1).astype(jnp.int32)
         n_own, n_near, n_far = counts[:rows], counts[rows:2 * rows], counts[2 * rows:]
-        skip = (n_near + 7) // 8 * 8
+        skip = (n_near + 15) // 16 * 16
         place = jnp.where(far, SLOT - 1 - skip[:, None] - rank[2 * rows:], SLOT)
         place = jnp.where(near, SLOT - 1 - rank[rows:2 * rows], place)
         place = jnp.where(own, rank[:rows], place)
         hit = place[:, :, None] == jnp.arange(SLOT)[None, None, :]
         code = jnp.where(src < n_loc, src, src - n_loc) + dst * n_loc
-        code = jnp.sum(jnp.where(hit, code[:, :, None], 0), axis=1)
-        wc = jnp.sum(jnp.where(hit, w[:, :, None], 0.0), axis=1)
+        picks = (jnp.where(hit, code[:, :, None], 0), jnp.where(hit, w[:, :, None], 0.0))
+        code, wc = lax.reduce(picks, (jnp.int32(0), jnp.float32(0.0)), lambda a, b: (a[0] + b[0], a[1] + b[1]), (1,))
         n_hal = jnp.where(n_far > 0, skip + n_far, n_near)
         return code, wc, n_own, n_hal, n_near, n_far, skip
 
@@ -458,11 +468,10 @@
         f_hid, classes = w_two.shape
         quad = 4 * n_loc
         sds = jax.ShapeDtypeStruct
-        x = jnp.pad(node_feats, ((0, 0), (0, 256 - f_in)))
-        w1 = jnp.pad(w_one.astype(BF16), ((0, 256 - f_in), (0, 0)))
-        w2 = jnp.pad(w_two.astype(BF16), ((0, 0), (0, LANES - classes)))
+        x = node_feats
+        w1 = w_one.astype(BF16)
+        w2t = jnp.pad(w_two.T.astype(BF16), ((0, LANES - classes), (0, 0)))
         ids = jnp.concatenate([send_rows[1], send_rows[0]])
-        mask_count = jnp.sum(label_mask.astype(F32))
         code, wc, n_own, n_hal, n_near, n_far, skip = compact(edge_src, edge_dst, edge_w, n_loc, halo)
         rows = n_own.shape[0]
         slots = code.size // LANES
@@ -474,13 +483,13 @@
             out_shape=[sds((8, LANES), F32)] + [sds((slots + 8, LANES), jnp.int32)] * 2 + [sds((slots, LANES), F32)] * 2,
             in_specs=[VMEM_SPEC] * 3,
             out_specs=[VMEM_SPEC] * 5,
-            scratch_shapes=[pltpu.VMEM((num_dev - 1, 8, LANES), F32)] + [pltpu.SemaphoreType.DMA((n,)) for n in (num_dev - 1, num_dev - 1, 4, 4)],
+            scratch_shapes=[pltpu.VMEM((8, LANES), F32), pltpu.VMEM((num_dev - 1, 8, LANES), F32)] + [pltpu.SemaphoreType.DMA((n,)) for n in (num_dev - 1, num_dev - 1, 4, 4)],
             compiler_params=params(1, collective_id=0, has_side_effects=True),
             name="lists",
-        )(jnp.broadcast_to(mask_count, (8, LANES)), lists, wc.reshape(slots, LANES))
+        )(label_mask.reshape(-1, LANES), lists, wc.reshape(slots, LANES))
         s, d = code % n_loc, code // n_loc
         s4, d4 = s * 4, d * 4
-        count, x_src = lax.optimization_barrier((count, x))
+        count, x = lax.optimization_barrier((count, x))
         x_next, x_prev = pl.pallas_call(
             halo_rows_kernel,
             out_shape=[sds((halo, 256), BF16)] * 2,
@@ -489,11 +498,14 @@
             scratch_shapes=[pltpu.VMEM((2 * n_loc, LANES), F32), pltpu.VMEM((4 * halo, LANES), F32)],
             compiler_params=params(12),
             name="halo_rows",
-        )(ids * 2, x_src)
+        )(ids * 2, x)
         xh_prev = shift_next(x_next)
         xh_next = shift_prev(x_prev)
         wide4 = [pltpu.VMEM((quad, LANES), F32)] * 4
         thin4 = [pltpu.VMEM((n_loc, LANES), F32)] * 4
+        marks = jnp.where(label_mask == 1, labels, -1)
+        ids4 = ids * 4
+        s4, w2t, marks, ids4 = lax.optimization_barrier((s4, w2t, marks, ids4))
         y_own = pl.pallas_call(
             one_own_kernel,
             out_shape=sds((quad, LANES), F32),
@@ -510,9 +522,9 @@
             in_specs=[SMEM_SPEC] * 5 + [VMEM_SPEC] * 5,
             out_specs=[VMEM_SPEC] * 5,
             scratch_shapes=[pltpu.VMEM((4 * 2 * halo, LANES), F32), pltpu.VMEM((2 * halo, LANES), F32)] + wide4,
-            compiler_params=params(30),
+            compiler_params=params(32),
             name="one_halo",
-        )(s4, d4, wc, n_hal, ids, y_own, xh_prev, xh_next, w1, w2)
+        )(s4, d4, wc, n_hal, ids, y_own, xh_prev, xh_next, w1, w2t)
         th_prev = shift_next(t_next)
         th_next = shift_prev(t_prev)
         ha_prev, ha_next = shift_next(hid_a), shift_prev(hid_a)
@@ -527,7 +539,7 @@
             cost_estimate=pl.CostEstimate(flops=200000000000, bytes_accessed=8000000, transcendentals=0),
         )
         z_own = narrow_own(name="two_own")(s, d, wc, n_own, t2)
-        marks = jnp.broadcast_to(jnp.where(label_mask == 1, labels, -1)[:, None], (n_loc, LANES))
+        marks = jnp.broadcast_to(marks[:, None], (n_loc, LANES))
         dz, bz_prev, bz_next, loss = pl.pallas_call(
             functools.partial(logits_kernel, classes),
             out_shape=[sds((n_loc, LANES), F32), sds((halo, LANES), F32), sds((halo, LANES), F32), sds((8, LANES), F32)],
@@ -542,12 +554,11 @@
         late_b, _ = lax.optimization_barrier((hid_b, bz_prev))
         hb_prev, hb_next = shift_next(late_b), shift_prev(late_b)
         dt2_own = narrow_own(name="two_back_own")(d, s, wc, n_own, dz)
-        w2t = w2.T
-        dt2, dy = pl.pallas_call(
+        dt2, dy, grad_two = pl.pallas_call(
             hidden_grad_kernel,
-            out_shape=[sds((n_loc, LANES), BF16), sds((quad, LANES), F32)],
+            out_shape=[sds((n_loc, LANES), BF16), sds((quad, LANES), F32), sds((f_hid, LANES), F32)],
             in_specs=[SMEM_SPEC] + [VMEM_SPEC] * 6,
-            out_specs=[VMEM_SPEC] * 2,
+            out_specs=[VMEM_SPEC] * 3,
             scratch_shapes=thin4,
             compiler_params=params(16),
             name="hidden_grad",
@@ -563,17 +574,15 @@
             cost_estimate=pl.CostEstimate(flops=200000000000, bytes_accessed=8000000, transcendentals=0),
             name="one_back_own",
         )(d4, s4, wc, n_own, dy)
-        grad_two = jnp.concatenate([lax.dot_general(h, dt2, CONTRACT_ROWS, preferred_element_type=F32) for h in (hid_a, hid_b)])
-        dt1 = pl.pallas_call(
+        grad_one = pl.pallas_call(
             functools.partial(table_grad_kernel, rows),
-            out_shape=sds((n_loc, f_hid), BF16),
-            in_specs=[SMEM_SPEC] * 5 + [VMEM_SPEC] * 8,
+            out_shape=sds((256, f_hid), F32),
+            in_specs=[SMEM_SPEC] * 5 + [VMEM_SPEC] * 9,
             out_specs=VMEM_SPEC,
             scratch_shapes=[pltpu.VMEM((quad, LANES), F32)] + wide4,
-            compiler_params=params(40),
+            compiler_params=params(36),
             name="table_grad",
-        )(ids * 4, code_next.reshape(-1), w_next.reshape(-1), code_prev.reshape(-1), w_prev.reshape(-1), dt1_own, dt_next, ha_next, hb_next, dt_prev, ha_prev, hb_prev, w2t)
-        grad_one = lax.dot_general(x, dt1, CONTRACT_ROWS, preferred_element_type=F32)
+        )(ids4, code_next.reshape(-1), w_next.reshape(-1), code_prev.reshape(-1), w_prev.reshape(-1), dt1_own, dt_next, ha_next, hb_next, dt_prev, ha_prev, hb_prev, w2t, x)
         grad_one, grad_two, loss = pl.pallas_call(
             functools.partial(reduce_kernel, num_dev),
             out_shape=[sds((256, f_hid), F32), sds((f_hid, LANES), F32), sds((8, LANES), F32)],

time: 213 us -> 218 us (1.023)
  Pallas kernels: 148 us -> 171 us
  waiting for transfers between devices: 21.5 us -> 14.4 us
  matrix products: 4.3 us -> 0.16 us
  local copies, waits for them, and re-layouts: 10.9 us -> 7.21 us
    reduce_sum x3 -> x0, other arithmetic: 7 us -> none  [the longest x1 2.83 us: compact(): code = jnp.sum(jnp.where(hit, code[:, :, None], 0), axis=1)]
    ppermute x6, waiting for transfers between devices: 7.54 us -> 0.55 us  [shift_prev(): return lax.ppermute(a, GRAPH_AXIS, to_prev)]
    pallas_call x1, Pallas kernels: 15.5 us -> 20.7 us  [device_step(): pl.pallas_call(wide_own_kernel, out_shape=sds((quad, LANES), F32), in_spe...]
    pallas_call x1, Pallas kernels: 13.6 us -> 18.8 us  [device_step(): dt2_own = narrow_own(name='two_back_own')(d, s, wc, n_own, dz)]
    pallas_call x1, Pallas kernels: 13.6 us -> 18.8 us  [device_step(): z_own = narrow_own(name='two_own')(s, d, wc, n_own, t2)]
    unnamed x27 -> x13, local copies, waits for them, and re-layouts: 6.57 us -> 1.55 us
    another operation x0 -> x1, other arithmetic: none -> 4.22 us  [compact(): lax.reduce(picks, (jnp.int32(0), jnp.float32(0.0)), lambda a, b: (a[0] +...]
    dot_general x3 -> x0, matrix products: 4.13 us -> none  [the longest x2 3.4 us: device_step(): lax.dot_general(h, dt2, CONTRACT_ROWS, preferred_element_type=F32)]
  transfers between devices with their start and end apart: 12 -> 12, of which waited for: 3 -> 3; matrix products, arithmetic and copies ran while one was open for 2% -> 0% of each run, Pallas kernels for 40% -> 50%
where the time goes in v3:
time: 218 us
  Pallas kernels  171 us (78%)
  waiting for transfers between devices  14.4 us (7%)
  starting transfers between devices  14.1 us (6%)
  other arithmetic  7.31 us (3%)
  local copies, waits for them, and re-layouts  7.21 us (3%)
  between operations  3.35 us (2%)
    pallas_call x1, Pallas kernels, device_step(): pl.pallas_call(one_own_kernel, out_shape=sds((quad, LANES), F32), in_spec...  21.1 us
    pallas_call x1, Pallas kernels, device_step(): pl.pallas_call(wide_own_kernel, out_shape=sds((quad, LANES), F32), in_spe...  20.7 us
    pallas_call x1, Pallas kernels, device_step(): pl.pallas_call(functools.partial(logits_kernel, classes), out_shape=[sds(...  19.5 us
    pallas_call x1, Pallas kernels, device_step(): dt2_own = narrow_own(name='two_back_own')(d, s, wc, n_own, dz)  18.8 us
    pallas_call x1, Pallas kernels, device_step(): z_own = narrow_own(name='two_own')(s, d, wc, n_own, t2)  18.8 us
    pallas_call x1, Pallas kernels, device_step(): pl.pallas_call(one_halo_kernel, out_shape=[sds((n_loc, f_hid // 2), BF16)...  17.8 us
    pallas_call x1, Pallas kernels, device_step(): pl.pallas_call(functools.partial(reduce_kernel, num_dev), out_shape=[sds(...  16.8 us
    pallas_call x1, Pallas kernels, device_step(): pl.pallas_call(functools.partial(table_grad_kernel, rows), out_shape=sds(...  15.6 us
  transfers between devices with their start and end apart: 12, of which 3 were waited for; matrix products, arithmetic and copies ran while one was open for 0% of the time, Pallas kernels for 50%

profile of v3, /device:TPU:0, one launch (start us, length us, event | category | flops | bytes accessed | tf_op | source)
XLA Modules:
  0.0 217.7 jit_solution(11858460078954195224)
XLA Ops:
  0.7 0.8 reshape.63
  3.6 4.2 %select_reduce_fusion = (s32[32,384]{1,0:T(8,128)S(1)}, f32[32,384]{1,0:T(8,128)S(1)}) fusion(f32[32,256]{1,0:T(8,128)S(1)} %reshape.63, s32[32,256]{1,0:T(8,128)S(1)} %get-tuple-element.89, s32[32,256]{1,0:T(8,128)S(1)} %get-tuple-element.90), kind=kLoop, calls=%fused_computation | loop fusion | flops 15704064 | bytes 196608 | tf_op jit(solution)/shard_map/reduce | solution.py:461
  7.9 0.8 fusion.8
  9.5 8.0 %lists.1 = (f32[8,128]{1,0:T(8,128)S(1)}, s32[104,128]{1,0:T(8,128)S(1)}, s32[104,128]{1,0:T(8,128)S(1)}, f32[96,128]{1,0:T(8,128)S(1)}, f32[96,128]{1,0:T(8,128)S(1)}) custom-call(s32[16,128]{1,0:T(8,128)S(1)} %bitcast.18, s32[104,128]{1,0:T(8,128)S(1)} %bitcast.13, f32[96,128]{1,0:T(8,128)S(1)} %reshape_reshape.3.wgt), custom_call_target="tpu_custom_call" | custom-call | tf_op jit(solution)/shard_map/lists/pallas_call | solution.py:481
  17.5 1.4 copy.16.x
  19.0 1.3 broadcast_multiply_fusion.3
  20.3 4.9 %halo_rows.1 = (bf16[1024,256]{1,0:T(8,128)(2,1)}, bf16[1024,256]{1,0:T(8,128)(2,1)}) custom-call(s32[2048]{0:T(1024)S(1)} %get-tuple-element.83.ids2, bf16[2048,200]{1,0:T(8,128)(2,1)S(1)} %copy.16.x), custom_call_target="tpu_custom_call" | custom-call | tf_op jit(solution)/shard_map/halo_rows/pallas_call | solution.py:493
  25.6 2.2 %collective-permute-start.1 = (bf16[1024,256]{1,0:T(8,128)(2,1)}, bf16[1024,256]{1,0:T(8,128)(2,1)}, u32[]{:S(2)}, u32[]{:S(2)}) collective-permute-start(bf16[1024,256]{1,0:T(8,128)(2,1)} %get-tuple-element.45), channel_id=1, source_target_pairs={{0,7},{1,0},{2,1},{3,2},{4,3},{5,4},{6,5},{7,6}} | collective-permute-start | bytes 1572872 | tf_op jit(solution)/shard_map/ppermute | solution.py:440
  28.0 21.1 %one_own.1.y_own = f32[8192,128]{1,0:T(8,128)S(1)} custom-call(s32[12288]{0:T(1024)S(1)} %get-tuple-element.41.s4.to, s32[12288]{0:T(1024)S(1)} %get-tuple-element.73.d4.frm, f32[12288]{0:T(1024)S(1)} %reshape.72.w, s32[32]{0:T(128)S(1)} %get-tuple-element.88.cnt, bf16[2048,200]{1,0:T(8,128)(2,1)S(1)} %copy.16.x, bf16[200,512]{1,0:T(8,128)(2,1)S(1)} %convert_element_type.30.w1), custom_call_target="tpu_custom_call" | custom-call | flops 199999995904 | bytes 8000000 | tf_op jit(solution)/shard_map/one_own/pallas_call | solution.py:509
  49.7 17.8 %one_halo.1 = (bf16[2048,256]{1,0:T(8,128)(2,1)}, bf16[2048,256]{1,0:T(8,128)(2,1)}, f32[2048,128]{1,0:T(8,128)S(1)}, bf16[1024,128]{1,0:T(8,128)(2,1)}, bf16[1024,128]{1,0:T(8,128)(2,1)}) custom-call(s32[12288]{0:T(1024)S(1)} %get-tuple-element.41.s4.to, s32[12288]{0:T(1024)S(1)} %get-tuple-element.73.d4.frm, f32[12288]{0:T(1024)S(1)} %reshape.72.w, ...), custom_call_target="tpu_custom_call" | custom-call | tf_op jit(solution)/shard_map/one_halo/pallas_call | solution.py:519
  67.5 1.6 collective-permute-start.7
  69.1 2.7 %collective-permute-start.3 = (bf16[1024,128]{1,0:T(8,128)(2,1)}, bf16[1024,128]{1,0:T(8,128)(2,1)}, u32[]{:S(2)}, u32[]{:S(2)}) collective-permute-start(bf16[1024,128]{1,0:T(8,128)(2,1)} %get-tuple-element.49), channel_id=1, source_target_pairs={{0,7},{1,0},{2,1},{3,2},{4,3},{5,4},{6,5},{7,6}} | collective-permute-start | bytes 786440 | tf_op jit(solution)/shard_map/ppermute | solution.py:440
  71.8 18.8 %two_own.1.z_own = f32[2048,128]{1,0:T(8,128)S(1)} custom-call(s32[12288]{0:T(1024)S(1)} %get-tuple-element.80.frm.s.to, s32[12288]{0:T(1024)S(1)} %get-tuple-element.74.to.d.frm, f32[12288]{0:T(1024)S(1)} %reshape.72.w, s32[32]{0:T(128)S(1)} %get-tuple-element.88.cnt, f32[2048,128]{1,0:T(8,128)S(1)} %get-tuple-element.47.table), custom_call_target="tpu_custom_call" | custom-call | flops 199999995904 | bytes 8000000 | tf_op jit(solution)/shard_map/two_own/pallas_call | solution.py:541
  90.5 9.8 %collective-permute-done.2.t_prev = bf16[1024,128]{1,0:T(8,128)(2,1)} collective-permute-done((bf16[1024,128]{1,0:T(8,128)(2,1)}, bf16[1024,128]{1,0:T(8,128)(2,1)}, u32[]{:S(2)}, u32[]{:S(2)}) %collective-permute-start.2) | collective-permute-done | bytes 262176 | tf_op jit(solution)/shard_map/ppermute | solution.py:437
  100.7 19.5 %logits.1 = (f32[2048,128]{1,0:T(8,128)S(1)}, f32[1024,128]{1,0:T(8,128)}, f32[1024,128]{1,0:T(8,128)}, f32[8,128]{1,0:T(8,128)S(1)}) custom-call(s32[12288]{0:T(1024)S(1)} %get-tuple-element.80.frm.s.to, s32[12288]{0:T(1024)S(1)} %get-tuple-element.74.to.d.frm, f32[12288]{0:T(1024)S(1)} %reshape.72.w, s32[32]{0:T(128)S(1)} %get-tuple-element.71.cnt, ...), custom_call_target="tpu_custom_call" | custom-call | tf_op jit(solution)/shard_map/logits/pallas_call | solution.py:543
  120.8 18.8 %two_back_own.1.own = f32[2048,128]{1,0:T(8,128)S(1)} custom-call(s32[12288]{0:T(1024)S(1)} %get-tuple-element.74.to.d.frm, s32[12288]{0:T(1024)S(1)} %get-tuple-element.80.frm.s.to, f32[12288]{0:T(1024)S(1)} %reshape.72.w, s32[32]{0:T(128)S(1)} %get-tuple-element.88.cnt, f32[2048,128]{1,0:T(8,128)S(1)} %get-tuple-element.52.table), custom_call_target="tpu_custom_call" | custom-call | flops 199999995904 | bytes 8000000 | tf_op jit(solution)/shard_map/two_back_own/pallas_call | solution.py:556
  139.6 3.9 %collective-permute-start.8 = (bf16[2048,256]{1,0:T(8,128)(2,1)}, bf16[2048,256]{1,0:T(8,128)(2,1)}, u32[]{:S(2)}, u32[]{:S(2)}) collective-permute-start(bf16[2048,256]{1,0:T(8,128)(2,1)} %get-tuple-element.59.hid_b), channel_id=1, source_target_pairs={{0,7},{1,0},{2,1},{3,2},{4,3},{5,4},{6,5},{7,6}} | collective-permute-start | bytes 3145736 | tf_op jit(solution)/shard_map/ppermute | solution.py:440
  143.6 9.1 %hidden_grad.1 = (bf16[2048,128]{1,0:T(8,128)(2,1)}, f32[8192,128]{1,0:T(8,128)S(1)}, f32[512,128]{1,0:T(8,128)S(1)}) custom-call(s32[2048]{0:T(1024)S(1)} %get-tuple-element.85.ids, f32[2048,128]{1,0:T(8,128)S(1)} %two_back_own.1.own, f32[1024,128]{1,0:T(8,128)} %collective-permute-done.4.ret_next, f32[1024,128]{1,0:T(8,128)} %collective-permute-done.5.ret_prev, ...), custom_call_target="tpu_custom_call" | custom-call | tf_op jit(solution)/shard_map/hidden_grad/pallas_call | solution.py:557
  152.6 2.6 %collective-permute-start.6 = (bf16[2048,128]{1,0:T(8,128)(2,1)}, bf16[2048,128]{1,0:T(8,128)(2,1)}, u32[]{:S(2)}, u32[]{:S(2)}) collective-permute-start(bf16[2048,128]{1,0:T(8,128)(2,1)} %get-tuple-element.58), channel_id=1, source_target_pairs={{0,7},{1,0},{2,1},{3,2},{4,3},{5,4},{6,5},{7,6}} | collective-permute-start | bytes 1572872 | tf_op jit(solution)/shard_map/ppermute | solution.py:440
  155.3 20.7 %one_back_own.1.own = f32[8192,128]{1,0:T(8,128)S(1)} custom-call(s32[12288]{0:T(1024)S(1)} %get-tuple-element.73.d4.frm, s32[12288]{0:T(1024)S(1)} %get-tuple-element.41.s4.to, f32[12288]{0:T(1024)S(1)} %reshape.72.w, s32[32]{0:T(128)S(1)} %get-tuple-element.88.cnt, f32[8192,128]{1,0:T(8,128)S(1)} %get-tuple-element.57.table), custom_call_target="tpu_custom_call" | custom-call | flops 199999995904 | bytes 8000000 | tf_op jit(solution)/shard_map/one_back_own/pallas_call | solution.py:567
  176.6 4.1 %collective-permute-done.9.tp = bf16[2048,128]{1,0:T(8,128)(2,1)} collective-permute-done((bf16[2048,128]{1,0:T(8,128)(2,1)}, bf16[2048,128]{1,0:T(8,128)(2,1)}, u32[]{:S(2)}, u32[]{:S(2)}) %collective-permute-start.9) | collective-permute-done | bytes 524320 | tf_op jit(solution)/shard_map/ppermute | solution.py:437
  180.7 15.6 %table_grad.1.g1 = f32[256,512]{1,0:T(8,128)S(1)} custom-call(s32[2048]{0:T(1024)S(1)} %get-tuple-element.35.ids4, s32[13312]{0:T(1024)S(1)} %bitcast.15, f32[12288]{0:T(1024)S(1)} %bitcast.17, s32[13312]{0:T(1024)S(1)} %bitcast.14, f32[12288]{0:T(1024)S(1)} %bitcast.16, f32[8192,128]{1,0:T(8,128)S(1)} %one_back_own.1.own, ...), custom_call_target="tpu_custom_call" | custom-call | tf_op jit(solution)/shard_map/table_grad/pallas_call | solution.py:577
  196.2 16.8 %reduce.18 = (f32[256,512]{1,0:T(8,128)S(1)}, f32[512,128]{1,0:T(8,128)S(1)}, f32[8,128]{1,0:T(8,128)S(1)}) custom-call(f32[256,512]{1,0:T(8,128)S(1)} %table_grad.1.g1, f32[512,128]{1,0:T(8,128)S(1)} %get-tuple-element.60.g2, f32[8,128]{1,0:T(8,128)S(1)} %get-tuple-element.61.loss), custom_call_target="tpu_custom_call" | custom-call | tf_op jit(solution)/shard_map/reduce/pallas_call | solution.py:586
  213.8 0.8 copy.19
  (54 shorter events, 6.9 us)
Async XLA Ops:
  0.6 27.3 %copy-start.4 = (f32[512,107]{0,1:T(8,128)S(1)}, f32[512,107]{0,1:T(8,128)}, u32[]{:S(2)}) copy-start(f32[512,107]{0,1:T(8,128)} %param.11) | copy-start | bytes 657412
  0.6 27.3 %copy-start.3 = (f32[200,512]{1,0:T(8,128)S(1)}, f32[200,512]{1,0:T(8,128)}, u32[]{:S(2)}) copy-start(f32[200,512]{1,0:T(8,128)} %param.10) | copy-start | bytes 1228804
  8.8 0.7 copy-start.2
  25.2 24.5 %collective-permute-start = (bf16[1024,256]{1,0:T(8,128)(2,1)}, bf16[1024,256]{1,0:T(8,128)(2,1)}, u32[]{:S(2)}, u32[]{:S(2)}) collective-permute-start(bf16[1024,256]{1,0:T(8,128)(2,1)} %get-tuple-element.44), channel_id=1, source_target_pairs={{0,1},{1,2},{2,3},{3,4},{4,5},{5,6},{6,7},{7,0}} | collective-permute-start | bytes 1572872 | tf_op jit(solution)/shard_map/ppermute | solution.py:437
  25.6 24.1 %collective-permute-start.1 = (bf16[1024,256]{1,0:T(8,128)(2,1)}, bf16[1024,256]{1,0:T(8,128)(2,1)}, u32[]{:S(2)}, u32[]{:S(2)}) collective-permute-start(bf16[1024,256]{1,0:T(8,128)(2,1)} %get-tuple-element.45), channel_id=1, source_target_pairs={{0,7},{1,0},{2,1},{3,2},{4,3},{5,4},{6,5},{7,6}} | collective-permute-start | bytes 1572872 | tf_op jit(solution)/shard_map/ppermute | solution.py:440
  27.9 115.6 %copy-start = (bf16[128,512]{1,0:T(8,128)(2,1)}, bf16[128,512]{1,0:T(8,128)(2,1)S(1)}, u32[]{:S(2)}) copy-start(bf16[128,512]{1,0:T(8,128)(2,1)S(1)} %pad.4.w2t) | copy-start | bytes 393220
  67.5 87.8 %collective-permute-start.7 = (bf16[2048,256]{1,0:T(8,128)(2,1)}, bf16[2048,256]{1,0:T(8,128)(2,1)}, u32[]{:S(2)}, u32[]{:S(2)}) collective-permute-start(bf16[2048,256]{1,0:T(8,128)(2,1)} %get-tuple-element.55.hid_a), channel_id=1, source_target_pairs={{0,7},{1,0},{2,1},{3,2},{4,3},{5,4},{6,5},{7,6}} | collective-permute-start | bytes 3145736 | tf_op jit(solution)/shard_map/ppermute | solution.py:440
  69.1 106.9 %collective-permute-start.10 = (bf16[2048,256]{1,0:T(8,128)(2,1)}, bf16[2048,256]{1,0:T(8,128)(2,1)}, u32[]{:S(2)}, u32[]{:S(2)}) collective-permute-start(bf16[2048,256]{1,0:T(8,128)(2,1)} %get-tuple-element.55.hid_a), channel_id=1, source_target_pairs={{0,1},{1,2},{2,3},{3,4},{4,5},{5,6},{6,7},{7,0}} | collective-permute-start | bytes 3145736 | tf_op jit(solution)/shard_map/ppermute | solution.py:437
  69.1 31.2 %collective-permute-start.2 = (bf16[1024,128]{1,0:T(8,128)(2,1)}, bf16[1024,128]{1,0:T(8,128)(2,1)}, u32[]{:S(2)}, u32[]{:S(2)}) collective-permute-start(bf16[1024,128]{1,0:T(8,128)(2,1)} %get-tuple-element.48), channel_id=1, source_target_pairs={{0,1},{1,2},{2,3},{3,4},{4,5},{5,6},{6,7},{7,0}} | collective-permute-start | bytes 786440 | tf_op jit(solution)/shard_map/ppermute | solution.py:437
  69.1 31.2 %collective-permute-start.3 = (bf16[1024,128]{1,0:T(8,128)(2,1)}, bf16[1024,128]{1,0:T(8,128)(2,1)}, u32[]{:S(2)}, u32[]{:S(2)}) collective-permute-start(bf16[1024,128]{1,0:T(8,128)(2,1)} %get-tuple-element.49), channel_id=1, source_target_pairs={{0,7},{1,0},{2,1},{3,2},{4,3},{5,4},{6,5},{7,6}} | collective-permute-start | bytes 786440 | tf_op jit(solution)/shard_map/ppermute | solution.py:440
  71.8 28.6 %copy-start.5 = (s32[2048]{0:T(1024)S(1)}, s32[2048]{0:T(1024)}, u32[]{:S(2)}) copy-start(s32[2048]{0:T(1024)} %get-tuple-element.50) | copy-start | bytes 24580
  120.2 23.4 %collective-permute-start.4 = (f32[1024,128]{1,0:T(8,128)}, f32[1024,128]{1,0:T(8,128)}, u32[]{:S(2)}, u32[]{:S(2)}) collective-permute-start(f32[1024,128]{1,0:T(8,128)} %get-tuple-element.53), channel_id=1, source_target_pairs={{0,7},{1,0},{2,1},{3,2},{4,3},{5,4},{6,5},{7,6}} | collective-permute-start | bytes 1572872 | tf_op jit(solution)/shard_map/ppermute | solution.py:440
  120.8 22.7 %collective-permute-start.5 = (f32[1024,128]{1,0:T(8,128)}, f32[1024,128]{1,0:T(8,128)}, u32[]{:S(2)}, u32[]{:S(2)}) collective-permute-start(f32[1024,128]{1,0:T(8,128)} %get-tuple-element.54), channel_id=1, source_target_pairs={{0,1},{1,2},{2,3},{3,4},{4,5},{5,6},{6,7},{7,0}} | collective-permute-start | bytes 1572872 | tf_op jit(solution)/shard_map/ppermute | solution.py:437
  139.6 37.0 %collective-permute-start.8 = (bf16[2048,256]{1,0:T(8,128)(2,1)}, bf16[2048,256]{1,0:T(8,128)(2,1)}, u32[]{:S(2)}, u32[]{:S(2)}) collective-permute-start(bf16[2048,256]{1,0:T(8,128)(2,1)} %get-tuple-element.59.hid_b), channel_id=1, source_target_pairs={{0,7},{1,0},{2,1},{3,2},{4,3},{5,4},{6,5},{7,6}} | collective-permute-start | bytes 3145736 | tf_op jit(solution)/shard_map/ppermute | solution.py:440
  143.6 37.1 %collective-permute-start.11 = (bf16[2048,256]{1,0:T(8,128)(2,1)}, bf16[2048,256]{1,0:T(8,128)(2,1)}, u32[]{:S(2)}, u32[]{:S(2)}) collective-permute-start(bf16[2048,256]{1,0:T(8,128)(2,1)} %get-tuple-element.59.hid_b), channel_id=1, source_target_pairs={{0,1},{1,2},{2,3},{3,4},{4,5},{5,6},{6,7},{7,0}} | collective-permute-start | bytes 3145736 | tf_op jit(solution)/shard_map/ppermute | solution.py:437
  152.6 23.9 %collective-permute-start.6 = (bf16[2048,128]{1,0:T(8,128)(2,1)}, bf16[2048,128]{1,0:T(8,128)(2,1)}, u32[]{:S(2)}, u32[]{:S(2)}) collective-permute-start(bf16[2048,128]{1,0:T(8,128)(2,1)} %get-tuple-element.58), channel_id=1, source_target_pairs={{0,7},{1,0},{2,1},{3,2},{4,3},{5,4},{6,5},{7,6}} | collective-permute-start | bytes 1572872 | tf_op jit(solution)/shard_map/ppermute | solution.py:440
  155.3 25.4 %collective-permute-start.9 = (bf16[2048,128]{1,0:T(8,128)(2,1)}, bf16[2048,128]{1,0:T(8,128)(2,1)}, u32[]{:S(2)}, u32[]{:S(2)}) collective-permute-start(bf16[2048,128]{1,0:T(8,128)(2,1)} %get-tuple-element.58), channel_id=1, source_target_pairs={{0,1},{1,2},{2,3},{3,4},{4,5},{5,6},{6,7},{7,0}} | collective-permute-start | bytes 1572872 | tf_op jit(solution)/shard_map/ppermute | solution.py:437
  155.3 25.4 %copy-start.1 = (bf16[128,512]{1,0:T(8,128)(2,1)S(1)}, bf16[128,512]{1,0:T(8,128)(2,1)}, u32[]{:S(2)}) copy-start(bf16[128,512]{1,0:T(8,128)(2,1)} %copy-done) | copy-start | bytes 393220

commit v4 on v3

--- a/solution.py
+++ b/solution.py
@@ -15,6 +15,7 @@
 F32 = jnp.float32
 BF16 = jnp.bfloat16
 LANES = 128
+BLOCK = 256
 CHUNK = 256
 SLOT = 384
 
@@ -22,6 +23,14 @@
 VMEM_SPEC = pl.BlockSpec(memory_space=pltpu.VMEM)
 
 
+def rows_at(i, base=0, size=BLOCK):
+    return pl.ds(base + i * size, size)
+
+
+def loop(count, body):
+    lax.fori_loop(0, count, lambda i, _: (body(i), 0)[1], 0)
+
+
 def params(mib, **kw):
     return pltpu.CompilerParams(vmem_limit_bytes=mib * 2**20, **kw)
 
@@ -29,54 +38,51 @@
 def zero_rows(refs):
     rows = refs[0].shape[0]
 
-    def body(i, _):
+    def body(i):
         for ref in refs:
             ref[pl.ds(i * 64, 64), :] = jnp.zeros((64, LANES), F32)
-        return 0
-
-    lax.fori_loop(0, rows // 64, body, 0)
+
+    loop(rows // 64, body)
 
 
 def sum_rows(out, refs):
     rows = refs[0].shape[0]
 
-    def body(i, _):
+    def body(i):
         total = refs[0][pl.ds(i * 64, 64), :]
         for ref in refs[1:]:
             total = total + ref[pl.ds(i * 64, 64), :]
         out[pl.ds(i * 64, 64), :] = total
-        return 0
-
-    lax.fori_loop(0, rows // 64, body, 0)
+
+    loop(rows // 64, body)
 
 
 def edge_pass(from_ref, to_ref, w_ref, cnt_ref, table, accs, width, unroll, back):
     n_acc = len(accs)
     shift = unroll.bit_length() - 1
 
-    def row(r, _):
+    def row(r):
         blocks = lax.shift_right_logical(cnt_ref[r] + (unroll - 1), shift)
 
-        def body(j, _):
+        def body(j):
             off = r * SLOT + (SLOT - unroll - j * unroll if back else j * unroll)
-            vals = [table[pl.ds(pl.multiple_of(from_ref[off + u], width), width), :] * w_ref[off + u] for u in range(unroll)]
-            for g in range(unroll // n_acc):
-                rows = [pl.multiple_of(to_ref[off + g * n_acc + k], width) for k in range(n_acc)]
+            frm, to, wgt = (ref.at[pl.ds(off, unroll)] for ref in (from_ref, to_ref, w_ref))
+            for g in range(0, unroll, n_acc):
+                vals = [table[pl.ds(pl.multiple_of(frm[g + k], width), width), :] * wgt[g + k] for k in range(n_acc)]
+                rows = [pl.multiple_of(to[g + k], width) for k in range(n_acc)]
                 old = [accs[k][pl.ds(rows[k], width), :] for k in range(n_acc)]
                 for k in range(n_acc):
-                    accs[k][pl.ds(rows[k], width), :] = old[k] + vals[g * n_acc + k]
-            return 0
-
-        lax.fori_loop(0, blocks, body, 0)
-        return 0
-
-    lax.fori_loop(0, cnt_ref.shape[0], row, 0)
+                    accs[k][pl.ds(rows[k], width), :] = old[k] + vals[k]
+
+        loop(blocks, body)
+
+    loop(cnt_ref.shape[0], row)
 
 
 def scatter_pass(ids_ref, table, accs, width, unroll):
     n_acc = len(accs)
 
-    def body(j, _):
+    def body(j):
         off = j * unroll
         for g in range(unroll // n_acc):
             rows = [pl.multiple_of(ids_ref[off + g * n_acc + k], width) for k in range(n_acc)]
@@ -84,19 +90,17 @@
             old = [accs[k][pl.ds(rows[k], width), :] for k in range(n_acc)]
             for k in range(n_acc):
                 accs[k][pl.ds(rows[k], width), :] = old[k] + vals[k]
-        return 0
-
-    lax.fori_loop(0, ids_ref.shape[0] // unroll, body, 0)
+
+    loop(ids_ref.shape[0] // unroll, body)
 
 
 def gather_pass(ids_ref, table, out, width, unroll=8):
-    def body(j, _):
+    def body(j):
         for u in range(unroll):
             i = j * unroll + u
             out[pl.ds(pl.multiple_of(i * width, width), width), :] = table[pl.ds(pl.multiple_of(ids_ref[i], width), width), :]
-        return 0
-
-    lax.fori_loop(0, ids_ref.shape[0] // unroll, body, 0)
+
+    loop(ids_ref.shape[0] // unroll, body)
 
 
 def spread(table, start, block):
@@ -146,33 +150,30 @@
 def halo_rows_kernel(ids2, x, to_next, to_prev, table, picked):
     rows = x.shape[0]
 
-    def put(i, _):
-        block = x[pl.ds(i * 256, 256), :].astype(F32)
-        pad = jnp.zeros((256, 2 * LANES - block.shape[1]), F32)
-        spread(table, i * 256, jnp.concatenate([block, pad], axis=1))
-        return 0
-
-    lax.fori_loop(0, rows // 256, put, 0)
+    def put(i):
+        block = x[rows_at(i), :].astype(F32)
+        pad = jnp.zeros((BLOCK, 2 * LANES - block.shape[1]), F32)
+        spread(table, i * BLOCK, jnp.concatenate([block, pad], axis=1))
+
+    loop(rows // BLOCK, put)
     gather_pass(ids2, table, picked, 2)
     half = to_next.shape[0]
 
-    def take(i, _):
-        to_next[pl.ds(i * 256, 256), :] = unspread(picked, i * 256, 256, 2).astype(BF16)
-        to_prev[pl.ds(i * 256, 256), :] = unspread(picked, half + i * 256, 256, 2).astype(BF16)
-        return 0
-
-    lax.fori_loop(0, half // 256, take, 0)
+    def take(i):
+        to_next[rows_at(i), :] = unspread(picked, i * BLOCK, BLOCK, 2).astype(BF16)
+        to_prev[rows_at(i), :] = unspread(picked, half + i * BLOCK, BLOCK, 2).astype(BF16)
+
+    loop(half // BLOCK, take)
 
 
 def one_own_kernel(s4, d4, w, cnt, x, w1, y, table, *accs):
     zero_rows(accs)
 
-    def put(i, _):
-        t = jnp.dot(x[pl.ds(i * 256, 256), :], w1[...], preferred_element_type=F32)
-        spread(table, i * 256, t.astype(BF16).astype(F32))
-        return 0
-
-    lax.fori_loop(0, x.shape[0] // 256, put, 0)
+    def put(i):
+        t = jnp.dot(x[rows_at(i), :], w1[...], preferred_element_type=F32)
+        spread(table, i * BLOCK, t.astype(BF16).astype(F32))
+
+    loop(x.shape[0] // BLOCK, put)
     edge_pass(s4, d4, w, cnt, table, accs, 4, 16, False)
     sum_rows(y, accs)
 
@@ -181,35 +182,32 @@
     zero_rows(accs)
     half = x_prev.shape[0]
 
-    def put(i, _):
-        t = jnp.dot(x_prev[pl.ds(i * 256, 256), :w1.shape[0]], w1[...], preferred_element_type=F32)
-        spread(table, i * 256, t.astype(BF16).astype(F32))
-        t = jnp.dot(x_next[pl.ds(i * 256, 256), :w1.shape[0]], w1[...], preferred_element_type=F32)
-        spread(table, half + i * 256, t.astype(BF16).astype(F32))
-        return 0
-
-    lax.fori_loop(0, half // 256, put, 0)
+    def put(i):
+        t = jnp.dot(x_prev[rows_at(i), :w1.shape[0]], w1[...], preferred_element_type=F32)
+        spread(table, i * BLOCK, t.astype(BF16).astype(F32))
+        t = jnp.dot(x_next[rows_at(i), :w1.shape[0]], w1[...], preferred_element_type=F32)
+        spread(table, half + i * BLOCK, t.astype(BF16).astype(F32))
+
+    loop(half // BLOCK, put)
     edge_pass(s4, d4, w, cnt, table, accs, 4, 16, True)
     sum_rows(accs[0], (y_own,) + accs)
 
-    def act(i, _):
-        h = jnp.maximum(unspread(accs[0], i * 256, 256, 4), 0.0).astype(BF16)
+    def act(i):
+        h = jnp.maximum(unspread(accs[0], i * BLOCK, BLOCK, 4), 0.0).astype(BF16)
         cut = hid_a.shape[1]
-        hid_a[pl.ds(i * 256, 256), :] = h[:, :cut]
-        hid_b[pl.ds(i * 256, 256), :] = h[:, cut:]
+        hid_a[rows_at(i), :] = h[:, :cut]
+        hid_b[rows_at(i), :] = h[:, cut:]
         t = lax.dot_general(h, w2t[...], CONTRACT_COLS, preferred_element_type=F32)
-        t2[pl.ds(i * 256, 256), :] = t.astype(BF16).astype(F32)
-        return 0
-
-    lax.fori_loop(0, t2.shape[0] // 256, act, 0)
+        t2[rows_at(i), :] = t.astype(BF16).astype(F32)
+
+    loop(t2.shape[0] // BLOCK, act)
     gather_pass(ids, t2, picked, 1)
 
-    def take(i, _):
-        to_next[pl.ds(i * 256, 256), :] = picked[pl.ds(i * 256, 256), :].astype(BF16)
-        to_prev[pl.ds(i * 256, 256), :] = picked[pl.ds(half + i * 256, 256), :].astype(BF16)
-        return 0
-
-    lax.fori_loop(0, half // 256, take, 0)
+    def take(i):
+        to_next[rows_at(i), :] = picked[rows_at(i), :].astype(BF16)
+        to_prev[rows_at(i), :] = picked[rows_at(i, half), :].astype(BF16)
+
+    loop(half // BLOCK, take)
 
 
 def narrow_own_kernel(frm, to, w, cnt, table, out, *accs):
@@ -228,17 +226,16 @@
     zero_rows(accs)
     half = t_prev.shape[0]
 
-    def put(i, _):
-        table[pl.ds(i * 256, 256), :] = t_prev[pl.ds(i * 256, 256), :].astype(F32)
-        table[pl.ds(half + i * 256, 256), :] = t_next[pl.ds(i * 256, 256), :].astype(F32)
-        return 0
-
-    lax.fori_loop(0, half // 256, put, 0)
+    def put(i):
+        table[rows_at(i), :] = t_prev[rows_at(i), :].astype(F32)
+        table[rows_at(i, half), :] = t_next[rows_at(i), :].astype(F32)
+
+    loop(half // BLOCK, put)
     edge_pass(s, d, w, cnt, table, accs, 1, 16, True)
     denom = count[0:1, :]
     loss[...] = jnp.zeros_like(loss)
 
-    def soft(i, _):
+    def soft(i):
         at = pl.ds(i * 64, 64)
         z = z_own[at, :]
         for acc in accs:
@@ -259,13 +256,12 @@
         loss[...] += part
         mask_f = jnp.where(keep, 1.0, 0.0)
         dz[at, :] = jnp.where(lane < classes, (jnp.exp(zm - log_norm) - hot_f) * (mask_f / denom), 0.0)
-        return 0
-
-    lax.fori_loop(0, dz.shape[0] // 64, soft, 0)
+
+    loop(dz.shape[0] // 64, soft)
     zero_rows(accs)
     edge_pass(d, s, w, cnt, dz, accs, 1, 16, True)
 
-    def fin(i, _):
+    def fin(i):
         at = pl.ds(i * 64, 64)
         bt = pl.ds(half + i * 64, 64)
         a, b = accs[0][at, :], accs[0][bt, :]
@@ -273,9 +269,8 @@
             a, b = a + acc[at, :], b + acc[bt, :]
         back_prev[at, :] = a
         back_next[at, :] = b
-        return 0
-
-    lax.fori_loop(0, half // 64, fin, 0)
+
+    loop(half // 64, fin)
 
 
 def masked(grad, hid_a, hid_b):
@@ -292,8 +287,8 @@
     scatter_pass(ids.at[pl.ds(half, half)], ret_prev, accs, 1, 8)
     g2[...] = jnp.zeros_like(g2)
 
-    def fold(i, _):
-        at = pl.ds(i * 256, 256)
+    def fold(i):
+        at = rows_at(i)
         total = own[at, :]
         for acc in accs:
             total = total + acc[at, :]
@@ -303,10 +298,9 @@
         g2[:cut, :] += lax.dot_general(hid_a[at, :], dt, CONTRACT_ROWS, preferred_element_type=F32)
         g2[cut:, :] += lax.dot_general(hid_b[at, :], dt, CONTRACT_ROWS, preferred_element_type=F32)
         dh = jnp.dot(dt, w2t[...], preferred_element_type=F32)
-        spread(dy, i * 256, masked(dh, hid_a[at, :], hid_b[at, :]))
-        return 0
-
-    lax.fori_loop(0, n_loc // 256, fold, 0)
+        spread(dy, i * BLOCK, masked(dh, hid_a[at, :], hid_b[at, :]))
+
+    loop(n_loc // BLOCK, fold)
 
 
 def peer_pass(ids4, code_ref, w_ref, rows, far, table, accs):
@@ -315,11 +309,11 @@
     n_loc = ids4.shape[0]
     shift = n_loc.bit_length() - 1
 
-    def row(r, _):
+    def row(r):
         first = SLOT - 16 - (code_ref[tally + 2 * rows + r] if far else 0)
         edges = code_ref[tally + far * rows + r]
 
-        def body(j, _):
+        def body(j):
             off = r * SLOT + first - j * 16
             codes, wgt = (ref.at[pl.ds(off, 16)] for ref in (code_ref, w_ref))
             for u in range(16):
@@ -329,12 +323,10 @@
                 val = table[pl.ds(pl.multiple_of(frm, 4), 4), :] * wgt[u]
                 at = pl.ds(pl.multiple_of(ids4[code & (n_loc - 1)], 4), 4)
                 acc[at, :] = acc[at, :] + val
-            return 0
-
-        lax.fori_loop(0, lax.shift_right_logical(edges + 15, 4), body, 0)
-        return 0
-
-    lax.fori_loop(0, rows, row, 0)
+
+        loop(lax.shift_right_logical(edges + 15, 4), body)
+
+    loop(rows, row)
 
 
 def table_grad_kernel(rows, ids4, cn, wn, cp, wp, own, tn, han, hbn, tp, hap, hbp, w2t, x, g1, table, *accs):
@@ -342,27 +334,25 @@
     g1[...] = jnp.zeros_like(g1)
 
     def fill(dt, hid_a, hid_b):
-        def put(i, _):
-            at = pl.ds(i * 256, 256)
+        def put(i):
+            at = rows_at(i)
             dh = jnp.dot(dt[at, :], w2t[...], preferred_element_type=F32)
-            spread(table, i * 256, masked(dh, hid_a[at, :], hid_b[at, :]))
-            return 0
-
-        lax.fori_loop(0, dt.shape[0] // 256, put, 0)
+            spread(table, i * BLOCK, masked(dh, hid_a[at, :], hid_b[at, :]))
+
+        loop(dt.shape[0] // BLOCK, put)
 
     fill(tn, han, hbn)
     peer_pass(ids4, cn, wn, rows, 0, table, accs)
     fill(tp, hap, hbp)
     peer_pass(ids4, cp, wp, rows, 1, table, accs)
 
-    def fold(i, _):
-        total = unspread(own, i * 256, 256, 4)
+    def fold(i):
+        total = unspread(own, i * BLOCK, BLOCK, 4)
         for acc in accs:
-            total = total + unspread(acc, i * 256, 256, 4)
-        g1[:x.shape[1], :] += lax.dot_general(x[pl.ds(i * 256, 256), :], total.astype(BF16), CONTRACT_ROWS, preferred_element_type=F32)
-        return 0
-
-    lax.fori_loop(0, x.shape[0] // 256, fold, 0)
+            total = total + unspread(acc, i * BLOCK, BLOCK, 4)
+        g1[:x.shape[1], :] += lax.dot_general(x[rows_at(i), :], total.astype(BF16), CONTRACT_ROWS, preferred_element_type=F32)
+
+    loop(x.shape[0] // BLOCK, fold)
 
 
 def reduce_kernel(num_dev, g1, g2, loss, o1, o2, lo, r1, r2, s1, s2, q1, q2, lslots, sem_s, sem_r, lsem_s, lsem_r):

time: 218 us -> 207 us (0.950)
  Pallas kernels: 171 us -> 153 us
  waiting for transfers between devices: 14.4 us -> 21.8 us
    ppermute x6, waiting for transfers between devices: 0.55 us -> 4.86 us  [shift_prev(): return lax.ppermute(a, GRAPH_AXIS, to_prev)]
    pallas_call x1, Pallas kernels: 20.7 us -> 16.7 us  [device_step(): pl.pallas_call(wide_own_kernel, out_shape=sds((quad, LANES), F32), in_spe...]
    pallas_call x1, Pallas kernels: 18.8 us -> 14.8 us  [device_step(): dt2_own = narrow_own(name='two_back_own')(d, s, wc, n_own, dz)]
    pallas_call x1, Pallas kernels: 18.8 us -> 14.7 us  [device_step(): z_own = narrow_own(name='two_own')(s, d, wc, n_own, t2)]
    ppermute x6, waiting for transfers between devices: 13.9 us -> 17 us  [shift_next(): return lax.ppermute(a, GRAPH_AXIS, to_next)]
    pallas_call x1, Pallas kernels: 21.1 us -> 18.2 us  [device_step(): pl.pallas_call(one_own_kernel, out_shape=sds((quad, LANES), F32), in_spec...]
  transfers between devices with their start and end apart: 12 -> 12, of which waited for: 3 -> 3; matrix products, arithmetic and copies ran while one was open for 0% -> 0% of each run, Pallas kernels for 50% -> 44%
where the time goes in v4:
time: 207 us; the launch traced here: 206 us
  Pallas kernels  153 us (74%)
  waiting for transfers between devices  21.8 us (11%)
  starting transfers between devices  13.3 us (6%)
  other arithmetic  7.31 us (4%)
  local copies, waits for them, and re-layouts  7.21 us (3%)
  between operations  3.35 us (2%)
    pallas_call x1, Pallas kernels, device_step(): pl.pallas_call(one_own_kernel, out_shape=sds((quad, LANES), F32), in_spec...  18.2 us
    pallas_call x1, Pallas kernels, device_step(): pl.pallas_call(functools.partial(logits_kernel, classes), out_shape=[sds(...  17.6 us
    ppermute x6, waiting for transfers between devices, shift_next(): return lax.ppermute(a, GRAPH_AXIS, to_next)  17 us
    pallas_call x1, Pallas kernels, device_step(): pl.pallas_call(functools.partial(reduce_kernel, num_dev), out_shape=[sds(...  16.8 us
    pallas_call x1, Pallas kernels, device_step(): pl.pallas_call(one_halo_kernel, out_shape=[sds((n_loc, f_hid // 2), BF16)...  16.7 us
    pallas_call x1, Pallas kernels, device_step(): pl.pallas_call(wide_own_kernel, out_shape=sds((quad, LANES), F32), in_spe...  16.7 us
    pallas_call x1, Pallas kernels, device_step(): pl.pallas_call(functools.partial(table_grad_kernel, rows), out_shape=sds(...  15.6 us
    pallas_call x1, Pallas kernels, device_step(): dt2_own = narrow_own(name='two_back_own')(d, s, wc, n_own, dz)  14.8 us
  transfers between devices with their start and end apart: 12, of which 3 were waited for; matrix products, arithmetic and copies ran while one was open for 0% of the time, Pallas kernels for 44%

profile of v4, /device:TPU:0, one launch (start us, length us, event | category | flops | bytes accessed | tf_op | source)
XLA Modules:
  0.0 206.2 jit_solution(11902297188094184299)
XLA Ops:
  0.7 0.8 reshape.63
  3.6 4.2 %select_reduce_fusion = (s32[32,384]{1,0:T(8,128)S(1)}, f32[32,384]{1,0:T(8,128)S(1)}) fusion(f32[32,256]{1,0:T(8,128)S(1)} %reshape.63, s32[32,256]{1,0:T(8,128)S(1)} %get-tuple-element.89, s32[32,256]{1,0:T(8,128)S(1)} %get-tuple-element.90), kind=kLoop, calls=%fused_computation | loop fusion | flops 15704064 | bytes 196608 | tf_op jit(solution)/shard_map/reduce | solution.py:451
  9.5 8.0 %lists.1 = (f32[8,128]{1,0:T(8,128)S(1)}, s32[104,128]{1,0:T(8,128)S(1)}, s32[104,128]{1,0:T(8,128)S(1)}, f32[96,128]{1,0:T(8,128)S(1)}, f32[96,128]{1,0:T(8,128)S(1)}) custom-call(s32[16,128]{1,0:T(8,128)S(1)} %bitcast.18, s32[104,128]{1,0:T(8,128)S(1)} %bitcast.13, f32[96,128]{1,0:T(8,128)S(1)} %reshape_reshape.3.wgt), custom_call_target="tpu_custom_call" | custom-call | tf_op jit(solution)/shard_map/lists/pallas_call | solution.py:471
  17.5 1.4 copy.16.x
  19.0 1.3 broadcast_multiply_fusion.3
  20.3 4.9 %halo_rows.1 = (bf16[1024,256]{1,0:T(8,128)(2,1)}, bf16[1024,256]{1,0:T(8,128)(2,1)}) custom-call(s32[2048]{0:T(1024)S(1)} %get-tuple-element.83.ids2, bf16[2048,200]{1,0:T(8,128)(2,1)S(1)} %copy.16.x), custom_call_target="tpu_custom_call" | custom-call | tf_op jit(solution)/shard_map/halo_rows/pallas_call | solution.py:483
  25.6 2.2 %collective-permute-start.1 = (bf16[1024,256]{1,0:T(8,128)(2,1)}, bf16[1024,256]{1,0:T(8,128)(2,1)}, u32[]{:S(2)}, u32[]{:S(2)}) collective-permute-start(bf16[1024,256]{1,0:T(8,128)(2,1)} %get-tuple-element.45), channel_id=1, source_target_pairs={{0,7},{1,0},{2,1},{3,2},{4,3},{5,4},{6,5},{7,6}} | collective-permute-start | bytes 1572872 | tf_op jit(solution)/shard_map/ppermute | solution.py:430
  28.0 18.2 %one_own.1.y_own = f32[8192,128]{1,0:T(8,128)S(1)} custom-call(s32[12288]{0:T(1024)S(1)} %get-tuple-element.41.s4.to, s32[12288]{0:T(1024)S(1)} %get-tuple-element.73.d4.frm, f32[12288]{0:T(1024)S(1)} %reshape.72.w, s32[32]{0:T(128)S(1)} %get-tuple-element.88.cnt, bf16[2048,200]{1,0:T(8,128)(2,1)S(1)} %copy.16.x, bf16[200,512]{1,0:T(8,128)(2,1)S(1)} %convert_element_type.30.w1), custom_call_target="tpu_custom_call" | custom-call | flops 199999995904 | bytes 8000000 | tf_op jit(solution)/shard_map/one_own/pallas_call | solution.py:499
  46.7 16.7 %one_halo.1 = (bf16[2048,256]{1,0:T(8,128)(2,1)}, bf16[2048,256]{1,0:T(8,128)(2,1)}, f32[2048,128]{1,0:T(8,128)S(1)}, bf16[1024,128]{1,0:T(8,128)(2,1)}, bf16[1024,128]{1,0:T(8,128)(2,1)}) custom-call(s32[12288]{0:T(1024)S(1)} %get-tuple-element.41.s4.to, s32[12288]{0:T(1024)S(1)} %get-tuple-element.73.d4.frm, f32[12288]{0:T(1024)S(1)} %reshape.72.w, ...), custom_call_target="tpu_custom_call" | custom-call | tf_op jit(solution)/shard_map/one_halo/pallas_call | solution.py:509
  63.5 1.3 collective-permute-start.7
  64.8 2.7 %collective-permute-start.3 = (bf16[1024,128]{1,0:T(8,128)(2,1)}, bf16[1024,128]{1,0:T(8,128)(2,1)}, u32[]{:S(2)}, u32[]{:S(2)}) collective-permute-start(bf16[1024,128]{1,0:T(8,128)(2,1)} %get-tuple-element.49), channel_id=1, source_target_pairs={{0,7},{1,0},{2,1},{3,2},{4,3},{5,4},{6,5},{7,6}} | collective-permute-start | bytes 786440 | tf_op jit(solution)/shard_map/ppermute | solution.py:430
  67.4 14.7 %two_own.1.z_own = f32[2048,128]{1,0:T(8,128)S(1)} custom-call(s32[12288]{0:T(1024)S(1)} %get-tuple-element.80.frm.s.to, s32[12288]{0:T(1024)S(1)} %get-tuple-element.74.to.d.frm, f32[12288]{0:T(1024)S(1)} %reshape.72.w, s32[32]{0:T(128)S(1)} %get-tuple-element.88.cnt, f32[2048,128]{1,0:T(8,128)S(1)} %get-tuple-element.47.table), custom_call_target="tpu_custom_call" | custom-call | flops 199999995904 | bytes 8000000 | tf_op jit(solution)/shard_map/two_own/pallas_call | solution.py:531
  82.2 13.6 %collective-permute-done.2.t_prev = bf16[1024,128]{1,0:T(8,128)(2,1)} collective-permute-done((bf16[1024,128]{1,0:T(8,128)(2,1)}, bf16[1024,128]{1,0:T(8,128)(2,1)}, u32[]{:S(2)}, u32[]{:S(2)}) %collective-permute-start.2) | collective-permute-done | bytes 262176 | tf_op jit(solution)/shard_map/ppermute | solution.py:427
  96.1 17.6 %logits.1 = (f32[2048,128]{1,0:T(8,128)S(1)}, f32[1024,128]{1,0:T(8,128)}, f32[1024,128]{1,0:T(8,128)}, f32[8,128]{1,0:T(8,128)S(1)}) custom-call(s32[12288]{0:T(1024)S(1)} %get-tuple-element.80.frm.s.to, s32[12288]{0:T(1024)S(1)} %get-tuple-element.74.to.d.frm, f32[12288]{0:T(1024)S(1)} %reshape.72.w, s32[32]{0:T(128)S(1)} %get-tuple-element.71.cnt, ...), custom_call_target="tpu_custom_call" | custom-call | tf_op jit(solution)/shard_map/logits/pallas_call | solution.py:533
  113.7 0.8 collective-permute-start.4
  114.5 14.8 %two_back_own.1.own = f32[2048,128]{1,0:T(8,128)S(1)} custom-call(s32[12288]{0:T(1024)S(1)} %get-tuple-element.74.to.d.frm, s32[12288]{0:T(1024)S(1)} %get-tuple-element.80.frm.s.to, f32[12288]{0:T(1024)S(1)} %reshape.72.w, s32[32]{0:T(128)S(1)} %get-tuple-element.88.cnt, f32[2048,128]{1,0:T(8,128)S(1)} %get-tuple-element.52.table), custom_call_target="tpu_custom_call" | custom-call | flops 199999995904 | bytes 8000000 | tf_op jit(solution)/shard_map/two_back_own/pallas_call | solution.py:546
  129.3 3.2 %collective-permute-start.8 = (bf16[2048,256]{1,0:T(8,128)(2,1)}, bf16[2048,256]{1,0:T(8,128)(2,1)}, u32[]{:S(2)}, u32[]{:S(2)}) collective-permute-start(bf16[2048,256]{1,0:T(8,128)(2,1)} %get-tuple-element.59.hid_b), channel_id=1, source_target_pairs={{0,7},{1,0},{2,1},{3,2},{4,3},{5,4},{6,5},{7,6}} | collective-permute-start | bytes 3145736 | tf_op jit(solution)/shard_map/ppermute | solution.py:430
  132.5 9.1 %hidden_grad.1 = (bf16[2048,128]{1,0:T(8,128)(2,1)}, f32[8192,128]{1,0:T(8,128)S(1)}, f32[512,128]{1,0:T(8,128)S(1)}) custom-call(s32[2048]{0:T(1024)S(1)} %get-tuple-element.85.ids, f32[2048,128]{1,0:T(8,128)S(1)} %two_back_own.1.own, f32[1024,128]{1,0:T(8,128)} %collective-permute-done.4.ret_next, f32[1024,128]{1,0:T(8,128)} %collective-permute-done.5.ret_prev, ...), custom_call_target="tpu_custom_call" | custom-call | tf_op jit(solution)/shard_map/hidden_grad/pallas_call | solution.py:547
  141.6 2.6 %collective-permute-start.6 = (bf16[2048,128]{1,0:T(8,128)(2,1)}, bf16[2048,128]{1,0:T(8,128)(2,1)}, u32[]{:S(2)}, u32[]{:S(2)}) collective-permute-start(bf16[2048,128]{1,0:T(8,128)(2,1)} %get-tuple-element.58), channel_id=1, source_target_pairs={{0,7},{1,0},{2,1},{3,2},{4,3},{5,4},{6,5},{7,6}} | collective-permute-start | bytes 1572872 | tf_op jit(solution)/shard_map/ppermute | solution.py:430
  144.2 16.7 %one_back_own.1.own = f32[8192,128]{1,0:T(8,128)S(1)} custom-call(s32[12288]{0:T(1024)S(1)} %get-tuple-element.73.d4.frm, s32[12288]{0:T(1024)S(1)} %get-tuple-element.41.s4.to, f32[12288]{0:T(1024)S(1)} %reshape.72.w, s32[32]{0:T(128)S(1)} %get-tuple-element.88.cnt, f32[8192,128]{1,0:T(8,128)S(1)} %get-tuple-element.57.table), custom_call_target="tpu_custom_call" | custom-call | flops 199999995904 | bytes 8000000 | tf_op jit(solution)/shard_map/one_back_own/pallas_call | solution.py:557
  161.0 4.8 %collective-permute-done.6.tn = bf16[2048,128]{1,0:T(8,128)(2,1)} collective-permute-done((bf16[2048,128]{1,0:T(8,128)(2,1)}, bf16[2048,128]{1,0:T(8,128)(2,1)}, u32[]{:S(2)}, u32[]{:S(2)}) %collective-permute-start.6) | collective-permute-done | bytes 524320 | tf_op jit(solution)/shard_map/ppermute | solution.py:430
  165.8 3.4 %collective-permute-done.9.tp = bf16[2048,128]{1,0:T(8,128)(2,1)} collective-permute-done((bf16[2048,128]{1,0:T(8,128)(2,1)}, bf16[2048,128]{1,0:T(8,128)(2,1)}, u32[]{:S(2)}, u32[]{:S(2)}) %collective-permute-start.9) | collective-permute-done | bytes 524320 | tf_op jit(solution)/shard_map/ppermute | solution.py:427
  169.2 15.6 %table_grad.1.g1 = f32[256,512]{1,0:T(8,128)S(1)} custom-call(s32[2048]{0:T(1024)S(1)} %get-tuple-element.35.ids4, s32[13312]{0:T(1024)S(1)} %bitcast.15, f32[12288]{0:T(1024)S(1)} %bitcast.17, s32[13312]{0:T(1024)S(1)} %bitcast.14, f32[12288]{0:T(1024)S(1)} %bitcast.16, f32[8192,128]{1,0:T(8,128)S(1)} %one_back_own.1.own, ...), custom_call_target="tpu_custom_call" | custom-call | tf_op jit(solution)/shard_map/table_grad/pallas_call | solution.py:567
  184.8 16.8 %reduce.18 = (f32[256,512]{1,0:T(8,128)S(1)}, f32[512,128]{1,0:T(8,128)S(1)}, f32[8,128]{1,0:T(8,128)S(1)}) custom-call(f32[256,512]{1,0:T(8,128)S(1)} %table_grad.1.g1, f32[512,128]{1,0:T(8,128)S(1)} %get-tuple-element.60.g2, f32[8,128]{1,0:T(8,128)S(1)} %get-tuple-element.61.loss), custom_call_target="tpu_custom_call" | custom-call | tf_op jit(solution)/shard_map/reduce/pallas_call | solution.py:576
  (54 shorter events, 7.3 us)
Async XLA Ops:
  0.6 27.3 %copy-start.4 = (f32[512,107]{0,1:T(8,128)S(1)}, f32[512,107]{0,1:T(8,128)}, u32[]{:S(2)}) copy-start(f32[512,107]{0,1:T(8,128)} %param.11) | copy-start | bytes 657412
  0.6 27.3 %copy-start.3 = (f32[200,512]{1,0:T(8,128)S(1)}, f32[200,512]{1,0:T(8,128)}, u32[]{:S(2)}) copy-start(f32[200,512]{1,0:T(8,128)} %param.10) | copy-start | bytes 1228804
  8.8 0.7 copy-start.2
  25.2 21.5 %collective-permute-start = (bf16[1024,256]{1,0:T(8,128)(2,1)}, bf16[1024,256]{1,0:T(8,128)(2,1)}, u32[]{:S(2)}, u32[]{:S(2)}) collective-permute-start(bf16[1024,256]{1,0:T(8,128)(2,1)} %get-tuple-element.44), channel_id=1, source_target_pairs={{0,1},{1,2},{2,3},{3,4},{4,5},{5,6},{6,7},{7,0}} | collective-permute-start | bytes 1572872 | tf_op jit(solution)/shard_map/ppermute | solution.py:427
  25.6 21.1 %collective-permute-start.1 = (bf16[1024,256]{1,0:T(8,128)(2,1)}, bf16[1024,256]{1,0:T(8,128)(2,1)}, u32[]{:S(2)}, u32[]{:S(2)}) collective-permute-start(bf16[1024,256]{1,0:T(8,128)(2,1)} %get-tuple-element.45), channel_id=1, source_target_pairs={{0,7},{1,0},{2,1},{3,2},{4,3},{5,4},{6,5},{7,6}} | collective-permute-start | bytes 1572872 | tf_op jit(solution)/shard_map/ppermute | solution.py:430
  27.9 104.6 %copy-start = (bf16[128,512]{1,0:T(8,128)(2,1)}, bf16[128,512]{1,0:T(8,128)(2,1)S(1)}, u32[]{:S(2)}) copy-start(bf16[128,512]{1,0:T(8,128)(2,1)S(1)} %pad.4.w2t) | copy-start | bytes 393220
  63.5 80.8 %collective-permute-start.7 = (bf16[2048,256]{1,0:T(8,128)(2,1)}, bf16[2048,256]{1,0:T(8,128)(2,1)}, u32[]{:S(2)}, u32[]{:S(2)}) collective-permute-start(bf16[2048,256]{1,0:T(8,128)(2,1)} %get-tuple-element.55.hid_a), channel_id=1, source_target_pairs={{0,7},{1,0},{2,1},{3,2},{4,3},{5,4},{6,5},{7,6}} | collective-permute-start | bytes 3145736 | tf_op jit(solution)/shard_map/ppermute | solution.py:430
  64.8 96.2 %collective-permute-start.10 = (bf16[2048,256]{1,0:T(8,128)(2,1)}, bf16[2048,256]{1,0:T(8,128)(2,1)}, u32[]{:S(2)}, u32[]{:S(2)}) collective-permute-start(bf16[2048,256]{1,0:T(8,128)(2,1)} %get-tuple-element.55.hid_a), channel_id=1, source_target_pairs={{0,1},{1,2},{2,3},{3,4},{4,5},{5,6},{6,7},{7,0}} | collective-permute-start | bytes 3145736 | tf_op jit(solution)/shard_map/ppermute | solution.py:427
  64.8 31.0 %collective-permute-start.2 = (bf16[1024,128]{1,0:T(8,128)(2,1)}, bf16[1024,128]{1,0:T(8,128)(2,1)}, u32[]{:S(2)}, u32[]{:S(2)}) collective-permute-start(bf16[1024,128]{1,0:T(8,128)(2,1)} %get-tuple-element.48), channel_id=1, source_target_pairs={{0,1},{1,2},{2,3},{3,4},{4,5},{5,6},{6,7},{7,0}} | collective-permute-start | bytes 786440 | tf_op jit(solution)/shard_map/ppermute | solution.py:427
  64.8 31.0 %collective-permute-start.3 = (bf16[1024,128]{1,0:T(8,128)(2,1)}, bf16[1024,128]{1,0:T(8,128)(2,1)}, u32[]{:S(2)}, u32[]{:S(2)}) collective-permute-start(bf16[1024,128]{1,0:T(8,128)(2,1)} %get-tuple-element.49), channel_id=1, source_target_pairs={{0,7},{1,0},{2,1},{3,2},{4,3},{5,4},{6,5},{7,6}} | collective-permute-start | bytes 786440 | tf_op jit(solution)/shard_map/ppermute | solution.py:430
  67.4 28.3 %copy-start.5 = (s32[2048]{0:T(1024)S(1)}, s32[2048]{0:T(1024)}, u32[]{:S(2)}) copy-start(s32[2048]{0:T(1024)} %get-tuple-element.50) | copy-start | bytes 24580
  113.7 18.8 %collective-permute-start.4 = (f32[1024,128]{1,0:T(8,128)}, f32[1024,128]{1,0:T(8,128)}, u32[]{:S(2)}, u32[]{:S(2)}) collective-permute-start(f32[1024,128]{1,0:T(8,128)} %get-tuple-element.53), channel_id=1, source_target_pairs={{0,7},{1,0},{2,1},{3,2},{4,3},{5,4},{6,5},{7,6}} | collective-permute-start | bytes 1572872 | tf_op jit(solution)/shard_map/ppermute | solution.py:430
  114.5 18.0 %collective-permute-start.5 = (f32[1024,128]{1,0:T(8,128)}, f32[1024,128]{1,0:T(8,128)}, u32[]{:S(2)}, u32[]{:S(2)}) collective-permute-start(f32[1024,128]{1,0:T(8,128)} %get-tuple-element.54), channel_id=1, source_target_pairs={{0,1},{1,2},{2,3},{3,4},{4,5},{5,6},{6,7},{7,0}} | collective-permute-start | bytes 1572872 | tf_op jit(solution)/shard_map/ppermute | solution.py:427
  129.3 36.5 %collective-permute-start.8 = (bf16[2048,256]{1,0:T(8,128)(2,1)}, bf16[2048,256]{1,0:T(8,128)(2,1)}, u32[]{:S(2)}, u32[]{:S(2)}) collective-permute-start(bf16[2048,256]{1,0:T(8,128)(2,1)} %get-tuple-element.59.hid_b), channel_id=1, source_target_pairs={{0,7},{1,0},{2,1},{3,2},{4,3},{5,4},{6,5},{7,6}} | collective-permute-start | bytes 3145736 | tf_op jit(solution)/shard_map/ppermute | solution.py:430
  132.5 36.7 %collective-permute-start.11 = (bf16[2048,256]{1,0:T(8,128)(2,1)}, bf16[2048,256]{1,0:T(8,128)(2,1)}, u32[]{:S(2)}, u32[]{:S(2)}) collective-permute-start(bf16[2048,256]{1,0:T(8,128)(2,1)} %get-tuple-element.59.hid_b), channel_id=1, source_target_pairs={{0,1},{1,2},{2,3},{3,4},{4,5},{5,6},{6,7},{7,0}} | collective-permute-start | bytes 3145736 | tf_op jit(solution)/shard_map/ppermute | solution.py:427
  141.6 24.2 %collective-permute-start.6 = (bf16[2048,128]{1,0:T(8,128)(2,1)}, bf16[2048,128]{1,0:T(8,128)(2,1)}, u32[]{:S(2)}, u32[]{:S(2)}) collective-permute-start(bf16[2048,128]{1,0:T(8,128)(2,1)} %get-tuple-element.58), channel_id=1, source_target_pairs={{0,7},{1,0},{2,1},{3,2},{4,3},{5,4},{6,5},{7,6}} | collective-permute-start | bytes 1572872 | tf_op jit(solution)/shard_map/ppermute | solution.py:430
  144.2 25.0 %collective-permute-start.9 = (bf16[2048,128]{1,0:T(8,128)(2,1)}, bf16[2048,128]{1,0:T(8,128)(2,1)}, u32[]{:S(2)}, u32[]{:S(2)}) collective-permute-start(bf16[2048,128]{1,0:T(8,128)(2,1)} %get-tuple-element.58), channel_id=1, source_target_pairs={{0,1},{1,2},{2,3},{3,4},{4,5},{5,6},{6,7},{7,0}} | collective-permute-start | bytes 1572872 | tf_op jit(solution)/shard_map/ppermute | solution.py:427
  144.2 25.0 %copy-start.1 = (bf16[128,512]{1,0:T(8,128)(2,1)S(1)}, bf16[128,512]{1,0:T(8,128)(2,1)}, u32[]{:S(2)}) copy-start(bf16[128,512]{1,0:T(8,128)(2,1)} %copy-done) | copy-start | bytes 393220

commit v5 on v4

--- a/solution.py
+++ b/solution.py
@@ -67,12 +67,11 @@
         def body(j):
             off = r * SLOT + (SLOT - unroll - j * unroll if back else j * unroll)
             frm, to, wgt = (ref.at[pl.ds(off, unroll)] for ref in (from_ref, to_ref, w_ref))
-            for g in range(0, unroll, n_acc):
-                vals = [table[pl.ds(pl.multiple_of(frm[g + k], width), width), :] * wgt[g + k] for k in range(n_acc)]
-                rows = [pl.multiple_of(to[g + k], width) for k in range(n_acc)]
-                old = [accs[k][pl.ds(rows[k], width), :] for k in range(n_acc)]
-                for k in range(n_acc):
-                    accs[k][pl.ds(rows[k], width), :] = old[k] + vals[k]
+            for u in range(unroll):
+                acc = accs[u % n_acc]
+                val = table[pl.ds(pl.multiple_of(frm[u], width), width), :] * wgt[u]
+                at = pl.ds(pl.multiple_of(to[u], width), width)
+                acc[at, :] = acc[at, :] + val
 
         loop(blocks, body)
 
@@ -94,11 +93,11 @@
     loop(ids_ref.shape[0] // unroll, body)
 
 
-def gather_pass(ids_ref, table, out, width, unroll=8):
+def gather_pass(ids_ref, table, out, width, unroll=16):
     def body(j):
         for u in range(unroll):
             i = j * unroll + u
-            out[pl.ds(pl.multiple_of(i * width, width), width), :] = table[pl.ds(pl.multiple_of(ids_ref[i], width), width), :]
+            out[pl.ds(pl.multiple_of(i * width, width), width), :] = table[pl.ds(pl.multiple_of(ids_ref[i] * width, width), width), :]
 
     loop(ids_ref.shape[0] // unroll, body)
 
@@ -147,7 +146,7 @@
     count[...] = jnp.maximum(total, 1.0)
 
 
-def halo_rows_kernel(ids2, x, to_next, to_prev, table, picked):
+def halo_rows_kernel(ids, x, to_next, to_prev, table, picked):
     rows = x.shape[0]
 
     def put(i):
@@ -156,7 +155,7 @@
         spread(table, i * BLOCK, jnp.concatenate([block, pad], axis=1))
 
     loop(rows // BLOCK, put)
-    gather_pass(ids2, table, picked, 2)
+    gather_pass(ids, table, picked, 2)
     half = to_next.shape[0]
 
     def take(i):
@@ -174,7 +173,7 @@
         spread(table, i * BLOCK, t.astype(BF16).astype(F32))
 
     loop(x.shape[0] // BLOCK, put)
-    edge_pass(s4, d4, w, cnt, table, accs, 4, 16, False)
+    edge_pass(s4, d4, w, cnt, table, accs, 4, 32, False)
     sum_rows(y, accs)
 
 
@@ -212,13 +211,13 @@
 
 def narrow_own_kernel(frm, to, w, cnt, table, out, *accs):
     zero_rows(accs)
-    edge_pass(frm, to, w, cnt, table, accs, 1, 16, False)
+    edge_pass(frm, to, w, cnt, table, accs, 1, 32, False)
     sum_rows(out, accs)
 
 
 def wide_own_kernel(frm, to, w, cnt, table, out, *accs):
     zero_rows(accs)
-    edge_pass(frm, to, w, cnt, table, accs, 4, 16, False)
+    edge_pass(frm, to, w, cnt, table, accs, 4, 32, False)
     sum_rows(out, accs)
 
 
@@ -303,10 +302,10 @@
     loop(n_loc // BLOCK, fold)
 
 
-def peer_pass(ids4, code_ref, w_ref, rows, far, table, accs):
+def peer_pass(ids, code_ref, w_ref, rows, far, table, accs):
     n_acc = len(accs)
     tally = rows * SLOT
-    n_loc = ids4.shape[0]
+    n_loc = ids.shape[0]
     shift = n_loc.bit_length() - 1
 
     def row(r):
@@ -321,7 +320,7 @@
                 code = codes[u]
                 frm = lax.shift_right_logical(code, shift) * 4
                 val = table[pl.ds(pl.multiple_of(frm, 4), 4), :] * wgt[u]
-                at = pl.ds(pl.multiple_of(ids4[code & (n_loc - 1)], 4), 4)
+                at = pl.ds(pl.multiple_of(ids[code & (n_loc - 1)] * 4, 4), 4)
                 acc[at, :] = acc[at, :] + val
 
         loop(lax.shift_right_logical(edges + 15, 4), body)
@@ -329,7 +328,7 @@
     loop(rows, row)
 
 
-def table_grad_kernel(rows, ids4, cn, wn, cp, wp, own, tn, han, hbn, tp, hap, hbp, w2t, x, g1, table, *accs):
+def table_grad_kernel(rows, ids, cn, wn, cp, wp, own, tn, han, hbn, tp, hap, hbp, w2t, x, g1, table, *accs):
     zero_rows(accs)
     g1[...] = jnp.zeros_like(g1)
 
@@ -342,9 +341,9 @@
         loop(dt.shape[0] // BLOCK, put)
 
     fill(tn, han, hbn)
-    peer_pass(ids4, cn, wn, rows, 0, table, accs)
+    peer_pass(ids, cn, wn, rows, 0, table, accs)
     fill(tp, hap, hbp)
-    peer_pass(ids4, cp, wp, rows, 1, table, accs)
+    peer_pass(ids, cp, wp, rows, 1, table, accs)
 
     def fold(i):
         total = unspread(own, i * BLOCK, BLOCK, 4)
@@ -355,7 +354,7 @@
     loop(x.shape[0] // BLOCK, fold)
 
 
-def reduce_kernel(num_dev, g1, g2, loss, o1, o2, lo, r1, r2, s1, s2, q1, q2, lslots, sem_s, sem_r, lsem_s, lsem_r):
+def reduce_kernel(num_dev, g1, g2, loss, count, o1, o2, lo, r1, r2, s1, s2, q1, q2, lslots, sem_s, sem_r, lsem_s, lsem_r):
     me = lax.axis_index(GRAPH_AXIS)
     core = lax.rem(me, 2)
     chip = me // 2
@@ -413,7 +412,8 @@
     total = loss[...]
     for step in range(num_dev - 1):
         total = total + lslots[step]
-    lo[...] = total
+    total = jnp.sum(jnp.sum(total, axis=1, keepdims=True), axis=0, keepdims=True)
+    lo[...] = total / count[...]
     for copy in tails:
         copy.wait()
 
@@ -488,14 +488,13 @@
             scratch_shapes=[pltpu.VMEM((2 * n_loc, LANES), F32), pltpu.VMEM((4 * halo, LANES), F32)],
             compiler_params=params(12),
             name="halo_rows",
-        )(ids * 2, x)
+        )(ids, x)
         xh_prev = shift_next(x_next)
         xh_next = shift_prev(x_prev)
         wide4 = [pltpu.VMEM((quad, LANES), F32)] * 4
         thin4 = [pltpu.VMEM((n_loc, LANES), F32)] * 4
         marks = jnp.where(label_mask == 1, labels, -1)
-        ids4 = ids * 4
-        s4, w2t, marks, ids4 = lax.optimization_barrier((s4, w2t, marks, ids4))
+        s4, w2t, marks, ids = lax.optimization_barrier((s4, w2t, marks, ids))
         y_own = pl.pallas_call(
             one_own_kernel,
             out_shape=sds((quad, LANES), F32),
@@ -572,11 +571,11 @@
             scratch_shapes=[pltpu.VMEM((quad, LANES), F32)] + wide4,
             compiler_params=params(36),
             name="table_grad",
-        )(ids4, code_next.reshape(-1), w_next.reshape(-1), code_prev.reshape(-1), w_prev.reshape(-1), dt1_own, dt_next, ha_next, hb_next, dt_prev, ha_prev, hb_prev, w2t, x)
+        )(ids, code_next.reshape(-1), w_next.reshape(-1), code_prev.reshape(-1), w_prev.reshape(-1), dt1_own, dt_next, ha_next, hb_next, dt_prev, ha_prev, hb_prev, w2t, x)
         grad_one, grad_two, loss = pl.pallas_call(
             functools.partial(reduce_kernel, num_dev),
             out_shape=[sds((256, f_hid), F32), sds((f_hid, LANES), F32), sds((8, LANES), F32)],
-            in_specs=[VMEM_SPEC] * 3,
+            in_specs=[VMEM_SPEC] * 4,
             out_specs=[VMEM_SPEC] * 3,
             scratch_shapes=[
                 pltpu.VMEM((128, f_hid), F32), pltpu.VMEM((f_hid // 2, LANES), F32),
@@ -588,9 +587,8 @@
             ],
             compiler_params=params(8, collective_id=1, has_side_effects=True),
             name="reduce",
-        )(grad_one, grad_two, loss)
-        mean_loss = jnp.sum(loss) / count[0, 0]
-        return mean_loss, grad_one[:f_in], grad_two[:, :classes]
+        )(grad_one, grad_two, loss, count)
+        return loss[0, 0], grad_one[:f_in], grad_two[:, :classes]
 
     row_spec = P(GRAPH_AXIS)
     return jax.shard_map(device_step, mesh=mesh, in_specs=(row_spec, P(), P(), row_spec, row_spec, row_spec, row_spec, row_spec, row_spec), out_specs=(P(), P(), P()), check_vma=False)

time: 207 us -> 201 us (0.971)
  Pallas kernels: 153 us -> 148 us
  between operations: 3.35 us -> 0.95 us
  transfers between devices with their start and end apart: 12 -> 12, of which waited for: 3 -> 3; matrix products, arithmetic and copies ran while one was open for 0% -> 0% of each run, Pallas kernels for 44% -> 43%
where the time goes in v5:
time: 201 us; the launch traced here: 200 us
  Pallas kernels  148 us (74%)
  waiting for transfers between devices  23.5 us (12%)
  starting transfers between devices  13.7 us (7%)
  local copies, waits for them, and re-layouts  7.2 us (4%)
  other arithmetic  6.71 us (3%)
    ppermute x6, waiting for transfers between devices, shift_next(): return lax.ppermute(a, GRAPH_AXIS, to_next)  17.9 us
    pallas_call x1, Pallas kernels, device_step(): pl.pallas_call(functools.partial(logits_kernel, classes), out_shape=[sds(...  17.4 us
    pallas_call x1, Pallas kernels, device_step(): pl.pallas_call(one_own_kernel, out_shape=sds((quad, LANES), F32), in_spec...  17.3 us
    pallas_call x1, Pallas kernels, device_step(): pl.pallas_call(functools.partial(reduce_kernel, num_dev), out_shape=[sds(...  16.9 us
    pallas_call x1, Pallas kernels, device_step(): pl.pallas_call(one_halo_kernel, out_shape=[sds((n_loc, f_hid // 2), BF16)...  16.1 us
    pallas_call x1, Pallas kernels, device_step(): pl.pallas_call(functools.partial(table_grad_kernel, rows), out_shape=sds(...  15.7 us
    pallas_call x1, Pallas kernels, device_step(): pl.pallas_call(wide_own_kernel, out_shape=sds((quad, LANES), F32), in_spe...  15.5 us
    pallas_call x1, Pallas kernels, device_step(): dt2_own = narrow_own(name='two_back_own')(d, s, wc, n_own, dz)  13.6 us
  transfers between devices with their start and end apart: 12, of which 3 were waited for; matrix products, arithmetic and copies ran while one was open for 0% of the time, Pallas kernels for 43%

profile of v5, /device:TPU:0, one launch (start us, length us, event | category | flops | bytes accessed | tf_op | source)
XLA Modules:
  0.0 200.3 jit_solution(3319766200305598004)
XLA Ops:
  0.7 0.8 reshape.63
  3.6 4.2 %select_reduce_fusion = (s32[32,384]{1,0:T(8,128)S(1)}, f32[32,384]{1,0:T(8,128)S(1)}) fusion(f32[32,256]{1,0:T(8,128)S(1)} %reshape.63, s32[32,256]{1,0:T(8,128)S(1)} %get-tuple-element.86, s32[32,256]{1,0:T(8,128)S(1)} %get-tuple-element.87), kind=kLoop, calls=%fused_computation | loop fusion | flops 15704064 | bytes 196608 | tf_op jit(solution)/shard_map/reduce | solution.py:451
  9.5 8.0 %lists.1 = (f32[8,128]{1,0:T(8,128)S(1)}, s32[104,128]{1,0:T(8,128)S(1)}, s32[104,128]{1,0:T(8,128)S(1)}, f32[96,128]{1,0:T(8,128)S(1)}, f32[96,128]{1,0:T(8,128)S(1)}) custom-call(s32[16,128]{1,0:T(8,128)S(1)} %bitcast.18, s32[104,128]{1,0:T(8,128)S(1)} %bitcast.13, f32[96,128]{1,0:T(8,128)S(1)} %reshape_reshape.3.wgt), custom_call_target="tpu_custom_call" | custom-call | tf_op jit(solution)/shard_map/lists/pallas_call | solution.py:471
  17.5 1.4 copy.16.x
  19.0 1.3 pad_add_fusion.1
  20.3 4.7 %halo_rows.1 = (bf16[1024,256]{1,0:T(8,128)(2,1)}, bf16[1024,256]{1,0:T(8,128)(2,1)}) custom-call(s32[2048]{0:T(1024)S(1)} %get-tuple-element.35.ids, bf16[2048,200]{1,0:T(8,128)(2,1)S(1)} %copy.16.x), custom_call_target="tpu_custom_call" | custom-call | tf_op jit(solution)/shard_map/halo_rows/pallas_call | solution.py:483
  25.4 2.2 %collective-permute-start.1 = (bf16[1024,256]{1,0:T(8,128)(2,1)}, bf16[1024,256]{1,0:T(8,128)(2,1)}, u32[]{:S(2)}, u32[]{:S(2)}) collective-permute-start(bf16[1024,256]{1,0:T(8,128)(2,1)} %get-tuple-element.45), channel_id=1, source_target_pairs={{0,7},{1,0},{2,1},{3,2},{4,3},{5,4},{6,5},{7,6}} | collective-permute-start | bytes 1572872 | tf_op jit(solution)/shard_map/ppermute | solution.py:430
  27.8 17.3 %one_own.1.y_own = f32[8192,128]{1,0:T(8,128)S(1)} custom-call(s32[12288]{0:T(1024)S(1)} %get-tuple-element.41.s4.to, s32[12288]{0:T(1024)S(1)} %get-tuple-element.73.d4.frm, f32[12288]{0:T(1024)S(1)} %reshape.72.w, s32[32]{0:T(128)S(1)} %get-tuple-element.85.cnt, bf16[2048,200]{1,0:T(8,128)(2,1)S(1)} %copy.16.x, bf16[200,512]{1,0:T(8,128)(2,1)S(1)} %convert_element_type.30.w1), custom_call_target="tpu_custom_call" | custom-call | flops 199999995904 | bytes 8000000 | tf_op jit(solution)/shard_map/one_own/pallas_call | solution.py:498
  45.2 16.1 %one_halo.1 = (bf16[2048,256]{1,0:T(8,128)(2,1)}, bf16[2048,256]{1,0:T(8,128)(2,1)}, f32[2048,128]{1,0:T(8,128)S(1)}, bf16[1024,128]{1,0:T(8,128)(2,1)}, bf16[1024,128]{1,0:T(8,128)(2,1)}) custom-call(s32[12288]{0:T(1024)S(1)} %get-tuple-element.41.s4.to, s32[12288]{0:T(1024)S(1)} %get-tuple-element.73.d4.frm, f32[12288]{0:T(1024)S(1)} %reshape.72.w, ...), custom_call_target="tpu_custom_call" | custom-call | tf_op jit(solution)/shard_map/one_halo/pallas_call | solution.py:508
  61.3 1.4 collective-permute-start.7
  62.7 2.7 %collective-permute-start.3 = (bf16[1024,128]{1,0:T(8,128)(2,1)}, bf16[1024,128]{1,0:T(8,128)(2,1)}, u32[]{:S(2)}, u32[]{:S(2)}) collective-permute-start(bf16[1024,128]{1,0:T(8,128)(2,1)} %get-tuple-element.49), channel_id=1, source_target_pairs={{0,7},{1,0},{2,1},{3,2},{4,3},{5,4},{6,5},{7,6}} | collective-permute-start | bytes 786440 | tf_op jit(solution)/shard_map/ppermute | solution.py:430
  65.4 13.6 %two_own.1.z_own = f32[2048,128]{1,0:T(8,128)S(1)} custom-call(s32[12288]{0:T(1024)S(1)} %get-tuple-element.80.frm.s.to, s32[12288]{0:T(1024)S(1)} %get-tuple-element.74.to.d.frm, f32[12288]{0:T(1024)S(1)} %reshape.72.w, s32[32]{0:T(128)S(1)} %get-tuple-element.85.cnt, f32[2048,128]{1,0:T(8,128)S(1)} %get-tuple-element.47.table), custom_call_target="tpu_custom_call" | custom-call | flops 199999995904 | bytes 8000000 | tf_op jit(solution)/shard_map/two_own/pallas_call | solution.py:530
  79.0 14.4 %collective-permute-done.2.t_prev = bf16[1024,128]{1,0:T(8,128)(2,1)} collective-permute-done((bf16[1024,128]{1,0:T(8,128)(2,1)}, bf16[1024,128]{1,0:T(8,128)(2,1)}, u32[]{:S(2)}, u32[]{:S(2)}) %collective-permute-start.2) | collective-permute-done | bytes 262176 | tf_op jit(solution)/shard_map/ppermute | solution.py:427
  93.7 17.4 %logits.1 = (f32[2048,128]{1,0:T(8,128)S(1)}, f32[1024,128]{1,0:T(8,128)}, f32[1024,128]{1,0:T(8,128)}, f32[8,128]{1,0:T(8,128)S(1)}) custom-call(s32[12288]{0:T(1024)S(1)} %get-tuple-element.80.frm.s.to, s32[12288]{0:T(1024)S(1)} %get-tuple-element.74.to.d.frm, f32[12288]{0:T(1024)S(1)} %reshape.72.w, s32[32]{0:T(128)S(1)} %get-tuple-element.71.cnt, ...), custom_call_target="tpu_custom_call" | custom-call | tf_op jit(solution)/shard_map/logits/pallas_call | solution.py:532
  111.1 1.0 collective-permute-start.4
  112.2 13.6 %two_back_own.1.own = f32[2048,128]{1,0:T(8,128)S(1)} custom-call(s32[12288]{0:T(1024)S(1)} %get-tuple-element.74.to.d.frm, s32[12288]{0:T(1024)S(1)} %get-tuple-element.80.frm.s.to, f32[12288]{0:T(1024)S(1)} %reshape.72.w, s32[32]{0:T(128)S(1)} %get-tuple-element.85.cnt, f32[2048,128]{1,0:T(8,128)S(1)} %get-tuple-element.52.table), custom_call_target="tpu_custom_call" | custom-call | flops 199999995904 | bytes 8000000 | tf_op jit(solution)/shard_map/two_back_own/pallas_call | solution.py:545
  125.7 3.3 %collective-permute-start.8 = (bf16[2048,256]{1,0:T(8,128)(2,1)}, bf16[2048,256]{1,0:T(8,128)(2,1)}, u32[]{:S(2)}, u32[]{:S(2)}) collective-permute-start(bf16[2048,256]{1,0:T(8,128)(2,1)} %get-tuple-element.59.hid_b), channel_id=1, source_target_pairs={{0,7},{1,0},{2,1},{3,2},{4,3},{5,4},{6,5},{7,6}} | collective-permute-start | bytes 3145736 | tf_op jit(solution)/shard_map/ppermute | solution.py:430
  129.1 9.1 %hidden_grad.1 = (bf16[2048,128]{1,0:T(8,128)(2,1)}, f32[8192,128]{1,0:T(8,128)S(1)}, f32[512,128]{1,0:T(8,128)S(1)}) custom-call(s32[2048]{0:T(1024)S(1)} %copy-done.3, f32[2048,128]{1,0:T(8,128)S(1)} %two_back_own.1.own, f32[1024,128]{1,0:T(8,128)} %collective-permute-done.4.ret_next, f32[1024,128]{1,0:T(8,128)} %collective-permute-done.5.ret_prev, ...), custom_call_target="tpu_custom_call" | custom-call | tf_op jit(solution)/shard_map/hidden_grad/pallas_call | solution.py:546
  138.2 2.6 %collective-permute-start.6 = (bf16[2048,128]{1,0:T(8,128)(2,1)}, bf16[2048,128]{1,0:T(8,128)(2,1)}, u32[]{:S(2)}, u32[]{:S(2)}) collective-permute-start(bf16[2048,128]{1,0:T(8,128)(2,1)} %get-tuple-element.58), channel_id=1, source_target_pairs={{0,7},{1,0},{2,1},{3,2},{4,3},{5,4},{6,5},{7,6}} | collective-permute-start | bytes 1572872 | tf_op jit(solution)/shard_map/ppermute | solution.py:430
  140.9 15.5 %one_back_own.1.own = f32[8192,128]{1,0:T(8,128)S(1)} custom-call(s32[12288]{0:T(1024)S(1)} %get-tuple-element.73.d4.frm, s32[12288]{0:T(1024)S(1)} %get-tuple-element.41.s4.to, f32[12288]{0:T(1024)S(1)} %reshape.72.w, s32[32]{0:T(128)S(1)} %get-tuple-element.85.cnt, f32[8192,128]{1,0:T(8,128)S(1)} %get-tuple-element.57.table), custom_call_target="tpu_custom_call" | custom-call | flops 199999995904 | bytes 8000000 | tf_op jit(solution)/shard_map/one_back_own/pallas_call | solution.py:556
  156.5 5.5 %collective-permute-done.6.tn = bf16[2048,128]{1,0:T(8,128)(2,1)} collective-permute-done((bf16[2048,128]{1,0:T(8,128)(2,1)}, bf16[2048,128]{1,0:T(8,128)(2,1)}, u32[]{:S(2)}, u32[]{:S(2)}) %collective-permute-start.6) | collective-permute-done | bytes 524320 | tf_op jit(solution)/shard_map/ppermute | solution.py:430
  162.0 3.5 %collective-permute-done.9.tp = bf16[2048,128]{1,0:T(8,128)(2,1)} collective-permute-done((bf16[2048,128]{1,0:T(8,128)(2,1)}, bf16[2048,128]{1,0:T(8,128)(2,1)}, u32[]{:S(2)}, u32[]{:S(2)}) %collective-permute-start.9) | collective-permute-done | bytes 524320 | tf_op jit(solution)/shard_map/ppermute | solution.py:427
  165.5 15.7 %table_grad.1.g1 = f32[256,512]{1,0:T(8,128)S(1)} custom-call(s32[2048]{0:T(1024)S(1)} %copy-done.4, s32[13312]{0:T(1024)S(1)} %bitcast.15, f32[12288]{0:T(1024)S(1)} %bitcast.17, s32[13312]{0:T(1024)S(1)} %bitcast.14, f32[12288]{0:T(1024)S(1)} %bitcast.16, f32[8192,128]{1,0:T(8,128)S(1)} %one_back_own.1.own, bf16[2048,128]{1,0:T(8,128)(2,1)} %collective-permute-done.6.tn, ...), custom_call_target="tpu_custom_call" | custom-call | tf_op jit(solution)/shard_map/table_grad/pallas_call | solution.py:566
  181.2 16.9 %reduce.18 = (f32[256,512]{1,0:T(8,128)S(1)}, f32[512,128]{1,0:T(8,128)S(1)}, f32[8,128]{1,0:T(8,128)S(1)}) custom-call(f32[256,512]{1,0:T(8,128)S(1)} %table_grad.1.g1, f32[512,128]{1,0:T(8,128)S(1)} %get-tuple-element.60.g2, f32[8,128]{1,0:T(8,128)S(1)} %get-tuple-element.61.loss, f32[8,128]{1,0:T(8,128)S(1)} %get-tuple-element.51.count), custom_call_target="tpu_custom_call" | custom-call | tf_op jit(solution)/shard_map/reduce/pallas_call | solution.py:575
  (59 shorter events, 6.7 us)
Async XLA Ops:
  0.6 27.1 %copy-start.7 = (f32[512,107]{0,1:T(8,128)S(1)}, f32[512,107]{0,1:T(8,128)}, u32[]{:S(2)}) copy-start(f32[512,107]{0,1:T(8,128)} %param.11) | copy-start | bytes 657412
  0.6 27.1 %copy-start.6 = (f32[200,512]{1,0:T(8,128)S(1)}, f32[200,512]{1,0:T(8,128)}, u32[]{:S(2)}) copy-start(f32[200,512]{1,0:T(8,128)} %param.10) | copy-start | bytes 1228804
  8.8 0.7 copy-start.5
  20.3 7.4 %copy-start.2 = (s32[2048]{0:T(1024)}, s32[2048]{0:T(1024)S(1)}, u32[]{:S(2)}) copy-start(s32[2048]{0:T(1024)S(1)} %get-tuple-element.35.ids) | copy-start | bytes 24580
  25.0 20.2 %collective-permute-start = (bf16[1024,256]{1,0:T(8,128)(2,1)}, bf16[1024,256]{1,0:T(8,128)(2,1)}, u32[]{:S(2)}, u32[]{:S(2)}) collective-permute-start(bf16[1024,256]{1,0:T(8,128)(2,1)} %get-tuple-element.44), channel_id=1, source_target_pairs={{0,1},{1,2},{2,3},{3,4},{4,5},{5,6},{6,7},{7,0}} | collective-permute-start | bytes 1572872 | tf_op jit(solution)/shard_map/ppermute | solution.py:427
  25.4 19.7 %collective-permute-start.1 = (bf16[1024,256]{1,0:T(8,128)(2,1)}, bf16[1024,256]{1,0:T(8,128)(2,1)}, u32[]{:S(2)}, u32[]{:S(2)}) collective-permute-start(bf16[1024,256]{1,0:T(8,128)(2,1)} %get-tuple-element.45), channel_id=1, source_target_pairs={{0,7},{1,0},{2,1},{3,2},{4,3},{5,4},{6,5},{7,6}} | collective-permute-start | bytes 1572872 | tf_op jit(solution)/shard_map/ppermute | solution.py:430
  27.8 101.3 %copy-start = (bf16[128,512]{1,0:T(8,128)(2,1)}, bf16[128,512]{1,0:T(8,128)(2,1)S(1)}, u32[]{:S(2)}) copy-start(bf16[128,512]{1,0:T(8,128)(2,1)S(1)} %pad.4.w2t) | copy-start | bytes 393220
  27.8 17.4 %copy-start.3 = (s32[2048]{0:T(1024)S(1)}, s32[2048]{0:T(1024)}, u32[]{:S(2)}) copy-start(s32[2048]{0:T(1024)} %copy-done.2) | copy-start | bytes 24580
  61.3 79.6 %collective-permute-start.7 = (bf16[2048,256]{1,0:T(8,128)(2,1)}, bf16[2048,256]{1,0:T(8,128)(2,1)}, u32[]{:S(2)}, u32[]{:S(2)}) collective-permute-start(bf16[2048,256]{1,0:T(8,128)(2,1)} %get-tuple-element.55.hid_a), channel_id=1, source_target_pairs={{0,7},{1,0},{2,1},{3,2},{4,3},{5,4},{6,5},{7,6}} | collective-permute-start | bytes 3145736 | tf_op jit(solution)/shard_map/ppermute | solution.py:430
  62.7 93.7 %collective-permute-start.10 = (bf16[2048,256]{1,0:T(8,128)(2,1)}, bf16[2048,256]{1,0:T(8,128)(2,1)}, u32[]{:S(2)}, u32[]{:S(2)}) collective-permute-start(bf16[2048,256]{1,0:T(8,128)(2,1)} %get-tuple-element.55.hid_a), channel_id=1, source_target_pairs={{0,1},{1,2},{2,3},{3,4},{4,5},{5,6},{6,7},{7,0}} | collective-permute-start | bytes 3145736 | tf_op jit(solution)/shard_map/ppermute | solution.py:427
  62.7 30.7 %collective-permute-start.2 = (bf16[1024,128]{1,0:T(8,128)(2,1)}, bf16[1024,128]{1,0:T(8,128)(2,1)}, u32[]{:S(2)}, u32[]{:S(2)}) collective-permute-start(bf16[1024,128]{1,0:T(8,128)(2,1)} %get-tuple-element.48), channel_id=1, source_target_pairs={{0,1},{1,2},{2,3},{3,4},{4,5},{5,6},{6,7},{7,0}} | collective-permute-start | bytes 786440 | tf_op jit(solution)/shard_map/ppermute | solution.py:427
  62.7 30.7 %collective-permute-start.3 = (bf16[1024,128]{1,0:T(8,128)(2,1)}, bf16[1024,128]{1,0:T(8,128)(2,1)}, u32[]{:S(2)}, u32[]{:S(2)}) collective-permute-start(bf16[1024,128]{1,0:T(8,128)(2,1)} %get-tuple-element.49), channel_id=1, source_target_pairs={{0,7},{1,0},{2,1},{3,2},{4,3},{5,4},{6,5},{7,6}} | collective-permute-start | bytes 786440 | tf_op jit(solution)/shard_map/ppermute | solution.py:430
  65.4 28.0 %copy-start.8 = (s32[2048]{0:T(1024)S(1)}, s32[2048]{0:T(1024)}, u32[]{:S(2)}) copy-start(s32[2048]{0:T(1024)} %get-tuple-element.50) | copy-start | bytes 24580
  111.1 17.9 %collective-permute-start.4 = (f32[1024,128]{1,0:T(8,128)}, f32[1024,128]{1,0:T(8,128)}, u32[]{:S(2)}, u32[]{:S(2)}) collective-permute-start(f32[1024,128]{1,0:T(8,128)} %get-tuple-element.53), channel_id=1, source_target_pairs={{0,7},{1,0},{2,1},{3,2},{4,3},{5,4},{6,5},{7,6}} | collective-permute-start | bytes 1572872 | tf_op jit(solution)/shard_map/ppermute | solution.py:430
  112.2 16.9 %collective-permute-start.5 = (f32[1024,128]{1,0:T(8,128)}, f32[1024,128]{1,0:T(8,128)}, u32[]{:S(2)}, u32[]{:S(2)}) collective-permute-start(f32[1024,128]{1,0:T(8,128)} %get-tuple-element.54), channel_id=1, source_target_pairs={{0,1},{1,2},{2,3},{3,4},{4,5},{5,6},{6,7},{7,0}} | collective-permute-start | bytes 1572872 | tf_op jit(solution)/shard_map/ppermute | solution.py:427
  125.7 36.3 %collective-permute-start.8 = (bf16[2048,256]{1,0:T(8,128)(2,1)}, bf16[2048,256]{1,0:T(8,128)(2,1)}, u32[]{:S(2)}, u32[]{:S(2)}) collective-permute-start(bf16[2048,256]{1,0:T(8,128)(2,1)} %get-tuple-element.59.hid_b), channel_id=1, source_target_pairs={{0,7},{1,0},{2,1},{3,2},{4,3},{5,4},{6,5},{7,6}} | collective-permute-start | bytes 3145736 | tf_op jit(solution)/shard_map/ppermute | solution.py:430
  129.1 36.4 %collective-permute-start.11 = (bf16[2048,256]{1,0:T(8,128)(2,1)}, bf16[2048,256]{1,0:T(8,128)(2,1)}, u32[]{:S(2)}, u32[]{:S(2)}) collective-permute-start(bf16[2048,256]{1,0:T(8,128)(2,1)} %get-tuple-element.59.hid_b), channel_id=1, source_target_pairs={{0,1},{1,2},{2,3},{3,4},{4,5},{5,6},{6,7},{7,0}} | collective-permute-start | bytes 3145736 | tf_op jit(solution)/shard_map/ppermute | solution.py:427
  138.2 23.8 %collective-permute-start.6 = (bf16[2048,128]{1,0:T(8,128)(2,1)}, bf16[2048,128]{1,0:T(8,128)(2,1)}, u32[]{:S(2)}, u32[]{:S(2)}) collective-permute-start(bf16[2048,128]{1,0:T(8,128)(2,1)} %get-tuple-element.58), channel_id=1, source_target_pairs={{0,7},{1,0},{2,1},{3,2},{4,3},{5,4},{6,5},{7,6}} | collective-permute-start | bytes 1572872 | tf_op jit(solution)/shard_map/ppermute | solution.py:430
  140.9 24.6 %collective-permute-start.9 = (bf16[2048,128]{1,0:T(8,128)(2,1)}, bf16[2048,128]{1,0:T(8,128)(2,1)}, u32[]{:S(2)}, u32[]{:S(2)}) collective-permute-start(bf16[2048,128]{1,0:T(8,128)(2,1)} %get-tuple-element.58), channel_id=1, source_target_pairs={{0,1},{1,2},{2,3},{3,4},{4,5},{5,6},{6,7},{7,0}} | collective-permute-start | bytes 1572872 | tf_op jit(solution)/shard_map/ppermute | solution.py:427
  140.9 24.6 %copy-start.1 = (bf16[128,512]{1,0:T(8,128)(2,1)S(1)}, bf16[128,512]{1,0:T(8,128)(2,1)}, u32[]{:S(2)}) copy-start(bf16[128,512]{1,0:T(8,128)(2,1)} %copy-done) | copy-start | bytes 393220
  140.9 24.6 %copy-start.4 = (s32[2048]{0:T(1024)S(1)}, s32[2048]{0:T(1024)}, u32[]{:S(2)}) copy-start(s32[2048]{0:T(1024)} %copy-done.2) | copy-start | bytes 24580

commit v6 on v5

--- a/solution.py
+++ b/solution.py
@@ -66,7 +66,11 @@
 
         def body(j):
             off = r * SLOT + (SLOT - unroll - j * unroll if back else j * unroll)
-            frm, to, wgt = (ref.at[pl.ds(off, unroll)] for ref in (from_ref, to_ref, w_ref))
+            frm, to = (ref.at[pl.ds(off, unroll)] for ref in (from_ref, to_ref))
+            if back:
+                wgt = w_ref.at[pl.ds(off, unroll)]
+            else:
+                wgt = [jnp.broadcast_to(w_ref[pl.ds(r * CHUNK + j * unroll + u, 1), :], (width, LANES)) for u in range(unroll)]
             for u in range(unroll):
                 acc = accs[u % n_acc]
                 val = table[pl.ds(pl.multiple_of(frm[u], width), width), :] * wgt[u]
@@ -165,7 +169,7 @@
     loop(half // BLOCK, take)
 
 
-def one_own_kernel(s4, d4, w, cnt, x, w1, y, table, *accs):
+def one_own_kernel(s4, d4, cnt, x, w1, w, y, table, *accs):
     zero_rows(accs)
 
     def put(i):
@@ -209,13 +213,13 @@
     loop(half // BLOCK, take)
 
 
-def narrow_own_kernel(frm, to, w, cnt, table, out, *accs):
+def narrow_own_kernel(frm, to, cnt, table, w, out, *accs):
     zero_rows(accs)
     edge_pass(frm, to, w, cnt, table, accs, 1, 32, False)
     sum_rows(out, accs)
 
 
-def wide_own_kernel(frm, to, w, cnt, table, out, *accs):
+def wide_own_kernel(frm, to, cnt, table, w, out, *accs):
     zero_rows(accs)
     edge_pass(frm, to, w, cnt, table, accs, 4, 32, False)
     sum_rows(out, accs)
@@ -465,6 +469,7 @@
         code, wc, n_own, n_hal, n_near, n_far, skip = compact(edge_src, edge_dst, edge_w, n_loc, halo)
         rows = n_own.shape[0]
         slots = code.size // LANES
+        w_own = jnp.broadcast_to(wc[:, :CHUNK].reshape(-1, 1), (rows * CHUNK, LANES))
         code, wc = code.reshape(-1), wc.reshape(-1)
         tally = jnp.concatenate([n_near, n_far, skip, jnp.zeros((8 * LANES - 3 * rows,), jnp.int32)])
         lists = jnp.concatenate([code, tally]).reshape(slots + 8, LANES)
@@ -494,17 +499,17 @@
         wide4 = [pltpu.VMEM((quad, LANES), F32)] * 4
         thin4 = [pltpu.VMEM((n_loc, LANES), F32)] * 4
         marks = jnp.where(label_mask == 1, labels, -1)
-        s4, w2t, marks, ids = lax.optimization_barrier((s4, w2t, marks, ids))
+        s4, w2t, marks, ids, w_own, wc = lax.optimization_barrier((s4, w2t, marks, ids, w_own, wc))
         y_own = pl.pallas_call(
             one_own_kernel,
             out_shape=sds((quad, LANES), F32),
-            in_specs=[SMEM_SPEC] * 4 + [VMEM_SPEC] * 2,
+            in_specs=[SMEM_SPEC] * 3 + [VMEM_SPEC] * 3,
             out_specs=VMEM_SPEC,
             scratch_shapes=[pltpu.VMEM((quad, LANES), F32)] + wide4,
-            compiler_params=params(28),
+            compiler_params=params(32),
             cost_estimate=pl.CostEstimate(flops=200000000000, bytes_accessed=8000000, transcendentals=0),
             name="one_own",
-        )(s4, d4, wc, n_own, x, w1)
+        )(s4, d4, n_own, x, w1, w_own)
         hid_a, hid_b, t2, t_next, t_prev = pl.pallas_call(
             one_halo_kernel,
             out_shape=[sds((n_loc, f_hid // 2), BF16)] * 2 + [sds((n_loc, LANES), F32), sds((halo, LANES), BF16), sds((halo, LANES), BF16)],
@@ -521,13 +526,13 @@
             pl.pallas_call,
             narrow_own_kernel,
             out_shape=sds((n_loc, LANES), F32),
-            in_specs=[SMEM_SPEC] * 4 + [VMEM_SPEC],
+            in_specs=[SMEM_SPEC] * 3 + [VMEM_SPEC] * 2,
             out_specs=VMEM_SPEC,
             scratch_shapes=thin4,
-            compiler_params=params(10),
+            compiler_params=params(14),
             cost_estimate=pl.CostEstimate(flops=200000000000, bytes_accessed=8000000, transcendentals=0),
         )
-        z_own = narrow_own(name="two_own")(s, d, wc, n_own, t2)
+        z_own = narrow_own(name="two_own")(s, d, n_own, t2, w_own)
         marks = jnp.broadcast_to(marks[:, None], (n_loc, LANES))
         dz, bz_prev, bz_next, loss = pl.pallas_call(
             functools.partial(logits_kernel, classes),
@@ -542,7 +547,7 @@
         rz_prev = shift_next(bz_next)
         late_b, _ = lax.optimization_barrier((hid_b, bz_prev))
         hb_prev, hb_next = shift_next(late_b), shift_prev(late_b)
-        dt2_own = narrow_own(name="two_back_own")(d, s, wc, n_own, dz)
+        dt2_own = narrow_own(name="two_back_own")(d, s, n_own, dz, w_own)
         dt2, dy, grad_two = pl.pallas_call(
             hidden_grad_kernel,
             out_shape=[sds((n_loc, LANES), BF16), sds((quad, LANES), F32), sds((f_hid, LANES), F32)],
@@ -556,13 +561,13 @@
         dt1_own = pl.pallas_call(
             wide_own_kernel,
             out_shape=sds((quad, LANES), F32),
-            in_specs=[SMEM_SPEC] * 4 + [VMEM_SPEC],
+            in_specs=[SMEM_SPEC] * 3 + [VMEM_SPEC] * 2,
             out_specs=VMEM_SPEC,
             scratch_shapes=wide4,
-            compiler_params=params(28),
+            compiler_params=params(32),
             cost_estimate=pl.CostEstimate(flops=200000000000, bytes_accessed=8000000, transcendentals=0),
             name="one_back_own",
-        )(d4, s4, wc, n_own, dy)
+        )(d4, s4, n_own, dy, w_own)
         grad_one = pl.pallas_call(
             functools.partial(table_grad_kernel, rows),
             out_shape=sds((256, f_hid), F32),

time: 201 us -> 197 us (0.980)
  Pallas kernels: 148 us -> 139 us
  waiting for transfers between devices: 23.5 us -> 27.7 us
    pallas_call x2, Pallas kernels: 27.1 us -> 22.9 us  [the longest x1 11.5 us: device_step(): dt2_own = narrow_own(name='two_back_own')(d, s, n_own, dz, w_own)]
    pallas_call x1, Pallas kernels: 17.3 us -> 15.1 us  [device_step(): pl.pallas_call(one_own_kernel, out_shape=sds((quad, LANES), F32), in_spec...]
    ppermute x6, waiting for transfers between devices: 17.9 us -> 20.1 us  [shift_next(): return lax.ppermute(a, GRAPH_AXIS, to_next)]
    pallas_call x1, Pallas kernels: 15.5 us -> 13.4 us  [device_step(): pl.pallas_call(wide_own_kernel, out_shape=sds((quad, LANES), F32), in_spe...]
    ppermute x6, waiting for transfers between devices: 5.56 us -> 7.57 us  [shift_prev(): return lax.ppermute(a, GRAPH_AXIS, to_prev)]
  transfers between devices with their start and end apart: 12 -> 12, of which waited for: 3 -> 4; matrix products, arithmetic and copies ran while one was open for 0% -> 1% of each run, Pallas kernels for 43% -> 40%
where the time goes in v6:
time: 197 us
  Pallas kernels  139 us (71%)
  waiting for transfers between devices  27.7 us (14%)
  starting transfers between devices  13.4 us (7%)
  local copies, waits for them, and re-layouts  8.33 us (4%)
  other arithmetic  6.71 us (3%)
    ppermute x6, waiting for transfers between devices, shift_next(): return lax.ppermute(a, GRAPH_AXIS, to_next)  20.1 us
    pallas_call x1, Pallas kernels, device_step(): pl.pallas_call(functools.partial(logits_kernel, classes), out_shape=[sds(...  17.4 us
    pallas_call x1, Pallas kernels, device_step(): pl.pallas_call(functools.partial(reduce_kernel, num_dev), out_shape=[sds(...  16.8 us
    pallas_call x1, Pallas kernels, device_step(): pl.pallas_call(one_halo_kernel, out_shape=[sds((n_loc, f_hid // 2), BF16)...  16.1 us
    pallas_call x1, Pallas kernels, device_step(): pl.pallas_call(functools.partial(table_grad_kernel, rows), out_shape=sds(...  15.7 us
    pallas_call x1, Pallas kernels, device_step(): pl.pallas_call(one_own_kernel, out_shape=sds((quad, LANES), F32), in_spec...  15.1 us
    pallas_call x1, Pallas kernels, device_step(): pl.pallas_call(wide_own_kernel, out_shape=sds((quad, LANES), F32), in_spe...  13.4 us
    ppermute x6, starting transfers between devices, shift_prev(): return lax.ppermute(a, GRAPH_AXIS, to_prev)  13 us
  transfers between devices with their start and end apart: 12, of which 4 were waited for; matrix products, arithmetic and copies ran while one was open for 1% of the time, Pallas kernels for 40%

profile of v6, /device:TPU:0, one launch (start us, length us, event | category | flops | bytes accessed | tf_op | source)
XLA Modules:
  0.0 196.5 jit_solution(14780059970629125470)
XLA Ops:
  3.6 4.2 %select_reduce_fusion = (s32[32,384]{1,0:T(8,128)S(1)}, f32[32,384]{1,0:T(8,128)S(1)}) fusion(f32[32,256]{1,0:T(8,128)S(1)} %reshape.65, s32[32,256]{1,0:T(8,128)S(1)} %get-tuple-element.90, s32[32,256]{1,0:T(8,128)S(1)} %get-tuple-element.91), kind=kLoop, calls=%fused_computation | loop fusion | flops 15704064 | bytes 196608 | tf_op jit(solution)/shard_map/reduce | solution.py:455
  9.4 8.0 %lists.1 = (f32[8,128]{1,0:T(8,128)S(1)}, s32[104,128]{1,0:T(8,128)S(1)}, s32[104,128]{1,0:T(8,128)S(1)}, f32[96,128]{1,0:T(8,128)S(1)}, f32[96,128]{1,0:T(8,128)S(1)}) custom-call(s32[16,128]{1,0:T(8,128)S(1)} %bitcast.21, s32[104,128]{1,0:T(8,128)S(1)} %bitcast.16, f32[96,128]{1,0:T(8,128)S(1)} %reshape_reshape.3.wgt), custom_call_target="tpu_custom_call" | custom-call | tf_op jit(solution)/shard_map/lists/pallas_call | solution.py:476
  17.5 1.4 copy.16.x
  18.9 1.3 pad_add_fusion.1
  20.2 4.7 %halo_rows.1 = (bf16[1024,256]{1,0:T(8,128)(2,1)}, bf16[1024,256]{1,0:T(8,128)(2,1)}) custom-call(s32[2048]{0:T(1024)S(1)} %get-tuple-element.38.ids, bf16[2048,200]{1,0:T(8,128)(2,1)S(1)} %copy.16.x), custom_call_target="tpu_custom_call" | custom-call | tf_op jit(solution)/shard_map/halo_rows/pallas_call | solution.py:488
  25.4 2.2 %collective-permute-start.1 = (bf16[1024,256]{1,0:T(8,128)(2,1)}, bf16[1024,256]{1,0:T(8,128)(2,1)}, u32[]{:S(2)}, u32[]{:S(2)}) collective-permute-start(bf16[1024,256]{1,0:T(8,128)(2,1)} %get-tuple-element.49), channel_id=1, source_target_pairs={{0,7},{1,0},{2,1},{3,2},{4,3},{5,4},{6,5},{7,6}} | collective-permute-start | bytes 1572872 | tf_op jit(solution)/shard_map/ppermute | solution.py:434
  27.8 1.1 broadcast_in_dim.61.w
  29.0 15.1 %one_own.1.y_own = f32[8192,128]{1,0:T(8,128)S(1)} custom-call(s32[12288]{0:T(1024)S(1)} %get-tuple-element.43.s4.to, s32[12288]{0:T(1024)S(1)} %get-tuple-element.77.d4.frm, s32[32]{0:T(128)S(1)} %get-tuple-element.89.cnt, bf16[2048,200]{1,0:T(8,128)(2,1)S(1)} %copy.16.x, bf16[200,512]{1,0:T(8,128)(2,1)S(1)} %convert_element_type.30.w1, ...), custom_call_target="tpu_custom_call" | custom-call | flops 199999995904 | bytes 8000000 | tf_op jit(solution)/shard_map/one_own/pallas_call | solution.py:503
  44.2 16.1 %one_halo.1 = (bf16[2048,256]{1,0:T(8,128)(2,1)}, bf16[2048,256]{1,0:T(8,128)(2,1)}, f32[2048,128]{1,0:T(8,128)S(1)}, bf16[1024,128]{1,0:T(8,128)(2,1)}, bf16[1024,128]{1,0:T(8,128)(2,1)}) custom-call(s32[12288]{0:T(1024)S(1)} %get-tuple-element.43.s4.to, s32[12288]{0:T(1024)S(1)} %get-tuple-element.77.d4.frm, f32[12288]{0:T(1024)S(1)} %reshape.68.w, ...), custom_call_target="tpu_custom_call" | custom-call | tf_op jit(solution)/shard_map/one_halo/pallas_call | solution.py:513
  60.3 1.4 collective-permute-start.7
  61.6 2.7 %collective-permute-start.3 = (bf16[1024,128]{1,0:T(8,128)(2,1)}, bf16[1024,128]{1,0:T(8,128)(2,1)}, u32[]{:S(2)}, u32[]{:S(2)}) collective-permute-start(bf16[1024,128]{1,0:T(8,128)(2,1)} %get-tuple-element.53), channel_id=1, source_target_pairs={{0,7},{1,0},{2,1},{3,2},{4,3},{5,4},{6,5},{7,6}} | collective-permute-start | bytes 786440 | tf_op jit(solution)/shard_map/ppermute | solution.py:434
  64.3 11.5 %two_own.1.z_own = f32[2048,128]{1,0:T(8,128)S(1)} custom-call(s32[12288]{0:T(1024)S(1)} %get-tuple-element.84.frm.s.to, s32[12288]{0:T(1024)S(1)} %get-tuple-element.78.to.d.frm, s32[32]{0:T(128)S(1)} %get-tuple-element.89.cnt, f32[2048,128]{1,0:T(8,128)S(1)} %get-tuple-element.51.table, f32[8192,128]{1,0:T(8,128)S(1)} %broadcast_in_dim.61.w), custom_call_target="tpu_custom_call" | custom-call | flops 199999995904 | bytes 8000000 | tf_op jit(solution)/shard_map/two_own/pallas_call | solution.py:535
  75.8 16.5 %collective-permute-done.2.t_prev = bf16[1024,128]{1,0:T(8,128)(2,1)} collective-permute-done((bf16[1024,128]{1,0:T(8,128)(2,1)}, bf16[1024,128]{1,0:T(8,128)(2,1)}, u32[]{:S(2)}, u32[]{:S(2)}) %collective-permute-start.2) | collective-permute-done | bytes 262176 | tf_op jit(solution)/shard_map/ppermute | solution.py:431
  92.6 17.4 %logits.1 = (f32[2048,128]{1,0:T(8,128)S(1)}, f32[1024,128]{1,0:T(8,128)}, f32[1024,128]{1,0:T(8,128)}, f32[8,128]{1,0:T(8,128)S(1)}) custom-call(s32[12288]{0:T(1024)S(1)} %get-tuple-element.84.frm.s.to, s32[12288]{0:T(1024)S(1)} %get-tuple-element.78.to.d.frm, f32[12288]{0:T(1024)S(1)} %reshape.68.w, s32[32]{0:T(128)S(1)} %get-tuple-element.75.cnt, ...), custom_call_target="tpu_custom_call" | custom-call | tf_op jit(solution)/shard_map/logits/pallas_call | solution.py:537
  109.9 1.2 collective-permute-start.4
  111.1 11.5 %two_back_own.1.own = f32[2048,128]{1,0:T(8,128)S(1)} custom-call(s32[12288]{0:T(1024)S(1)} %get-tuple-element.78.to.d.frm, s32[12288]{0:T(1024)S(1)} %get-tuple-element.84.frm.s.to, s32[32]{0:T(128)S(1)} %get-tuple-element.89.cnt, f32[2048,128]{1,0:T(8,128)S(1)} %get-tuple-element.56.table, f32[8192,128]{1,0:T(8,128)S(1)} %broadcast_in_dim.61.w), custom_call_target="tpu_custom_call" | custom-call | flops 199999995904 | bytes 8000000 | tf_op jit(solution)/shard_map/two_back_own/pallas_call | solution.py:550
  122.6 3.3 %collective-permute-start.8 = (bf16[2048,256]{1,0:T(8,128)(2,1)}, bf16[2048,256]{1,0:T(8,128)(2,1)}, u32[]{:S(2)}, u32[]{:S(2)}) collective-permute-start(bf16[2048,256]{1,0:T(8,128)(2,1)} %get-tuple-element.63.hid_b), channel_id=1, source_target_pairs={{0,7},{1,0},{2,1},{3,2},{4,3},{5,4},{6,5},{7,6}} | collective-permute-start | bytes 3145736 | tf_op jit(solution)/shard_map/ppermute | solution.py:434
  126.2 9.1 %hidden_grad.1 = (bf16[2048,128]{1,0:T(8,128)(2,1)}, f32[8192,128]{1,0:T(8,128)S(1)}, f32[512,128]{1,0:T(8,128)S(1)}) custom-call(s32[2048]{0:T(1024)S(1)} %copy-done.3, f32[2048,128]{1,0:T(8,128)S(1)} %two_back_own.1.own, f32[1024,128]{1,0:T(8,128)} %collective-permute-done.4.ret_next, f32[1024,128]{1,0:T(8,128)} %collective-permute-done.5.ret_prev, ...), custom_call_target="tpu_custom_call" | custom-call | tf_op jit(solution)/shard_map/hidden_grad/pallas_call | solution.py:551
  135.3 2.3 %collective-permute-start.6 = (bf16[2048,128]{1,0:T(8,128)(2,1)}, bf16[2048,128]{1,0:T(8,128)(2,1)}, u32[]{:S(2)}, u32[]{:S(2)}) collective-permute-start(bf16[2048,128]{1,0:T(8,128)(2,1)} %get-tuple-element.62), channel_id=1, source_target_pairs={{0,7},{1,0},{2,1},{3,2},{4,3},{5,4},{6,5},{7,6}} | collective-permute-start | bytes 1572872 | tf_op jit(solution)/shard_map/ppermute | solution.py:434
  137.6 13.4 %one_back_own.1.own = f32[8192,128]{1,0:T(8,128)S(1)} custom-call(s32[12288]{0:T(1024)S(1)} %get-tuple-element.77.d4.frm, s32[12288]{0:T(1024)S(1)} %get-tuple-element.43.s4.to, s32[32]{0:T(128)S(1)} %get-tuple-element.89.cnt, f32[8192,128]{1,0:T(8,128)S(1)} %get-tuple-element.61.table, f32[8192,128]{1,0:T(8,128)S(1)} %broadcast_in_dim.61.w), custom_call_target="tpu_custom_call" | custom-call | flops 199999995904 | bytes 8000000 | tf_op jit(solution)/shard_map/one_back_own/pallas_call | solution.py:561
  151.1 7.6 %collective-permute-done.6.tn = bf16[2048,128]{1,0:T(8,128)(2,1)} collective-permute-done((bf16[2048,128]{1,0:T(8,128)(2,1)}, bf16[2048,128]{1,0:T(8,128)(2,1)}, u32[]{:S(2)}, u32[]{:S(2)}) %collective-permute-start.6) | collective-permute-done | bytes 524320 | tf_op jit(solution)/shard_map/ppermute | solution.py:434
  158.6 3.3 %collective-permute-done.9.tp = bf16[2048,128]{1,0:T(8,128)(2,1)} collective-permute-done((bf16[2048,128]{1,0:T(8,128)(2,1)}, bf16[2048,128]{1,0:T(8,128)(2,1)}, u32[]{:S(2)}, u32[]{:S(2)}) %collective-permute-start.9) | collective-permute-done | bytes 524320 | tf_op jit(solution)/shard_map/ppermute | solution.py:431
  161.9 15.7 %table_grad.1.g1 = f32[256,512]{1,0:T(8,128)S(1)} custom-call(s32[2048]{0:T(1024)S(1)} %copy-done.3, s32[13312]{0:T(1024)S(1)} %bitcast.18, f32[12288]{0:T(1024)S(1)} %bitcast.20, s32[13312]{0:T(1024)S(1)} %bitcast.17, f32[12288]{0:T(1024)S(1)} %bitcast.19, f32[8192,128]{1,0:T(8,128)S(1)} %one_back_own.1.own, bf16[2048,128]{1,0:T(8,128)(2,1)} %collective-permute-done.6.tn, ...), custom_call_target="tpu_custom_call" | custom-call | tf_op jit(solution)/shard_map/table_grad/pallas_call | solution.py:571
  177.6 16.8 %reduce.18 = (f32[256,512]{1,0:T(8,128)S(1)}, f32[512,128]{1,0:T(8,128)S(1)}, f32[8,128]{1,0:T(8,128)S(1)}) custom-call(f32[256,512]{1,0:T(8,128)S(1)} %table_grad.1.g1, f32[512,128]{1,0:T(8,128)S(1)} %get-tuple-element.64.g2, f32[8,128]{1,0:T(8,128)S(1)} %get-tuple-element.65.loss, f32[8,128]{1,0:T(8,128)S(1)} %get-tuple-element.55.count), custom_call_target="tpu_custom_call" | custom-call | tf_op jit(solution)/shard_map/reduce/pallas_call | solution.py:580
  (60 shorter events, 7.9 us)
Async XLA Ops:
  0.6 27.1 %copy-start.6 = (f32[512,107]{0,1:T(8,128)S(1)}, f32[512,107]{0,1:T(8,128)}, u32[]{:S(2)}) copy-start(f32[512,107]{0,1:T(8,128)} %param.11) | copy-start | bytes 657412
  8.7 0.7 copy-start.4
  9.4 19.5 %copy-start.5 = (f32[200,512]{1,0:T(8,128)S(1)}, f32[200,512]{1,0:T(8,128)}, u32[]{:S(2)}) copy-start(f32[200,512]{1,0:T(8,128)} %param.10) | copy-start | bytes 1228804
  20.2 7.4 %copy-start.2 = (s32[2048]{0:T(1024)}, s32[2048]{0:T(1024)S(1)}, u32[]{:S(2)}) copy-start(s32[2048]{0:T(1024)S(1)} %get-tuple-element.38.ids) | copy-start | bytes 24580
  25.0 19.2 %collective-permute-start = (bf16[1024,256]{1,0:T(8,128)(2,1)}, bf16[1024,256]{1,0:T(8,128)(2,1)}, u32[]{:S(2)}, u32[]{:S(2)}) collective-permute-start(bf16[1024,256]{1,0:T(8,128)(2,1)} %get-tuple-element.48), channel_id=1, source_target_pairs={{0,1},{1,2},{2,3},{3,4},{4,5},{5,6},{6,7},{7,0}} | collective-permute-start | bytes 1572872 | tf_op jit(solution)/shard_map/ppermute | solution.py:431
  25.4 18.8 %collective-permute-start.1 = (bf16[1024,256]{1,0:T(8,128)(2,1)}, bf16[1024,256]{1,0:T(8,128)(2,1)}, u32[]{:S(2)}, u32[]{:S(2)}) collective-permute-start(bf16[1024,256]{1,0:T(8,128)(2,1)} %get-tuple-element.49), channel_id=1, source_target_pairs={{0,7},{1,0},{2,1},{3,2},{4,3},{5,4},{6,5},{7,6}} | collective-permute-start | bytes 1572872 | tf_op jit(solution)/shard_map/ppermute | solution.py:434
  27.8 98.4 %copy-start = (bf16[128,512]{1,0:T(8,128)(2,1)}, bf16[128,512]{1,0:T(8,128)(2,1)S(1)}, u32[]{:S(2)}) copy-start(bf16[128,512]{1,0:T(8,128)(2,1)S(1)} %pad.4.w2t) | copy-start | bytes 393220
  29.0 15.2 %copy-start.3 = (s32[2048]{0:T(1024)S(1)}, s32[2048]{0:T(1024)}, u32[]{:S(2)}) copy-start(s32[2048]{0:T(1024)} %copy-done.2) | copy-start | bytes 24580
  60.3 77.3 %collective-permute-start.7 = (bf16[2048,256]{1,0:T(8,128)(2,1)}, bf16[2048,256]{1,0:T(8,128)(2,1)}, u32[]{:S(2)}, u32[]{:S(2)}) collective-permute-start(bf16[2048,256]{1,0:T(8,128)(2,1)} %get-tuple-element.59.hid_a), channel_id=1, source_target_pairs={{0,7},{1,0},{2,1},{3,2},{4,3},{5,4},{6,5},{7,6}} | collective-permute-start | bytes 3145736 | tf_op jit(solution)/shard_map/ppermute | solution.py:434
  61.6 89.4 %collective-permute-start.10 = (bf16[2048,256]{1,0:T(8,128)(2,1)}, bf16[2048,256]{1,0:T(8,128)(2,1)}, u32[]{:S(2)}, u32[]{:S(2)}) collective-permute-start(bf16[2048,256]{1,0:T(8,128)(2,1)} %get-tuple-element.59.hid_a), channel_id=1, source_target_pairs={{0,1},{1,2},{2,3},{3,4},{4,5},{5,6},{6,7},{7,0}} | collective-permute-start | bytes 3145736 | tf_op jit(solution)/shard_map/ppermute | solution.py:431
  61.6 30.6 %collective-permute-start.2 = (bf16[1024,128]{1,0:T(8,128)(2,1)}, bf16[1024,128]{1,0:T(8,128)(2,1)}, u32[]{:S(2)}, u32[]{:S(2)}) collective-permute-start(bf16[1024,128]{1,0:T(8,128)(2,1)} %get-tuple-element.52), channel_id=1, source_target_pairs={{0,1},{1,2},{2,3},{3,4},{4,5},{5,6},{6,7},{7,0}} | collective-permute-start | bytes 786440 | tf_op jit(solution)/shard_map/ppermute | solution.py:431
  61.6 30.6 %collective-permute-start.3 = (bf16[1024,128]{1,0:T(8,128)(2,1)}, bf16[1024,128]{1,0:T(8,128)(2,1)}, u32[]{:S(2)}, u32[]{:S(2)}) collective-permute-start(bf16[1024,128]{1,0:T(8,128)(2,1)} %get-tuple-element.53), channel_id=1, source_target_pairs={{0,7},{1,0},{2,1},{3,2},{4,3},{5,4},{6,5},{7,6}} | collective-permute-start | bytes 786440 | tf_op jit(solution)/shard_map/ppermute | solution.py:434
  64.3 27.9 %copy-start.7 = (s32[2048]{0:T(1024)S(1)}, s32[2048]{0:T(1024)}, u32[]{:S(2)}) copy-start(s32[2048]{0:T(1024)} %get-tuple-element.54) | copy-start | bytes 24580
  109.9 15.9 %collective-permute-start.4 = (f32[1024,128]{1,0:T(8,128)}, f32[1024,128]{1,0:T(8,128)}, u32[]{:S(2)}, u32[]{:S(2)}) collective-permute-start(f32[1024,128]{1,0:T(8,128)} %get-tuple-element.57), channel_id=1, source_target_pairs={{0,7},{1,0},{2,1},{3,2},{4,3},{5,4},{6,5},{7,6}} | collective-permute-start | bytes 1572872 | tf_op jit(solution)/shard_map/ppermute | solution.py:434
  111.1 15.1 %collective-permute-start.5 = (f32[1024,128]{1,0:T(8,128)}, f32[1024,128]{1,0:T(8,128)}, u32[]{:S(2)}, u32[]{:S(2)}) collective-permute-start(f32[1024,128]{1,0:T(8,128)} %get-tuple-element.58), channel_id=1, source_target_pairs={{0,1},{1,2},{2,3},{3,4},{4,5},{5,6},{6,7},{7,0}} | collective-permute-start | bytes 1572872 | tf_op jit(solution)/shard_map/ppermute | solution.py:431
  122.6 36.0 %collective-permute-start.8 = (bf16[2048,256]{1,0:T(8,128)(2,1)}, bf16[2048,256]{1,0:T(8,128)(2,1)}, u32[]{:S(2)}, u32[]{:S(2)}) collective-permute-start(bf16[2048,256]{1,0:T(8,128)(2,1)} %get-tuple-element.63.hid_b), channel_id=1, source_target_pairs={{0,7},{1,0},{2,1},{3,2},{4,3},{5,4},{6,5},{7,6}} | collective-permute-start | bytes 3145736 | tf_op jit(solution)/shard_map/ppermute | solution.py:434
  125.9 36.0 %collective-permute-start.11 = (bf16[2048,256]{1,0:T(8,128)(2,1)}, bf16[2048,256]{1,0:T(8,128)(2,1)}, u32[]{:S(2)}, u32[]{:S(2)}) collective-permute-start(bf16[2048,256]{1,0:T(8,128)(2,1)} %get-tuple-element.63.hid_b), channel_id=1, source_target_pairs={{0,1},{1,2},{2,3},{3,4},{4,5},{5,6},{6,7},{7,0}} | collective-permute-start | bytes 3145736 | tf_op jit(solution)/shard_map/ppermute | solution.py:431
  135.3 23.3 %collective-permute-start.6 = (bf16[2048,128]{1,0:T(8,128)(2,1)}, bf16[2048,128]{1,0:T(8,128)(2,1)}, u32[]{:S(2)}, u32[]{:S(2)}) collective-permute-start(bf16[2048,128]{1,0:T(8,128)(2,1)} %get-tuple-element.62), channel_id=1, source_target_pairs={{0,7},{1,0},{2,1},{3,2},{4,3},{5,4},{6,5},{7,6}} | collective-permute-start | bytes 1572872 | tf_op jit(solution)/shard_map/ppermute | solution.py:434
  137.6 24.3 %collective-permute-start.9 = (bf16[2048,128]{1,0:T(8,128)(2,1)}, bf16[2048,128]{1,0:T(8,128)(2,1)}, u32[]{:S(2)}, u32[]{:S(2)}) collective-permute-start(bf16[2048,128]{1,0:T(8,128)(2,1)} %get-tuple-element.62), channel_id=1, source_target_pairs={{0,1},{1,2},{2,3},{3,4},{4,5},{5,6},{6,7},{7,0}} | collective-permute-start | bytes 1572872 | tf_op jit(solution)/shard_map/ppermute | solution.py:431
  137.6 24.3 %copy-start.1 = (bf16[128,512]{1,0:T(8,128)(2,1)S(1)}, bf16[128,512]{1,0:T(8,128)(2,1)}, u32[]{:S(2)}) copy-start(bf16[128,512]{1,0:T(8,128)(2,1)} %copy-done) | copy-start | bytes 393220

commit v7 on v6

--- a/solution.py
+++ b/solution.py
@@ -129,7 +129,7 @@
     return copy
 
 
-def lists_kernel(num_dev, mask, code, wgt, count, code_prev, code_next, w_prev, w_next, part, slots, send_sem, recv_sem, lsend, lrecv):
+def lists_kernel(num_dev, mask, code, wgt, x, w1, count, code_prev, code_next, w_prev, w_next, table, part, slots, send_sem, recv_sem, lsend, lrecv):
     ones = jnp.sum(jnp.sum(mask[...].astype(F32), axis=1, keepdims=True), axis=0, keepdims=True)
     part[...] = jnp.broadcast_to(ones, part.shape)
     me = lax.axis_index(GRAPH_AXIS)
@@ -142,6 +142,12 @@
     copies.append(push(code, code_next, lsend.at[1], lrecv.at[1], pred))
     copies.append(push(wgt, w_prev, lsend.at[2], lrecv.at[2], succ))
     copies.append(push(wgt, w_next, lsend.at[3], lrecv.at[3], pred))
+
+    def put(i):
+        t = jnp.dot(x[rows_at(i), :], w1[...], preferred_element_type=F32)
+        spread(table, i * BLOCK, t.astype(BF16).astype(F32))
+
+    loop(x.shape[0] // BLOCK, put)
     for copy in copies:
         copy.wait()
     total = part[...]
@@ -163,22 +169,10 @@
     half = to_next.shape[0]
 
     def take(i):
-        to_next[rows_at(i), :] = unspread(picked, i * BLOCK, BLOCK, 2).astype(BF16)
-        to_prev[rows_at(i), :] = unspread(picked, half + i * BLOCK, BLOCK, 2).astype(BF16)
+        to_prev[rows_at(i), :] = unspread(picked, i * BLOCK, BLOCK, 2).astype(BF16)
+        to_next[rows_at(i), :] = unspread(picked, half + i * BLOCK, BLOCK, 2).astype(BF16)
 
     loop(half // BLOCK, take)
-
-
-def one_own_kernel(s4, d4, cnt, x, w1, w, y, table, *accs):
-    zero_rows(accs)
-
-    def put(i):
-        t = jnp.dot(x[rows_at(i), :], w1[...], preferred_element_type=F32)
-        spread(table, i * BLOCK, t.astype(BF16).astype(F32))
-
-    loop(x.shape[0] // BLOCK, put)
-    edge_pass(s4, d4, w, cnt, table, accs, 4, 32, False)
-    sum_rows(y, accs)
 
 
 def one_halo_kernel(s4, d4, w, cnt, ids, y_own, x_prev, x_next, w1, w2t, hid_a, hid_b, t2, to_next, to_prev, table, picked, *accs):
@@ -207,8 +201,8 @@
     gather_pass(ids, t2, picked, 1)
 
     def take(i):
-        to_next[rows_at(i), :] = picked[rows_at(i), :].astype(BF16)
-        to_prev[rows_at(i), :] = picked[rows_at(i, half), :].astype(BF16)
+        to_prev[rows_at(i), :] = picked[rows_at(i), :].astype(BF16)
+        to_next[rows_at(i), :] = picked[rows_at(i, half), :].astype(BF16)
 
     loop(half // BLOCK, take)
 
@@ -286,8 +280,8 @@
 def hidden_grad_kernel(ids, own, ret_next, ret_prev, hid_a, hid_b, w2t, dt2, dy, g2, *accs):
     n_loc, half = own.shape[0], ret_next.shape[0]
     zero_rows(accs)
-    scatter_pass(ids.at[pl.ds(0, half)], ret_next, accs, 1, 8)
-    scatter_pass(ids.at[pl.ds(half, half)], ret_prev, accs, 1, 8)
+    scatter_pass(ids.at[pl.ds(half, half)], ret_next, accs, 1, 8)
+    scatter_pass(ids.at[pl.ds(0, half)], ret_prev, accs, 1, 8)
     g2[...] = jnp.zeros_like(g2)
 
     def fold(i):
@@ -311,6 +305,8 @@
     tally = rows * SLOT
     n_loc = ids.shape[0]
     shift = n_loc.bit_length() - 1
+    half = n_loc // 2
+    owners = ids.at[pl.ds(0 if far else half, half)]
 
     def row(r):
         first = SLOT - 16 - (code_ref[tally + 2 * rows + r] if far else 0)
@@ -324,7 +320,7 @@
                 code = codes[u]
                 frm = lax.shift_right_logical(code, shift) * 4
                 val = table[pl.ds(pl.multiple_of(frm, 4), 4), :] * wgt[u]
-                at = pl.ds(pl.multiple_of(ids[code & (n_loc - 1)] * 4, 4), 4)
+                at = pl.ds(pl.multiple_of(owners[code & (half - 1)] * 4, 4), 4)
                 acc[at, :] = acc[at, :] + val
 
         loop(lax.shift_right_logical(edges + 15, 4), body)
@@ -353,73 +349,68 @@
         total = unspread(own, i * BLOCK, BLOCK, 4)
         for acc in accs:
             total = total + unspread(acc, i * BLOCK, BLOCK, 4)
-        g1[:x.shape[1], :] += lax.dot_general(x[rows_at(i), :], total.astype(BF16), CONTRACT_ROWS, preferred_element_type=F32)
+        g1[...] += lax.dot_general(x[rows_at(i), :], total.astype(BF16), CONTRACT_ROWS, preferred_element_type=F32)
 
     loop(x.shape[0] // BLOCK, fold)
 
 
-def reduce_kernel(num_dev, g1, g2, loss, count, o1, o2, lo, r1, r2, s1, s2, q1, q2, lslots, sem_s, sem_r, lsem_s, lsem_r):
+def reduce_kernel(num_dev, g1, g2, loss, count, o1, o2, lo, pack, total, other_half, sums, parts, lslots, sem_s, sem_r, lsem_s, lsem_r):
+    rows, tiles = g1.shape[0], g1.shape[1] // LANES
+    base = rows * tiles
+    for c in range(tiles):
+        pack[c * rows:(c + 1) * rows, :] = g1[:, c * LANES:(c + 1) * LANES]
+    end = base + g2.shape[0]
+    pack[base:end, :] = g2[...]
+    pack[end:, :] = jnp.zeros((pack.shape[0] - end, LANES), F32)
     me = lax.axis_index(GRAPH_AXIS)
     core = lax.rem(me, 2)
     chip = me // 2
     mate = me + 1 - 2 * core
-    h1, h2 = g1.shape[0] // 2, g2.shape[0] // 2
-    e1, e2 = h1 // 4, h2 // 4
+    half = pack.shape[0] // 2
+    part = half // 4
     enter(me, num_dev)
-    other = 1 - core
-    pair = [
-        push(g1.at[pl.ds(pl.multiple_of(other * h1, h1), h1)], r1, sem_s.at[0], sem_r.at[0], mate),
-        push(g2.at[pl.ds(pl.multiple_of(other * h2, h2), h2)], r2, sem_s.at[1], sem_r.at[1], mate),
-    ]
+
+    def piece(owner):
+        return pl.ds(pl.multiple_of(core * half + owner * part, 8), part)
+
+    pair = push(pack.at[pl.ds(pl.multiple_of((1 - core) * half, 8), half)], other_half, sem_s.at[0], sem_r.at[0], mate)
     scalar = []
     for step in range(1, num_dev):
         scalar.append(push(loss, lslots.at[step - 1], lsem_s.at[step - 1], lsem_r.at[step - 1], lax.rem(me + step, num_dev)))
-    for copy in pair:
-        copy.wait()
-    s1[...] = g1[pl.ds(pl.multiple_of(core * h1, h1), h1), :] + r1[...]
-    s2[...] = g2[pl.ds(pl.multiple_of(core * h2, h2), h2), :] + r2[...]
+    pair.wait()
+    sums[...] = pack[pl.ds(pl.multiple_of(core * half, 8), half), :] + other_half[...]
     spreads = []
     for step in range(1, 4):
         far = lax.rem(chip + step, 4)
-        dev = far * 2 + core
-        k = 2 * step
-        spreads.append(push(s1.at[pl.ds(pl.multiple_of(far * e1, e1), e1)], q1.at[step - 1], sem_s.at[k], sem_r.at[k], dev))
-        spreads.append(push(s2.at[pl.ds(pl.multiple_of(far * e2, e2), e2)], q2.at[step - 1], sem_s.at[k + 1], sem_r.at[k + 1], dev))
+        at = pl.ds(pl.multiple_of(far * part, 8), part)
+        spreads.append(push(sums.at[at], parts.at[step - 1], sem_s.at[step], sem_r.at[step], far * 2 + core))
     for copy in spreads:
         copy.wait()
-    mine1 = pl.ds(pl.multiple_of(core * h1 + chip * e1, e1), e1)
-    mine2 = pl.ds(pl.multiple_of(core * h2 + chip * e2, e2), e2)
-    t1 = s1[pl.ds(pl.multiple_of(chip * e1, e1), e1), :]
-    t2 = s2[pl.ds(pl.multiple_of(chip * e2, e2), e2), :]
+    mine = sums[pl.ds(pl.multiple_of(chip * part, 8), part), :]
     for step in range(3):
-        t1 = t1 + q1[step]
-        t2 = t2 + q2[step]
-    o1[mine1, :] = t1
-    o2[mine2, :] = t2
+        mine = mine + parts[step]
+    total[piece(chip), :] = mine
     gathers = []
     for step in range(1, 4):
         dev = lax.rem(chip + step, 4) * 2 + core
-        k = 6 + 2 * step
-        gathers.append((push(o1.at[mine1], o1.at[mine1], sem_s.at[k], sem_r.at[k], dev), push(o2.at[mine2], o2.at[mine2], sem_s.at[k + 1], sem_r.at[k + 1], dev)))
-    tails = [push(o1.at[mine1], o1.at[mine1], sem_s.at[14], sem_r.at[14], mate), push(o2.at[mine2], o2.at[mine2], sem_s.at[15], sem_r.at[15], mate)]
+        gathers.append(push(total.at[piece(chip)], total.at[piece(chip)], sem_s.at[3 + step], sem_r.at[3 + step], dev))
+    tails = [push(total.at[piece(chip)], total.at[piece(chip)], sem_s.at[7], sem_r.at[7], mate)]
     for step in range(1, 4):
         near = lax.rem(chip + 4 - step, 4)
-        at1 = pl.ds(pl.multiple_of(core * h1 + near * e1, e1), e1)
-        at2 = pl.ds(pl.multiple_of(core * h2 + near * e2, e2), e2)
-        for copy in gathers[step - 1]:
-            copy.wait()
-        k = 14 + 2 * step
-        tails.append(push(o1.at[at1], o1.at[at1], sem_s.at[k], sem_r.at[k], mate))
-        tails.append(push(o2.at[at2], o2.at[at2], sem_s.at[k + 1], sem_r.at[k + 1], mate))
+        gathers[step - 1].wait()
+        tails.append(push(total.at[piece(near)], total.at[piece(near)], sem_s.at[7 + step], sem_r.at[7 + step], mate))
     for copy in scalar:
         copy.wait()
-    total = loss[...]
+    lsum = loss[...]
     for step in range(num_dev - 1):
-        total = total + lslots[step]
-    total = jnp.sum(jnp.sum(total, axis=1, keepdims=True), axis=0, keepdims=True)
-    lo[...] = total / count[...]
+        lsum = lsum + lslots[step]
+    lsum = jnp.sum(jnp.sum(lsum, axis=1, keepdims=True), axis=0, keepdims=True)
+    lo[...] = lsum / count[...]
     for copy in tails:
         copy.wait()
+    for c in range(tiles):
+        o1[:, c * LANES:(c + 1) * LANES] = total[c * rows:(c + 1) * rows, :]
+    o2[...] = total[base:end, :]
 
 
 def solution(mesh):
@@ -465,7 +456,7 @@
         x = node_feats
         w1 = w_one.astype(BF16)
         w2t = jnp.pad(w_two.T.astype(BF16), ((0, LANES - classes), (0, 0)))
-        ids = jnp.concatenate([send_rows[1], send_rows[0]])
+        ids = send_rows.reshape(-1)
         code, wc, n_own, n_hal, n_near, n_far, skip = compact(edge_src, edge_dst, edge_w, n_loc, halo)
         rows = n_own.shape[0]
         slots = code.size // LANES
@@ -473,15 +464,15 @@
         code, wc = code.reshape(-1), wc.reshape(-1)
         tally = jnp.concatenate([n_near, n_far, skip, jnp.zeros((8 * LANES - 3 * rows,), jnp.int32)])
         lists = jnp.concatenate([code, tally]).reshape(slots + 8, LANES)
-        count, code_prev, code_next, w_prev, w_next = pl.pallas_call(
+        count, code_prev, code_next, w_prev, w_next, t1 = pl.pallas_call(
             functools.partial(lists_kernel, num_dev),
-            out_shape=[sds((8, LANES), F32)] + [sds((slots + 8, LANES), jnp.int32)] * 2 + [sds((slots, LANES), F32)] * 2,
-            in_specs=[VMEM_SPEC] * 3,
-            out_specs=[VMEM_SPEC] * 5,
+            out_shape=[sds((8, LANES), F32)] + [sds((slots + 8, LANES), jnp.int32)] * 2 + [sds((slots, LANES), F32)] * 2 + [sds((quad, LANES), F32)],
+            in_specs=[VMEM_SPEC] * 5,
+            out_specs=[VMEM_SPEC] * 6,
             scratch_shapes=[pltpu.VMEM((8, LANES), F32), pltpu.VMEM((num_dev - 1, 8, LANES), F32)] + [pltpu.SemaphoreType.DMA((n,)) for n in (num_dev - 1, num_dev - 1, 4, 4)],
-            compiler_params=params(1, collective_id=0, has_side_effects=True),
+            compiler_params=params(8, collective_id=0, has_side_effects=True),
             name="lists",
-        )(label_mask.reshape(-1, LANES), lists, wc.reshape(slots, LANES))
+        )(label_mask.reshape(-1, LANES), lists, wc.reshape(slots, LANES), x, w1)
         s, d = code % n_loc, code // n_loc
         s4, d4 = s * 4, d * 4
         count, x = lax.optimization_barrier((count, x))
@@ -500,16 +491,17 @@
         thin4 = [pltpu.VMEM((n_loc, LANES), F32)] * 4
         marks = jnp.where(label_mask == 1, labels, -1)
         s4, w2t, marks, ids, w_own, wc = lax.optimization_barrier((s4, w2t, marks, ids, w_own, wc))
-        y_own = pl.pallas_call(
-            one_own_kernel,
+        wide_own = functools.partial(
+            pl.pallas_call,
+            wide_own_kernel,
             out_shape=sds((quad, LANES), F32),
-            in_specs=[SMEM_SPEC] * 3 + [VMEM_SPEC] * 3,
+            in_specs=[SMEM_SPEC] * 3 + [VMEM_SPEC] * 2,
             out_specs=VMEM_SPEC,
-            scratch_shapes=[pltpu.VMEM((quad, LANES), F32)] + wide4,
-            compiler_params=params(32),
+            scratch_shapes=wide4,
+            compiler_params=params(28),
             cost_estimate=pl.CostEstimate(flops=200000000000, bytes_accessed=8000000, transcendentals=0),
-            name="one_own",
-        )(s4, d4, n_own, x, w1, w_own)
+        )
+        y_own = wide_own(name="one_own")(s4, d4, n_own, t1, w_own)
         hid_a, hid_b, t2, t_next, t_prev = pl.pallas_call(
             one_halo_kernel,
             out_shape=[sds((n_loc, f_hid // 2), BF16)] * 2 + [sds((n_loc, LANES), F32), sds((halo, LANES), BF16), sds((halo, LANES), BF16)],
@@ -558,42 +550,32 @@
             name="hidden_grad",
         )(ids, dt2_own, rz_next, rz_prev, hid_a, hid_b, w2t)
         dt_prev, dt_next = shift_next(dt2), shift_prev(dt2)
-        dt1_own = pl.pallas_call(
-            wide_own_kernel,
-            out_shape=sds((quad, LANES), F32),
-            in_specs=[SMEM_SPEC] * 3 + [VMEM_SPEC] * 2,
-            out_specs=VMEM_SPEC,
-            scratch_shapes=wide4,
-            compiler_params=params(32),
-            cost_estimate=pl.CostEstimate(flops=200000000000, bytes_accessed=8000000, transcendentals=0),
-            name="one_back_own",
-        )(d4, s4, n_own, dy, w_own)
+        dt1_own = wide_own(name="one_back_own")(d4, s4, n_own, dy, w_own)
         grad_one = pl.pallas_call(
             functools.partial(table_grad_kernel, rows),
-            out_shape=sds((256, f_hid), F32),
+            out_shape=sds((f_in, f_hid), F32),
             in_specs=[SMEM_SPEC] * 5 + [VMEM_SPEC] * 9,
             out_specs=VMEM_SPEC,
             scratch_shapes=[pltpu.VMEM((quad, LANES), F32)] + wide4,
             compiler_params=params(36),
             name="table_grad",
         )(ids, code_next.reshape(-1), w_next.reshape(-1), code_prev.reshape(-1), w_prev.reshape(-1), dt1_own, dt_next, ha_next, hb_next, dt_prev, ha_prev, hb_prev, w2t, x)
+        pack_rows = f_in * f_hid // LANES + f_hid
+        pack_rows += -pack_rows % 64
         grad_one, grad_two, loss = pl.pallas_call(
             functools.partial(reduce_kernel, num_dev),
-            out_shape=[sds((256, f_hid), F32), sds((f_hid, LANES), F32), sds((8, LANES), F32)],
+            out_shape=[sds((f_in, f_hid), F32), sds((f_hid, LANES), F32), sds((8, LANES), F32)],
             in_specs=[VMEM_SPEC] * 4,
             out_specs=[VMEM_SPEC] * 3,
             scratch_shapes=[
-                pltpu.VMEM((128, f_hid), F32), pltpu.VMEM((f_hid // 2, LANES), F32),
-                pltpu.VMEM((128, f_hid), F32), pltpu.VMEM((f_hid // 2, LANES), F32),
-                pltpu.VMEM((3, 32, f_hid), F32), pltpu.VMEM((3, f_hid // 8, LANES), F32),
-                pltpu.VMEM((num_dev - 1, 8, LANES), F32),
-                pltpu.SemaphoreType.DMA((22,)), pltpu.SemaphoreType.DMA((22,)),
-                pltpu.SemaphoreType.DMA((num_dev - 1,)), pltpu.SemaphoreType.DMA((num_dev - 1,)),
-            ],
+                pltpu.VMEM((pack_rows, LANES), F32), pltpu.VMEM((pack_rows, LANES), F32),
+                pltpu.VMEM((pack_rows // 2, LANES), F32), pltpu.VMEM((pack_rows // 2, LANES), F32),
+                pltpu.VMEM((3, pack_rows // 8, LANES), F32), pltpu.VMEM((num_dev - 1, 8, LANES), F32),
+            ] + [pltpu.SemaphoreType.DMA((n,)) for n in (11, 11, num_dev - 1, num_dev - 1)],
             compiler_params=params(8, collective_id=1, has_side_effects=True),
             name="reduce",
         )(grad_one, grad_two, loss, count)
-        return loss[0, 0], grad_one[:f_in], grad_two[:, :classes]
+        return loss[0, 0], grad_one, grad_two[:, :classes]
 
     row_spec = P(GRAPH_AXIS)
     return jax.shard_map(device_step, mesh=mesh, in_specs=(row_spec, P(), P(), row_spec, row_spec, row_spec, row_spec, row_spec, row_spec), out_specs=(P(), P(), P()), check_vma=False)

time: 197 us -> 197 us (level)
  local copies, waits for them, and re-layouts: 8.33 us -> 11 us
  Pallas kernels: 139 us -> 137 us
    unnamed x19 -> x22, local copies, waits for them, and re-layouts: 1.58 us -> 6.75 us
  transfers between devices with their start and end apart: 12 -> 12, of which waited for: 4 -> 4; matrix products, arithmetic and copies ran while one was open for 1% -> 1% of each run, Pallas kernels for 40% -> 39%
where the time goes in v7:
time: 197 us
  Pallas kernels  137 us (70%)
  waiting for transfers between devices  27.6 us (14%)
  starting transfers between devices  13.4 us (7%)
  local copies, waits for them, and re-layouts  11 us (6%)
  other arithmetic  7 us (4%)
    ppermute x6, waiting for transfers between devices, shift_next(): return lax.ppermute(a, GRAPH_AXIS, to_next)  20.1 us
    pallas_call x1, Pallas kernels, device_step(): pl.pallas_call(functools.partial(logits_kernel, classes), out_shape=[sds(...  17.5 us
    pallas_call x1, Pallas kernels, device_step(): pl.pallas_call(one_halo_kernel, out_shape=[sds((n_loc, f_hid // 2), BF16)...  16.1 us
    pallas_call x1, Pallas kernels, device_step(): pl.pallas_call(functools.partial(table_grad_kernel, rows), out_shape=sds(...  15.8 us
    pallas_call x1, Pallas kernels, device_step(): pl.pallas_call(functools.partial(reduce_kernel, num_dev), out_shape=[sds(...  15.5 us
    pallas_call x1, Pallas kernels, device_step(): dt1_own = wide_own(name='one_back_own')(d4, s4, n_own, dy, w_own)  13.5 us
    pallas_call x1, Pallas kernels, device_step(): y_own = wide_own(name='one_own')(s4, d4, n_own, t1, w_own)  13.5 us
    ppermute x6, starting transfers between devices, shift_prev(): return lax.ppermute(a, GRAPH_AXIS, to_prev)  12.9 us
  transfers between devices with their start and end apart: 12, of which 4 were waited for; matrix products, arithmetic and copies ran while one was open for 1% of the time, Pallas kernels for 39%

profile of v7, /device:TPU:0, one launch (start us, length us, event | category | flops | bytes accessed | tf_op | source)
XLA Modules:
  0.0 196.7 jit_solution(13783438597153747760)
XLA Ops:
  3.6 4.2 %select_reduce_fusion = (s32[32,384]{1,0:T(8,128)S(1)}, f32[32,384]{1,0:T(8,128)S(1)}) fusion(f32[32,256]{1,0:T(8,128)S(1)} %reshape.68, s32[32,256]{1,0:T(8,128)S(1)} %get-tuple-element.90, s32[32,256]{1,0:T(8,128)S(1)} %get-tuple-element.91), kind=kLoop, calls=%fused_computation | loop fusion | flops 15704064 | bytes 196608 | tf_op jit(solution)/shard_map/reduce | solution.py:446
  8.6 1.4 copy.16.x
  11.9 8.0 %lists.1 = (f32[8,128]{1,0:T(8,128)S(1)}, s32[104,128]{1,0:T(8,128)S(1)}, s32[104,128]{1,0:T(8,128)S(1)}, f32[96,128]{1,0:T(8,128)S(1)}, f32[96,128]{1,0:T(8,128)S(1)}, /*index=5*/f32[8192,128]{1,0:T(8,128)S(1)}) custom-call(s32[16,128]{1,0:T(8,128)S(1)} %bitcast.27, s32[104,128]{1,0:T(8,128)S(1)} %bitcast.18, f32[96,128]{1,0:T(8,128)S(1)} %reshape_reshape.3.wgt, ...), custom_call_target="tpu_custom_call" | custom-call | tf_op jit(solution)/shard_map/lists/pallas_call | solution.py:467
  19.9 1.9 copy-done.2
  22.4 4.7 %halo_rows.1 = (bf16[1024,256]{1,0:T(8,128)(2,1)}, bf16[1024,256]{1,0:T(8,128)(2,1)}) custom-call(s32[2048]{0:T(1024)S(1)} %bitcast.19, bf16[2048,200]{1,0:T(8,128)(2,1)S(1)} %copy.17.x), custom_call_target="tpu_custom_call" | custom-call | tf_op jit(solution)/shard_map/halo_rows/pallas_call | solution.py:479
  27.5 2.2 %collective-permute-start.1 = (bf16[1024,256]{1,0:T(8,128)(2,1)}, bf16[1024,256]{1,0:T(8,128)(2,1)}, u32[]{:S(2)}, u32[]{:S(2)}) collective-permute-start(bf16[1024,256]{1,0:T(8,128)(2,1)} %get-tuple-element.51), channel_id=1, source_target_pairs={{0,7},{1,0},{2,1},{3,2},{4,3},{5,4},{6,5},{7,6}} | collective-permute-start | bytes 1572872 | tf_op jit(solution)/shard_map/ppermute | solution.py:425
  30.5 1.1 broadcast_in_dim.61.w
  32.0 13.5 %one_own.1.y_own = f32[8192,128]{1,0:T(8,128)S(1)} custom-call(s32[12288]{0:T(1024)S(1)} %get-tuple-element.44.frm.s4.to, s32[12288]{0:T(1024)S(1)} %get-tuple-element.79.to.d4.frm, s32[32]{0:T(128)S(1)} %get-tuple-element.89.cnt, f32[8192,128]{1,0:T(8,128)S(1)} %copy-done.3, f32[8192,128]{1,0:T(8,128)S(1)} %broadcast_in_dim.61.w), custom_call_target="tpu_custom_call" | custom-call | flops 199999995904 | bytes 8000000 | tf_op jit(solution)/shard_map/one_own/pallas_call | solution.py:504
  45.5 16.1 %one_halo.1 = (bf16[2048,256]{1,0:T(8,128)(2,1)}, bf16[2048,256]{1,0:T(8,128)(2,1)}, f32[2048,128]{1,0:T(8,128)S(1)}, bf16[1024,128]{1,0:T(8,128)(2,1)}, bf16[1024,128]{1,0:T(8,128)(2,1)}) custom-call(s32[12288]{0:T(1024)S(1)} %get-tuple-element.44.frm.s4.to, s32[12288]{0:T(1024)S(1)} %get-tuple-element.79.to.d4.frm, f32[12288]{0:T(1024)S(1)} %reshape.72.w, ...), custom_call_target="tpu_custom_call" | custom-call | tf_op jit(solution)/shard_map/one_halo/pallas_call | solution.py:505
  61.6 1.4 collective-permute-start.7
  63.0 2.7 %collective-permute-start.3 = (bf16[1024,128]{1,0:T(8,128)(2,1)}, bf16[1024,128]{1,0:T(8,128)(2,1)}, u32[]{:S(2)}, u32[]{:S(2)}) collective-permute-start(bf16[1024,128]{1,0:T(8,128)(2,1)} %get-tuple-element.55), channel_id=1, source_target_pairs={{0,7},{1,0},{2,1},{3,2},{4,3},{5,4},{6,5},{7,6}} | collective-permute-start | bytes 786440 | tf_op jit(solution)/shard_map/ppermute | solution.py:425
  65.7 11.5 %two_own.1.z_own = f32[2048,128]{1,0:T(8,128)S(1)} custom-call(s32[12288]{0:T(1024)S(1)} %get-tuple-element.86.frm.s.to, s32[12288]{0:T(1024)S(1)} %get-tuple-element.80.to.d.frm, s32[32]{0:T(128)S(1)} %get-tuple-element.89.cnt, f32[2048,128]{1,0:T(8,128)S(1)} %get-tuple-element.53.table, f32[8192,128]{1,0:T(8,128)S(1)} %broadcast_in_dim.61.w), custom_call_target="tpu_custom_call" | custom-call | flops 199999995904 | bytes 8000000 | tf_op jit(solution)/shard_map/two_own/pallas_call | solution.py:527
  77.2 16.4 %collective-permute-done.2.t_prev = bf16[1024,128]{1,0:T(8,128)(2,1)} collective-permute-done((bf16[1024,128]{1,0:T(8,128)(2,1)}, bf16[1024,128]{1,0:T(8,128)(2,1)}, u32[]{:S(2)}, u32[]{:S(2)}) %collective-permute-start.2) | collective-permute-done | bytes 262176 | tf_op jit(solution)/shard_map/ppermute | solution.py:422
  93.9 17.5 %logits.1 = (f32[2048,128]{1,0:T(8,128)S(1)}, f32[1024,128]{1,0:T(8,128)}, f32[1024,128]{1,0:T(8,128)}, f32[8,128]{1,0:T(8,128)S(1)}) custom-call(s32[12288]{0:T(1024)S(1)} %get-tuple-element.86.frm.s.to, s32[12288]{0:T(1024)S(1)} %get-tuple-element.80.to.d.frm, f32[12288]{0:T(1024)S(1)} %reshape.72.w, s32[32]{0:T(128)S(1)} %get-tuple-element.77.cnt, ...), custom_call_target="tpu_custom_call" | custom-call | tf_op jit(solution)/shard_map/logits/pallas_call | solution.py:529
  111.4 1.2 collective-permute-start.4
  112.6 11.5 %two_back_own.1.own = f32[2048,128]{1,0:T(8,128)S(1)} custom-call(s32[12288]{0:T(1024)S(1)} %get-tuple-element.80.to.d.frm, s32[12288]{0:T(1024)S(1)} %get-tuple-element.86.frm.s.to, s32[32]{0:T(128)S(1)} %get-tuple-element.89.cnt, f32[2048,128]{1,0:T(8,128)S(1)} %get-tuple-element.58.table, f32[8192,128]{1,0:T(8,128)S(1)} %broadcast_in_dim.61.w), custom_call_target="tpu_custom_call" | custom-call | flops 199999995904 | bytes 8000000 | tf_op jit(solution)/shard_map/two_back_own/pallas_call | solution.py:542
  124.0 3.3 %collective-permute-start.8 = (bf16[2048,256]{1,0:T(8,128)(2,1)}, bf16[2048,256]{1,0:T(8,128)(2,1)}, u32[]{:S(2)}, u32[]{:S(2)}) collective-permute-start(bf16[2048,256]{1,0:T(8,128)(2,1)} %get-tuple-element.65.hid_b), channel_id=1, source_target_pairs={{0,7},{1,0},{2,1},{3,2},{4,3},{5,4},{6,5},{7,6}} | collective-permute-start | bytes 3145736 | tf_op jit(solution)/shard_map/ppermute | solution.py:425
  127.7 9.1 %hidden_grad.1 = (bf16[2048,128]{1,0:T(8,128)(2,1)}, f32[8192,128]{1,0:T(8,128)S(1)}, f32[512,128]{1,0:T(8,128)S(1)}) custom-call(s32[2048]{0:T(1024)S(1)} %bitcast.21, f32[2048,128]{1,0:T(8,128)S(1)} %two_back_own.1.own, f32[1024,128]{1,0:T(8,128)} %collective-permute-done.4.ret_next, f32[1024,128]{1,0:T(8,128)} %collective-permute-done.5.ret_prev, ...), custom_call_target="tpu_custom_call" | custom-call | tf_op jit(solution)/shard_map/hidden_grad/pallas_call | solution.py:543
  136.9 2.2 %collective-permute-start.6 = (bf16[2048,128]{1,0:T(8,128)(2,1)}, bf16[2048,128]{1,0:T(8,128)(2,1)}, u32[]{:S(2)}, u32[]{:S(2)}) collective-permute-start(bf16[2048,128]{1,0:T(8,128)(2,1)} %get-tuple-element.64), channel_id=1, source_target_pairs={{0,7},{1,0},{2,1},{3,2},{4,3},{5,4},{6,5},{7,6}} | collective-permute-start | bytes 1572872 | tf_op jit(solution)/shard_map/ppermute | solution.py:425
  139.1 13.5 %one_back_own.1.own = f32[8192,128]{1,0:T(8,128)S(1)} custom-call(s32[12288]{0:T(1024)S(1)} %get-tuple-element.79.to.d4.frm, s32[12288]{0:T(1024)S(1)} %get-tuple-element.44.frm.s4.to, s32[32]{0:T(128)S(1)} %get-tuple-element.89.cnt, f32[8192,128]{1,0:T(8,128)S(1)} %get-tuple-element.63.table, f32[8192,128]{1,0:T(8,128)S(1)} %broadcast_in_dim.61.w), custom_call_target="tpu_custom_call" | custom-call | flops 199999995904 | bytes 8000000 | tf_op jit(solution)/shard_map/one_back_own/pallas_call | solution.py:553
  152.6 7.5 %collective-permute-done.6.tn = bf16[2048,128]{1,0:T(8,128)(2,1)} collective-permute-done((bf16[2048,128]{1,0:T(8,128)(2,1)}, bf16[2048,128]{1,0:T(8,128)(2,1)}, u32[]{:S(2)}, u32[]{:S(2)}) %collective-permute-start.6) | collective-permute-done | bytes 524320 | tf_op jit(solution)/shard_map/ppermute | solution.py:425
  160.1 3.3 %collective-permute-done.9.tp = bf16[2048,128]{1,0:T(8,128)(2,1)} collective-permute-done((bf16[2048,128]{1,0:T(8,128)(2,1)}, bf16[2048,128]{1,0:T(8,128)(2,1)}, u32[]{:S(2)}, u32[]{:S(2)}) %collective-permute-start.9) | collective-permute-done | bytes 524320 | tf_op jit(solution)/shard_map/ppermute | solution.py:422
  163.4 15.8 %table_grad.1.g1 = f32[200,512]{1,0:T(8,128)S(1)} custom-call(s32[2048]{0:T(1024)S(1)} %bitcast.22, s32[13312]{0:T(1024)S(1)} %bitcast.24, f32[12288]{0:T(1024)S(1)} %bitcast.26, s32[13312]{0:T(1024)S(1)} %bitcast.23, f32[12288]{0:T(1024)S(1)} %bitcast.25, f32[8192,128]{1,0:T(8,128)S(1)} %one_back_own.1.own, bf16[2048,128]{1,0:T(8,128)(2,1)} %collective-permute-done.6.tn, ...), custom_call_target="tpu_custom_call" | custom-call | tf_op jit(solution)/shard_map/table_grad/pallas_call | solution.py:554
  179.1 15.5 %reduce.18 = (f32[200,512]{1,0:T(8,128)S(1)}, f32[512,128]{1,0:T(8,128)S(1)}, f32[8,128]{1,0:T(8,128)S(1)}) custom-call(f32[200,512]{1,0:T(8,128)S(1)} %table_grad.1.g1, f32[512,128]{1,0:T(8,128)S(1)} %get-tuple-element.66.g2, f32[8,128]{1,0:T(8,128)S(1)} %get-tuple-element.67.loss, f32[8,128]{1,0:T(8,128)S(1)} %get-tuple-element.57.count), custom_call_target="tpu_custom_call" | custom-call | tf_op jit(solution)/shard_map/reduce/pallas_call | solution.py:565
  (61 shorter events, 10.3 us)
Async XLA Ops:
  0.6 21.2 %copy-start.4 = (bf16[2048,200]{0,1:T(8,128)(2,1)S(1)}, bf16[2048,200]{0,1:T(8,128)(2,1)}, u32[]{:S(2)}) copy-start(bf16[2048,200]{0,1:T(8,128)(2,1)} %param.9) | copy-start | bytes 2457604
  2.3 27.5 %copy-start.5 = (f32[512,107]{0,1:T(8,128)S(1)}, f32[512,107]{0,1:T(8,128)}, u32[]{:S(2)}) copy-start(f32[512,107]{0,1:T(8,128)} %param.11) | copy-start | bytes 657412
  3.5 26.3 %copy-start.1 = (s32[2048]{0:T(1024)S(1)}, s32[2048]{0:T(1024)}, u32[]{:S(2)}) copy-start(s32[2048]{0:T(1024)} %param.17) | copy-start | bytes 24580
  3.5 26.3 %copy-start.7 = (s32[2048]{0:T(1024)S(1)}, s32[2048]{0:T(1024)}, u32[]{:S(2)}) copy-start(s32[2048]{0:T(1024)} %param.16) | copy-start | bytes 24580
  11.2 0.7 copy-start
  19.9 1.9 copy-start.2
  27.1 18.4 %collective-permute-start = (bf16[1024,256]{1,0:T(8,128)(2,1)}, bf16[1024,256]{1,0:T(8,128)(2,1)}, u32[]{:S(2)}, u32[]{:S(2)}) collective-permute-start(bf16[1024,256]{1,0:T(8,128)(2,1)} %get-tuple-element.50), channel_id=1, source_target_pairs={{0,1},{1,2},{2,3},{3,4},{4,5},{5,6},{6,7},{7,0}} | collective-permute-start | bytes 1572872 | tf_op jit(solution)/shard_map/ppermute | solution.py:422
  27.5 18.0 %collective-permute-start.1 = (bf16[1024,256]{1,0:T(8,128)(2,1)}, bf16[1024,256]{1,0:T(8,128)(2,1)}, u32[]{:S(2)}, u32[]{:S(2)}) collective-permute-start(bf16[1024,256]{1,0:T(8,128)(2,1)} %get-tuple-element.51), channel_id=1, source_target_pairs={{0,7},{1,0},{2,1},{3,2},{4,3},{5,4},{6,5},{7,6}} | collective-permute-start | bytes 1572872 | tf_op jit(solution)/shard_map/ppermute | solution.py:425
  29.8 2.2 %copy-start.3 = (f32[8192,128]{1,0:T(8,128)S(1)}, f32[8192,128]{1,0:T(8,128)}, u32[]{:S(2)}) copy-start(f32[8192,128]{1,0:T(8,128)} %copy-done.2) | copy-start | bytes 12582916
  61.6 77.5 %collective-permute-start.7 = (bf16[2048,256]{1,0:T(8,128)(2,1)}, bf16[2048,256]{1,0:T(8,128)(2,1)}, u32[]{:S(2)}, u32[]{:S(2)}) collective-permute-start(bf16[2048,256]{1,0:T(8,128)(2,1)} %get-tuple-element.61.hid_a), channel_id=1, source_target_pairs={{0,7},{1,0},{2,1},{3,2},{4,3},{5,4},{6,5},{7,6}} | collective-permute-start | bytes 3145736 | tf_op jit(solution)/shard_map/ppermute | solution.py:425
  63.0 89.6 %collective-permute-start.10 = (bf16[2048,256]{1,0:T(8,128)(2,1)}, bf16[2048,256]{1,0:T(8,128)(2,1)}, u32[]{:S(2)}, u32[]{:S(2)}) collective-permute-start(bf16[2048,256]{1,0:T(8,128)(2,1)} %get-tuple-element.61.hid_a), channel_id=1, source_target_pairs={{0,1},{1,2},{2,3},{3,4},{4,5},{5,6},{6,7},{7,0}} | collective-permute-start | bytes 3145736 | tf_op jit(solution)/shard_map/ppermute | solution.py:422
  63.0 30.6 %collective-permute-start.2 = (bf16[1024,128]{1,0:T(8,128)(2,1)}, bf16[1024,128]{1,0:T(8,128)(2,1)}, u32[]{:S(2)}, u32[]{:S(2)}) collective-permute-start(bf16[1024,128]{1,0:T(8,128)(2,1)} %get-tuple-element.54), channel_id=1, source_target_pairs={{0,1},{1,2},{2,3},{3,4},{4,5},{5,6},{6,7},{7,0}} | collective-permute-start | bytes 786440 | tf_op jit(solution)/shard_map/ppermute | solution.py:422
  63.0 30.6 %collective-permute-start.3 = (bf16[1024,128]{1,0:T(8,128)(2,1)}, bf16[1024,128]{1,0:T(8,128)(2,1)}, u32[]{:S(2)}, u32[]{:S(2)}) collective-permute-start(bf16[1024,128]{1,0:T(8,128)(2,1)} %get-tuple-element.55), channel_id=1, source_target_pairs={{0,7},{1,0},{2,1},{3,2},{4,3},{5,4},{6,5},{7,6}} | collective-permute-start | bytes 786440 | tf_op jit(solution)/shard_map/ppermute | solution.py:425
  65.7 27.9 %copy-start.6 = (s32[2048]{0:T(1024)S(1)}, s32[2048]{0:T(1024)}, u32[]{:S(2)}) copy-start(s32[2048]{0:T(1024)} %compare_select_fusion) | copy-start | bytes 24580
  111.4 15.9 %collective-permute-start.4 = (f32[1024,128]{1,0:T(8,128)}, f32[1024,128]{1,0:T(8,128)}, u32[]{:S(2)}, u32[]{:S(2)}) collective-permute-start(f32[1024,128]{1,0:T(8,128)} %get-tuple-element.59), channel_id=1, source_target_pairs={{0,7},{1,0},{2,1},{3,2},{4,3},{5,4},{6,5},{7,6}} | collective-permute-start | bytes 1572872 | tf_op jit(solution)/shard_map/ppermute | solution.py:425
  112.6 15.2 %collective-permute-start.5 = (f32[1024,128]{1,0:T(8,128)}, f32[1024,128]{1,0:T(8,128)}, u32[]{:S(2)}, u32[]{:S(2)}) collective-permute-start(f32[1024,128]{1,0:T(8,128)} %get-tuple-element.60), channel_id=1, source_target_pairs={{0,1},{1,2},{2,3},{3,4},{4,5},{5,6},{6,7},{7,0}} | collective-permute-start | bytes 1572872 | tf_op jit(solution)/shard_map/ppermute | solution.py:422
  124.0 36.0 %collective-permute-start.8 = (bf16[2048,256]{1,0:T(8,128)(2,1)}, bf16[2048,256]{1,0:T(8,128)(2,1)}, u32[]{:S(2)}, u32[]{:S(2)}) collective-permute-start(bf16[2048,256]{1,0:T(8,128)(2,1)} %get-tuple-element.65.hid_b), channel_id=1, source_target_pairs={{0,7},{1,0},{2,1},{3,2},{4,3},{5,4},{6,5},{7,6}} | collective-permute-start | bytes 3145736 | tf_op jit(solution)/shard_map/ppermute | solution.py:425
  127.3 36.0 %collective-permute-start.11 = (bf16[2048,256]{1,0:T(8,128)(2,1)}, bf16[2048,256]{1,0:T(8,128)(2,1)}, u32[]{:S(2)}, u32[]{:S(2)}) collective-permute-start(bf16[2048,256]{1,0:T(8,128)(2,1)} %get-tuple-element.65.hid_b), channel_id=1, source_target_pairs={{0,1},{1,2},{2,3},{3,4},{4,5},{5,6},{6,7},{7,0}} | collective-permute-start | bytes 3145736 | tf_op jit(solution)/shard_map/ppermute | solution.py:422
  136.9 23.2 %collective-permute-start.6 = (bf16[2048,128]{1,0:T(8,128)(2,1)}, bf16[2048,128]{1,0:T(8,128)(2,1)}, u32[]{:S(2)}, u32[]{:S(2)}) collective-permute-start(bf16[2048,128]{1,0:T(8,128)(2,1)} %get-tuple-element.64), channel_id=1, source_target_pairs={{0,7},{1,0},{2,1},{3,2},{4,3},{5,4},{6,5},{7,6}} | collective-permute-start | bytes 1572872 | tf_op jit(solution)/shard_map/ppermute | solution.py:425
  139.1 24.2 %collective-permute-start.9 = (bf16[2048,128]{1,0:T(8,128)(2,1)}, bf16[2048,128]{1,0:T(8,128)(2,1)}, u32[]{:S(2)}, u32[]{:S(2)}) collective-permute-start(bf16[2048,128]{1,0:T(8,128)(2,1)} %get-tuple-element.64), channel_id=1, source_target_pairs={{0,1},{1,2},{2,3},{3,4},{4,5},{5,6},{6,7},{7,0}} | collective-permute-start | bytes 1572872 | tf_op jit(solution)/shard_map/ppermute | solution.py:422

commit v8 on v7

--- a/solution.py
+++ b/solution.py
@@ -129,7 +129,7 @@
     return copy
 
 
-def lists_kernel(num_dev, mask, code, wgt, x, w1, count, code_prev, code_next, w_prev, w_next, table, part, slots, send_sem, recv_sem, lsend, lrecv):
+def lists_kernel(num_dev, mask, code, wgt, count, code_prev, code_next, w_prev, w_next, part, slots, send_sem, recv_sem, lsend, lrecv):
     ones = jnp.sum(jnp.sum(mask[...].astype(F32), axis=1, keepdims=True), axis=0, keepdims=True)
     part[...] = jnp.broadcast_to(ones, part.shape)
     me = lax.axis_index(GRAPH_AXIS)
@@ -142,12 +142,6 @@
     copies.append(push(code, code_next, lsend.at[1], lrecv.at[1], pred))
     copies.append(push(wgt, w_prev, lsend.at[2], lrecv.at[2], succ))
     copies.append(push(wgt, w_next, lsend.at[3], lrecv.at[3], pred))
-
-    def put(i):
-        t = jnp.dot(x[rows_at(i), :], w1[...], preferred_element_type=F32)
-        spread(table, i * BLOCK, t.astype(BF16).astype(F32))
-
-    loop(x.shape[0] // BLOCK, put)
     for copy in copies:
         copy.wait()
     total = part[...]
@@ -173,6 +167,18 @@
         to_next[rows_at(i), :] = unspread(picked, half + i * BLOCK, BLOCK, 2).astype(BF16)
 
     loop(half // BLOCK, take)
+
+
+def one_own_kernel(s4, d4, cnt, x, w1, w, y, table, *accs):
+    zero_rows(accs)
+
+    def put(i):
+        t = jnp.dot(x[rows_at(i), :], w1[...], preferred_element_type=F32)
+        spread(table, i * BLOCK, t.astype(BF16).astype(F32))
+
+    loop(x.shape[0] // BLOCK, put)
+    edge_pass(s4, d4, w, cnt, table, accs, 4, 32, False)
+    sum_rows(y, accs)
 
 
 def one_halo_kernel(s4, d4, w, cnt, ids, y_own, x_prev, x_next, w1, w2t, hid_a, hid_b, t2, to_next, to_prev, table, picked, *accs):
@@ -464,15 +470,15 @@
         code, wc = code.reshape(-1), wc.reshape(-1)
         tally = jnp.concatenate([n_near, n_far, skip, jnp.zeros((8 * LANES - 3 * rows,), jnp.int32)])
         lists = jnp.concatenate([code, tally]).reshape(slots + 8, LANES)
-        count, code_prev, code_next, w_prev, w_next, t1 = pl.pallas_call(
+        count, code_prev, code_next, w_prev, w_next = pl.pallas_call(
             functools.partial(lists_kernel, num_dev),
-            out_shape=[sds((8, LANES), F32)] + [sds((slots + 8, LANES), jnp.int32)] * 2 + [sds((slots, LANES), F32)] * 2 + [sds((quad, LANES), F32)],
-            in_specs=[VMEM_SPEC] * 5,
-            out_specs=[VMEM_SPEC] * 6,
+            out_shape=[sds((8, LANES), F32)] + [sds((slots + 8, LANES), jnp.int32)] * 2 + [sds((slots, LANES), F32)] * 2,
+            in_specs=[VMEM_SPEC] * 3,
+            out_specs=[VMEM_SPEC] * 5,
             scratch_shapes=[pltpu.VMEM((8, LANES), F32), pltpu.VMEM((num_dev - 1, 8, LANES), F32)] + [pltpu.SemaphoreType.DMA((n,)) for n in (num_dev - 1, num_dev - 1, 4, 4)],
-            compiler_params=params(8, collective_id=0, has_side_effects=True),
+            compiler_params=params(1, collective_id=0, has_side_effects=True),
             name="lists",
-        )(label_mask.reshape(-1, LANES), lists, wc.reshape(slots, LANES), x, w1)
+        )(label_mask.reshape(-1, LANES), lists, wc.reshape(slots, LANES))
         s, d = code % n_loc, code // n_loc
         s4, d4 = s * 4, d * 4
         count, x = lax.optimization_barrier((count, x))
@@ -491,17 +497,16 @@
         thin4 = [pltpu.VMEM((n_loc, LANES), F32)] * 4
         marks = jnp.where(label_mask == 1, labels, -1)
         s4, w2t, marks, ids, w_own, wc = lax.optimization_barrier((s4, w2t, marks, ids, w_own, wc))
-        wide_own = functools.partial(
-            pl.pallas_call,
-            wide_own_kernel,
+        y_own = pl.pallas_call(
+            one_own_kernel,
             out_shape=sds((quad, LANES), F32),
-            in_specs=[SMEM_SPEC] * 3 + [VMEM_SPEC] * 2,
+            in_specs=[SMEM_SPEC] * 3 + [VMEM_SPEC] * 3,
             out_specs=VMEM_SPEC,
-            scratch_shapes=wide4,
-            compiler_params=params(28),
+            scratch_shapes=[pltpu.VMEM((quad, LANES), F32)] + wide4,
+            compiler_params=params(32),
             cost_estimate=pl.CostEstimate(flops=200000000000, bytes_accessed=8000000, transcendentals=0),
-        )
-        y_own = wide_own(name="one_own")(s4, d4, n_own, t1, w_own)
+            name="one_own",
+        )(s4, d4, n_own, x, w1, w_own)
         hid_a, hid_b, t2, t_next, t_prev = pl.pallas_call(
             one_halo_kernel,
             out_shape=[sds((n_loc, f_hid // 2), BF16)] * 2 + [sds((n_loc, LANES), F32), sds((halo, LANES), BF16), sds((halo, LANES), BF16)],
@@ -550,7 +555,16 @@
             name="hidden_grad",
         )(ids, dt2_own, rz_next, rz_prev, hid_a, hid_b, w2t)
         dt_prev, dt_next = shift_next(dt2), shift_prev(dt2)
-        dt1_own = wide_own(name="one_back_own")(d4, s4, n_own, dy, w_own)
+        dt1_own = pl.pallas_call(
+            wide_own_kernel,
+            out_shape=sds((quad, LANES), F32),
+            in_specs=[SMEM_SPEC] * 3 + [VMEM_SPEC] * 2,
+            out_specs=VMEM_SPEC,
+            scratch_shapes=wide4,
+            compiler_params=params(32),
+            cost_estimate=pl.CostEstimate(flops=200000000000, bytes_accessed=8000000, transcendentals=0),
+            name="one_back_own",
+        )(d4, s4, n_own, dy, w_own)
         grad_one = pl.pallas_call(
             functools.partial(table_grad_kernel, rows),
             out_shape=sds((f_in, f_hid), F32),

time: 197 us -> 195 us (0.990)
  local copies, waits for them, and re-layouts: 11 us -> 8.23 us
    unnamed x22 -> x25, local copies, waits for them, and re-layouts: 6.75 us -> 3.04 us
  transfers between devices with their start and end apart: 12 -> 12, of which waited for: 4 -> 4; matrix products, arithmetic and copies ran while one was open for 1% -> 1% of each run, Pallas kernels for 39% -> 40%
where the time goes in v8:
time: 195 us
  Pallas kernels  138 us (71%)
  waiting for transfers between devices  27.6 us (14%)
  starting transfers between devices  13.4 us (7%)
  local copies, waits for them, and re-layouts  8.23 us (4%)
  other arithmetic  5.99 us (3%)
    ppermute x6, waiting for transfers between devices, shift_next(): return lax.ppermute(a, GRAPH_AXIS, to_next)  20.1 us
    pallas_call x1, Pallas kernels, device_step(): pl.pallas_call(functools.partial(logits_kernel, classes), out_shape=[sds(...  17.5 us
    pallas_call x1, Pallas kernels, device_step(): pl.pallas_call(one_halo_kernel, out_shape=[sds((n_loc, f_hid // 2), BF16)...  16.1 us
    pallas_call x1, Pallas kernels, device_step(): pl.pallas_call(functools.partial(table_grad_kernel, rows), out_shape=sds(...  15.7 us
    pallas_call x1, Pallas kernels, device_step(): pl.pallas_call(functools.partial(reduce_kernel, num_dev), out_shape=[sds(...  15.5 us
    pallas_call x1, Pallas kernels, device_step(): pl.pallas_call(one_own_kernel, out_shape=sds((quad, LANES), F32), in_spec...  15.1 us
    pallas_call x1, Pallas kernels, device_step(): pl.pallas_call(wide_own_kernel, out_shape=sds((quad, LANES), F32), in_spe...  13.5 us
    ppermute x6, starting transfers between devices, shift_prev(): return lax.ppermute(a, GRAPH_AXIS, to_prev)  13 us
  transfers between devices with their start and end apart: 12, of which 4 were waited for; matrix products, arithmetic and copies ran while one was open for 1% of the time, Pallas kernels for 40%

profile of v8, /device:TPU:0, one launch (start us, length us, event | category | flops | bytes accessed | tf_op | source)
XLA Modules:
  0.0 194.5 jit_solution(16919721168211335247)
XLA Ops:
  3.6 4.2 %select_reduce_fusion = (s32[32,384]{1,0:T(8,128)S(1)}, f32[32,384]{1,0:T(8,128)S(1)}) fusion(f32[32,256]{1,0:T(8,128)S(1)} %reshape.68, s32[32,256]{1,0:T(8,128)S(1)} %get-tuple-element.88, s32[32,256]{1,0:T(8,128)S(1)} %get-tuple-element.89), kind=kLoop, calls=%fused_computation | loop fusion | flops 15704064 | bytes 196608 | tf_op jit(solution)/shard_map/reduce | solution.py:452
  9.4 8.0 %lists.1 = (f32[8,128]{1,0:T(8,128)S(1)}, s32[104,128]{1,0:T(8,128)S(1)}, s32[104,128]{1,0:T(8,128)S(1)}, f32[96,128]{1,0:T(8,128)S(1)}, f32[96,128]{1,0:T(8,128)S(1)}) custom-call(s32[16,128]{1,0:T(8,128)S(1)} %bitcast.27, s32[104,128]{1,0:T(8,128)S(1)} %bitcast.18, f32[96,128]{1,0:T(8,128)S(1)} %reshape_reshape.3.wgt), custom_call_target="tpu_custom_call" | custom-call | tf_op jit(solution)/shard_map/lists/pallas_call | solution.py:473
  17.4 1.4 copy.16.x
  18.8 4.7 %halo_rows.1 = (bf16[1024,256]{1,0:T(8,128)(2,1)}, bf16[1024,256]{1,0:T(8,128)(2,1)}) custom-call(s32[2048]{0:T(1024)S(1)} %bitcast.19, bf16[2048,200]{1,0:T(8,128)(2,1)S(1)} %copy.16.x), custom_call_target="tpu_custom_call" | custom-call | tf_op jit(solution)/shard_map/halo_rows/pallas_call | solution.py:485
  24.0 2.2 %collective-permute-start.1 = (bf16[1024,256]{1,0:T(8,128)(2,1)}, bf16[1024,256]{1,0:T(8,128)(2,1)}, u32[]{:S(2)}, u32[]{:S(2)}) collective-permute-start(bf16[1024,256]{1,0:T(8,128)(2,1)} %get-tuple-element.49), channel_id=1, source_target_pairs={{0,7},{1,0},{2,1},{3,2},{4,3},{5,4},{6,5},{7,6}} | collective-permute-start | bytes 1572872 | tf_op jit(solution)/shard_map/ppermute | solution.py:431
  27.0 1.1 broadcast_in_dim.61.w
  28.2 15.1 %one_own.1.y_own = f32[8192,128]{1,0:T(8,128)S(1)} custom-call(s32[12288]{0:T(1024)S(1)} %get-tuple-element.43.s4.to, s32[12288]{0:T(1024)S(1)} %get-tuple-element.77.d4.frm, s32[32]{0:T(128)S(1)} %get-tuple-element.87.cnt, bf16[2048,200]{1,0:T(8,128)(2,1)S(1)} %copy.16.x, bf16[200,512]{1,0:T(8,128)(2,1)S(1)} %convert_element_type.30.w1, ...), custom_call_target="tpu_custom_call" | custom-call | flops 199999995904 | bytes 8000000 | tf_op jit(solution)/shard_map/one_own/pallas_call | solution.py:500
  43.4 16.1 %one_halo.1 = (bf16[2048,256]{1,0:T(8,128)(2,1)}, bf16[2048,256]{1,0:T(8,128)(2,1)}, f32[2048,128]{1,0:T(8,128)S(1)}, bf16[1024,128]{1,0:T(8,128)(2,1)}, bf16[1024,128]{1,0:T(8,128)(2,1)}) custom-call(s32[12288]{0:T(1024)S(1)} %get-tuple-element.43.s4.to, s32[12288]{0:T(1024)S(1)} %get-tuple-element.77.d4.frm, f32[12288]{0:T(1024)S(1)} %reshape.72.w, ...), custom_call_target="tpu_custom_call" | custom-call | tf_op jit(solution)/shard_map/one_halo/pallas_call | solution.py:510
  59.5 1.4 collective-permute-start.7
  60.9 2.7 %collective-permute-start.3 = (bf16[1024,128]{1,0:T(8,128)(2,1)}, bf16[1024,128]{1,0:T(8,128)(2,1)}, u32[]{:S(2)}, u32[]{:S(2)}) collective-permute-start(bf16[1024,128]{1,0:T(8,128)(2,1)} %get-tuple-element.53), channel_id=1, source_target_pairs={{0,7},{1,0},{2,1},{3,2},{4,3},{5,4},{6,5},{7,6}} | collective-permute-start | bytes 786440 | tf_op jit(solution)/shard_map/ppermute | solution.py:431
  63.5 11.5 %two_own.1.z_own = f32[2048,128]{1,0:T(8,128)S(1)} custom-call(s32[12288]{0:T(1024)S(1)} %get-tuple-element.84.frm.s.to, s32[12288]{0:T(1024)S(1)} %get-tuple-element.78.to.d.frm, s32[32]{0:T(128)S(1)} %get-tuple-element.87.cnt, f32[2048,128]{1,0:T(8,128)S(1)} %get-tuple-element.51.table, f32[8192,128]{1,0:T(8,128)S(1)} %broadcast_in_dim.61.w), custom_call_target="tpu_custom_call" | custom-call | flops 199999995904 | bytes 8000000 | tf_op jit(solution)/shard_map/two_own/pallas_call | solution.py:532
  75.0 16.4 %collective-permute-done.2.t_prev = bf16[1024,128]{1,0:T(8,128)(2,1)} collective-permute-done((bf16[1024,128]{1,0:T(8,128)(2,1)}, bf16[1024,128]{1,0:T(8,128)(2,1)}, u32[]{:S(2)}, u32[]{:S(2)}) %collective-permute-start.2) | collective-permute-done | bytes 262176 | tf_op jit(solution)/shard_map/ppermute | solution.py:428
  91.8 17.5 %logits.1 = (f32[2048,128]{1,0:T(8,128)S(1)}, f32[1024,128]{1,0:T(8,128)}, f32[1024,128]{1,0:T(8,128)}, f32[8,128]{1,0:T(8,128)S(1)}) custom-call(s32[12288]{0:T(1024)S(1)} %get-tuple-element.84.frm.s.to, s32[12288]{0:T(1024)S(1)} %get-tuple-element.78.to.d.frm, f32[12288]{0:T(1024)S(1)} %reshape.72.w, s32[32]{0:T(128)S(1)} %get-tuple-element.75.cnt, ...), custom_call_target="tpu_custom_call" | custom-call | tf_op jit(solution)/shard_map/logits/pallas_call | solution.py:534
  109.2 1.2 collective-permute-start.4
  110.4 11.5 %two_back_own.1.own = f32[2048,128]{1,0:T(8,128)S(1)} custom-call(s32[12288]{0:T(1024)S(1)} %get-tuple-element.78.to.d.frm, s32[12288]{0:T(1024)S(1)} %get-tuple-element.84.frm.s.to, s32[32]{0:T(128)S(1)} %get-tuple-element.87.cnt, f32[2048,128]{1,0:T(8,128)S(1)} %get-tuple-element.56.table, f32[8192,128]{1,0:T(8,128)S(1)} %broadcast_in_dim.61.w), custom_call_target="tpu_custom_call" | custom-call | flops 199999995904 | bytes 8000000 | tf_op jit(solution)/shard_map/two_back_own/pallas_call | solution.py:547
  121.9 3.3 %collective-permute-start.8 = (bf16[2048,256]{1,0:T(8,128)(2,1)}, bf16[2048,256]{1,0:T(8,128)(2,1)}, u32[]{:S(2)}, u32[]{:S(2)}) collective-permute-start(bf16[2048,256]{1,0:T(8,128)(2,1)} %get-tuple-element.63.hid_b), channel_id=1, source_target_pairs={{0,7},{1,0},{2,1},{3,2},{4,3},{5,4},{6,5},{7,6}} | collective-permute-start | bytes 3145736 | tf_op jit(solution)/shard_map/ppermute | solution.py:431
  125.5 9.1 %hidden_grad.1 = (bf16[2048,128]{1,0:T(8,128)(2,1)}, f32[8192,128]{1,0:T(8,128)S(1)}, f32[512,128]{1,0:T(8,128)S(1)}) custom-call(s32[2048]{0:T(1024)S(1)} %bitcast.21, f32[2048,128]{1,0:T(8,128)S(1)} %two_back_own.1.own, f32[1024,128]{1,0:T(8,128)} %collective-permute-done.4.ret_next, f32[1024,128]{1,0:T(8,128)} %collective-permute-done.5.ret_prev, ...), custom_call_target="tpu_custom_call" | custom-call | tf_op jit(solution)/shard_map/hidden_grad/pallas_call | solution.py:548
  134.7 2.3 %collective-permute-start.6 = (bf16[2048,128]{1,0:T(8,128)(2,1)}, bf16[2048,128]{1,0:T(8,128)(2,1)}, u32[]{:S(2)}, u32[]{:S(2)}) collective-permute-start(bf16[2048,128]{1,0:T(8,128)(2,1)} %get-tuple-element.62), channel_id=1, source_target_pairs={{0,7},{1,0},{2,1},{3,2},{4,3},{5,4},{6,5},{7,6}} | collective-permute-start | bytes 1572872 | tf_op jit(solution)/shard_map/ppermute | solution.py:431
  137.0 13.5 %one_back_own.1.own = f32[8192,128]{1,0:T(8,128)S(1)} custom-call(s32[12288]{0:T(1024)S(1)} %get-tuple-element.77.d4.frm, s32[12288]{0:T(1024)S(1)} %get-tuple-element.43.s4.to, s32[32]{0:T(128)S(1)} %get-tuple-element.87.cnt, f32[8192,128]{1,0:T(8,128)S(1)} %get-tuple-element.61.table, f32[8192,128]{1,0:T(8,128)S(1)} %broadcast_in_dim.61.w), custom_call_target="tpu_custom_call" | custom-call | flops 199999995904 | bytes 8000000 | tf_op jit(solution)/shard_map/one_back_own/pallas_call | solution.py:558
  150.4 7.4 %collective-permute-done.6.tn = bf16[2048,128]{1,0:T(8,128)(2,1)} collective-permute-done((bf16[2048,128]{1,0:T(8,128)(2,1)}, bf16[2048,128]{1,0:T(8,128)(2,1)}, u32[]{:S(2)}, u32[]{:S(2)}) %collective-permute-start.6) | collective-permute-done | bytes 524320 | tf_op jit(solution)/shard_map/ppermute | solution.py:431
  157.9 3.3 %collective-permute-done.9.tp = bf16[2048,128]{1,0:T(8,128)(2,1)} collective-permute-done((bf16[2048,128]{1,0:T(8,128)(2,1)}, bf16[2048,128]{1,0:T(8,128)(2,1)}, u32[]{:S(2)}, u32[]{:S(2)}) %collective-permute-start.9) | collective-permute-done | bytes 524320 | tf_op jit(solution)/shard_map/ppermute | solution.py:428
  161.2 15.7 %table_grad.1.g1 = f32[200,512]{1,0:T(8,128)S(1)} custom-call(s32[2048]{0:T(1024)S(1)} %bitcast.22, s32[13312]{0:T(1024)S(1)} %bitcast.24, f32[12288]{0:T(1024)S(1)} %bitcast.26, s32[13312]{0:T(1024)S(1)} %bitcast.23, f32[12288]{0:T(1024)S(1)} %bitcast.25, f32[8192,128]{1,0:T(8,128)S(1)} %one_back_own.1.own, bf16[2048,128]{1,0:T(8,128)(2,1)} %collective-permute-done.6.tn, ...), custom_call_target="tpu_custom_call" | custom-call | tf_op jit(solution)/shard_map/table_grad/pallas_call | solution.py:568
  176.9 15.5 %reduce.18 = (f32[200,512]{1,0:T(8,128)S(1)}, f32[512,128]{1,0:T(8,128)S(1)}, f32[8,128]{1,0:T(8,128)S(1)}) custom-call(f32[200,512]{1,0:T(8,128)S(1)} %table_grad.1.g1, f32[512,128]{1,0:T(8,128)S(1)} %get-tuple-element.64.g2, f32[8,128]{1,0:T(8,128)S(1)} %get-tuple-element.65.loss, f32[8,128]{1,0:T(8,128)S(1)} %get-tuple-element.55.count), custom_call_target="tpu_custom_call" | custom-call | tf_op jit(solution)/shard_map/reduce/pallas_call | solution.py:579
  192.9 0.8 copy.19
  (64 shorter events, 7.6 us)
Async XLA Ops:
  0.6 25.7 %copy-start.5 = (s32[2048]{0:T(1024)S(1)}, s32[2048]{0:T(1024)}, u32[]{:S(2)}) copy-start(s32[2048]{0:T(1024)} %param.17) | copy-start | bytes 24580
  0.6 25.7 %copy-start.7 = (f32[512,107]{0,1:T(8,128)S(1)}, f32[512,107]{0,1:T(8,128)}, u32[]{:S(2)}) copy-start(f32[512,107]{0,1:T(8,128)} %param.11) | copy-start | bytes 657412
  0.7 25.7 %copy-start.9 = (s32[2048]{0:T(1024)S(1)}, s32[2048]{0:T(1024)}, u32[]{:S(2)}) copy-start(s32[2048]{0:T(1024)} %param.16) | copy-start | bytes 24580
  8.6 17.7 %copy-start.2 = (s32[1,8,2,128]{3,1,2,0:T(8,128)}, s32[1,8,2,128]{3,1,2,0:T(8,128)S(1)}, u32[]{:S(2)}) copy-start(s32[1,8,2,128]{3,1,2,0:T(8,128)S(1)} %copy.23) | copy-start | bytes 24580
  8.7 0.7 copy-start.4
  9.4 18.8 %copy-start.6 = (f32[200,512]{1,0:T(8,128)S(1)}, f32[200,512]{1,0:T(8,128)}, u32[]{:S(2)}) copy-start(f32[200,512]{1,0:T(8,128)} %param.10) | copy-start | bytes 1228804
  23.6 19.8 %collective-permute-start = (bf16[1024,256]{1,0:T(8,128)(2,1)}, bf16[1024,256]{1,0:T(8,128)(2,1)}, u32[]{:S(2)}, u32[]{:S(2)}) collective-permute-start(bf16[1024,256]{1,0:T(8,128)(2,1)} %get-tuple-element.48), channel_id=1, source_target_pairs={{0,1},{1,2},{2,3},{3,4},{4,5},{5,6},{6,7},{7,0}} | collective-permute-start | bytes 1572872 | tf_op jit(solution)/shard_map/ppermute | solution.py:428
  24.0 19.4 %collective-permute-start.1 = (bf16[1024,256]{1,0:T(8,128)(2,1)}, bf16[1024,256]{1,0:T(8,128)(2,1)}, u32[]{:S(2)}, u32[]{:S(2)}) collective-permute-start(bf16[1024,256]{1,0:T(8,128)(2,1)} %get-tuple-element.49), channel_id=1, source_target_pairs={{0,7},{1,0},{2,1},{3,2},{4,3},{5,4},{6,5},{7,6}} | collective-permute-start | bytes 1572872 | tf_op jit(solution)/shard_map/ppermute | solution.py:431
  27.0 98.5 %copy-start = (bf16[128,512]{1,0:T(8,128)(2,1)}, bf16[128,512]{1,0:T(8,128)(2,1)S(1)}, u32[]{:S(2)}) copy-start(bf16[128,512]{1,0:T(8,128)(2,1)S(1)} %pad.4.w2t) | copy-start | bytes 393220
  28.2 15.2 %copy-start.3 = (s32[1,8,2,128]{3,1,2,0:T(8,128)S(1)}, s32[1,8,2,128]{3,1,2,0:T(8,128)}, u32[]{:S(2)}) copy-start(s32[1,8,2,128]{3,1,2,0:T(8,128)} %copy-done.2) | copy-start | bytes 24580
  59.5 77.5 %collective-permute-start.7 = (bf16[2048,256]{1,0:T(8,128)(2,1)}, bf16[2048,256]{1,0:T(8,128)(2,1)}, u32[]{:S(2)}, u32[]{:S(2)}) collective-permute-start(bf16[2048,256]{1,0:T(8,128)(2,1)} %get-tuple-element.59.hid_a), channel_id=1, source_target_pairs={{0,7},{1,0},{2,1},{3,2},{4,3},{5,4},{6,5},{7,6}} | collective-permute-start | bytes 3145736 | tf_op jit(solution)/shard_map/ppermute | solution.py:431
  60.9 89.6 %collective-permute-start.10 = (bf16[2048,256]{1,0:T(8,128)(2,1)}, bf16[2048,256]{1,0:T(8,128)(2,1)}, u32[]{:S(2)}, u32[]{:S(2)}) collective-permute-start(bf16[2048,256]{1,0:T(8,128)(2,1)} %get-tuple-element.59.hid_a), channel_id=1, source_target_pairs={{0,1},{1,2},{2,3},{3,4},{4,5},{5,6},{6,7},{7,0}} | collective-permute-start | bytes 3145736 | tf_op jit(solution)/shard_map/ppermute | solution.py:428
  60.9 30.6 %collective-permute-start.2 = (bf16[1024,128]{1,0:T(8,128)(2,1)}, bf16[1024,128]{1,0:T(8,128)(2,1)}, u32[]{:S(2)}, u32[]{:S(2)}) collective-permute-start(bf16[1024,128]{1,0:T(8,128)(2,1)} %get-tuple-element.52), channel_id=1, source_target_pairs={{0,1},{1,2},{2,3},{3,4},{4,5},{5,6},{6,7},{7,0}} | collective-permute-start | bytes 786440 | tf_op jit(solution)/shard_map/ppermute | solution.py:428
  60.9 30.6 %collective-permute-start.3 = (bf16[1024,128]{1,0:T(8,128)(2,1)}, bf16[1024,128]{1,0:T(8,128)(2,1)}, u32[]{:S(2)}, u32[]{:S(2)}) collective-permute-start(bf16[1024,128]{1,0:T(8,128)(2,1)} %get-tuple-element.53), channel_id=1, source_target_pairs={{0,7},{1,0},{2,1},{3,2},{4,3},{5,4},{6,5},{7,6}} | collective-permute-start | bytes 786440 | tf_op jit(solution)/shard_map/ppermute | solution.py:431
  63.5 27.9 %copy-start.8 = (s32[2048]{0:T(1024)S(1)}, s32[2048]{0:T(1024)}, u32[]{:S(2)}) copy-start(s32[2048]{0:T(1024)} %compare_select_fusion) | copy-start | bytes 24580
  109.2 15.9 %collective-permute-start.4 = (f32[1024,128]{1,0:T(8,128)}, f32[1024,128]{1,0:T(8,128)}, u32[]{:S(2)}, u32[]{:S(2)}) collective-permute-start(f32[1024,128]{1,0:T(8,128)} %get-tuple-element.57), channel_id=1, source_target_pairs={{0,7},{1,0},{2,1},{3,2},{4,3},{5,4},{6,5},{7,6}} | collective-permute-start | bytes 1572872 | tf_op jit(solution)/shard_map/ppermute | solution.py:431
  110.4 15.1 %collective-permute-start.5 = (f32[1024,128]{1,0:T(8,128)}, f32[1024,128]{1,0:T(8,128)}, u32[]{:S(2)}, u32[]{:S(2)}) collective-permute-start(f32[1024,128]{1,0:T(8,128)} %get-tuple-element.58), channel_id=1, source_target_pairs={{0,1},{1,2},{2,3},{3,4},{4,5},{5,6},{6,7},{7,0}} | collective-permute-start | bytes 1572872 | tf_op jit(solution)/shard_map/ppermute | solution.py:428
  121.9 36.0 %collective-permute-start.8 = (bf16[2048,256]{1,0:T(8,128)(2,1)}, bf16[2048,256]{1,0:T(8,128)(2,1)}, u32[]{:S(2)}, u32[]{:S(2)}) collective-permute-start(bf16[2048,256]{1,0:T(8,128)(2,1)} %get-tuple-element.63.hid_b), channel_id=1, source_target_pairs={{0,7},{1,0},{2,1},{3,2},{4,3},{5,4},{6,5},{7,6}} | collective-permute-start | bytes 3145736 | tf_op jit(solution)/shard_map/ppermute | solution.py:431
  125.2 36.0 %collective-permute-start.11 = (bf16[2048,256]{1,0:T(8,128)(2,1)}, bf16[2048,256]{1,0:T(8,128)(2,1)}, u32[]{:S(2)}, u32[]{:S(2)}) collective-permute-start(bf16[2048,256]{1,0:T(8,128)(2,1)} %get-tuple-element.63.hid_b), channel_id=1, source_target_pairs={{0,1},{1,2},{2,3},{3,4},{4,5},{5,6},{6,7},{7,0}} | collective-permute-start | bytes 3145736 | tf_op jit(solution)/shard_map/ppermute | solution.py:428
  134.7 23.2 %collective-permute-start.6 = (bf16[2048,128]{1,0:T(8,128)(2,1)}, bf16[2048,128]{1,0:T(8,128)(2,1)}, u32[]{:S(2)}, u32[]{:S(2)}) collective-permute-start(bf16[2048,128]{1,0:T(8,128)(2,1)} %get-tuple-element.62), channel_id=1, source_target_pairs={{0,7},{1,0},{2,1},{3,2},{4,3},{5,4},{6,5},{7,6}} | collective-permute-start | bytes 1572872 | tf_op jit(solution)/shard_map/ppermute | solution.py:431
  137.0 24.2 %collective-permute-start.9 = (bf16[2048,128]{1,0:T(8,128)(2,1)}, bf16[2048,128]{1,0:T(8,128)(2,1)}, u32[]{:S(2)}, u32[]{:S(2)}) collective-permute-start(bf16[2048,128]{1,0:T(8,128)(2,1)} %get-tuple-element.62), channel_id=1, source_target_pairs={{0,1},{1,2},{2,3},{3,4},{4,5},{5,6},{6,7},{7,0}} | collective-permute-start | bytes 1572872 | tf_op jit(solution)/shard_map/ppermute | solution.py:428
  137.0 24.2 %copy-start.1 = (bf16[128,512]{1,0:T(8,128)(2,1)S(1)}, bf16[128,512]{1,0:T(8,128)(2,1)}, u32[]{:S(2)}) copy-start(bf16[128,512]{1,0:T(8,128)(2,1)} %copy-done) | copy-start | bytes 393220

commit v9 on v8

--- a/solution.py
+++ b/solution.py
@@ -286,8 +286,8 @@
 def hidden_grad_kernel(ids, own, ret_next, ret_prev, hid_a, hid_b, w2t, dt2, dy, g2, *accs):
     n_loc, half = own.shape[0], ret_next.shape[0]
     zero_rows(accs)
-    scatter_pass(ids.at[pl.ds(half, half)], ret_next, accs, 1, 8)
-    scatter_pass(ids.at[pl.ds(0, half)], ret_prev, accs, 1, 8)
+    scatter_pass(ids.at[pl.ds(half, half)], ret_next, accs, 1, 16)
+    scatter_pass(ids.at[pl.ds(0, half)], ret_prev, accs, 1, 16)
     g2[...] = jnp.zeros_like(g2)
 
     def fold(i):
@@ -324,7 +324,7 @@
             for u in range(16):
                 acc = accs[u % n_acc]
                 code = codes[u]
-                frm = lax.shift_right_logical(code, shift) * 4
+                frm = lax.shift_right_logical(code, shift)
                 val = table[pl.ds(pl.multiple_of(frm, 4), 4), :] * wgt[u]
                 at = pl.ds(pl.multiple_of(owners[code & (half - 1)] * 4, 4), 4)
                 acc[at, :] = acc[at, :] + val
@@ -432,7 +432,8 @@
 
     def compact(edge_src, edge_dst, edge_w, n_loc, halo):
         rows = edge_src.shape[0] // CHUNK
-        src, dst, w = (a.reshape(rows, CHUNK) for a in (edge_src, edge_dst, edge_w))
+        views = [a.reshape(2, rows, LANES) for a in (edge_src, edge_dst, edge_w)]
+        src, dst, w = (jnp.concatenate([v[0], v[1]], axis=1) for v in views)
         live = w != 0.0
         own = live & (src < n_loc)
         far = live & (src >= n_loc + halo)
@@ -447,7 +448,7 @@
         place = jnp.where(near, SLOT - 1 - rank[rows:2 * rows], place)
         place = jnp.where(own, rank[:rows], place)
         hit = place[:, :, None] == jnp.arange(SLOT)[None, None, :]
-        code = jnp.where(src < n_loc, src, src - n_loc) + dst * n_loc
+        code = jnp.where(src < n_loc, src, src - n_loc) + dst * (4 * n_loc)
         picks = (jnp.where(hit, code[:, :, None], 0), jnp.where(hit, w[:, :, None], 0.0))
         code, wc = lax.reduce(picks, (jnp.int32(0), jnp.float32(0.0)), lambda a, b: (a[0] + b[0], a[1] + b[1]), (1,))
         n_hal = jnp.where(n_far > 0, skip + n_far, n_near)
@@ -479,8 +480,8 @@
             compiler_params=params(1, collective_id=0, has_side_effects=True),
             name="lists",
         )(label_mask.reshape(-1, LANES), lists, wc.reshape(slots, LANES))
-        s, d = code % n_loc, code // n_loc
-        s4, d4 = s * 4, d * 4
+        s, d4 = code % n_loc, code // n_loc
+        s4, d = s * 4, d4 // 4
         count, x = lax.optimization_barrier((count, x))
         x_next, x_prev = pl.pallas_call(
             halo_rows_kernel,

time: 195 us -> 195 us (level)
  Pallas kernels: 138 us -> 140 us
  transfers between devices with their start and end apart: 12 -> 12, of which waited for: 4 -> 3; matrix products, arithmetic and copies ran while one was open for 1% -> 1% of each run, Pallas kernels for 40% -> 41%
where the time goes in v9:
time: 195 us
  Pallas kernels  140 us (72%)
  waiting for transfers between devices  26.5 us (14%)
  starting transfers between devices  13.9 us (7%)
  local copies, waits for them, and re-layouts  8.19 us (4%)
  other arithmetic  5.26 us (3%)
    ppermute x6, waiting for transfers between devices, shift_next(): return lax.ppermute(a, GRAPH_AXIS, to_next)  19.5 us
    pallas_call x1, Pallas kernels, device_step(): pl.pallas_call(functools.partial(logits_kernel, classes), out_shape=[sds(...  17.6 us
    pallas_call x1, Pallas kernels, device_step(): pl.pallas_call(one_halo_kernel, out_shape=[sds((n_loc, f_hid // 2), BF16)...  16.1 us
    pallas_call x1, Pallas kernels, device_step(): pl.pallas_call(functools.partial(table_grad_kernel, rows), out_shape=sds(...  15.9 us
    pallas_call x1, Pallas kernels, device_step(): pl.pallas_call(functools.partial(reduce_kernel, num_dev), out_shape=[sds(...  15.6 us
    pallas_call x1, Pallas kernels, device_step(): pl.pallas_call(one_own_kernel, out_shape=sds((quad, LANES), F32), in_spec...  15.6 us
    pallas_call x1, Pallas kernels, device_step(): pl.pallas_call(wide_own_kernel, out_shape=sds((quad, LANES), F32), in_spe...  13.9 us
    ppermute x6, starting transfers between devices, shift_prev(): return lax.ppermute(a, GRAPH_AXIS, to_prev)  13.4 us
  transfers between devices with their start and end apart: 12, of which 3 were waited for; matrix products, arithmetic and copies ran while one was open for 1% of the time, Pallas kernels for 41%

profile of v9, /device:TPU:0, one launch (start us, length us, event | category | flops | bytes accessed | tf_op | source)
XLA Modules:
  0.0 194.8 jit_solution(17607464236478967520)
XLA Ops:
  2.8 4.2 %select_reduce_fusion = (s32[32,384]{1,0:T(8,128)S(1)}, f32[32,384]{1,0:T(8,128)S(1)}) fusion(f32[32,256]{1,0:T(8,128)S(1)} %pad_maximum_fusion, s32[32,256]{1,0:T(8,128)S(1)} %fusion.3, s32[32,256]{1,0:T(8,128)S(1)} %fusion.6), kind=kLoop, calls=%fused_computation | loop fusion | flops 15704064 | bytes 196608 | tf_op jit(solution)/shard_map/reduce | solution.py:453
  8.6 8.0 %lists.1 = (f32[8,128]{1,0:T(8,128)S(1)}, s32[104,128]{1,0:T(8,128)S(1)}, s32[104,128]{1,0:T(8,128)S(1)}, f32[96,128]{1,0:T(8,128)S(1)}, f32[96,128]{1,0:T(8,128)S(1)}) custom-call(s32[16,128]{1,0:T(8,128)S(1)} %bitcast.39, s32[104,128]{1,0:T(8,128)S(1)} %bitcast.30, f32[96,128]{1,0:T(8,128)S(1)} %reshape_reshape.3.wgt), custom_call_target="tpu_custom_call" | custom-call | tf_op jit(solution)/shard_map/lists/pallas_call | solution.py:474
  16.6 1.4 copy.16.x
  18.0 4.7 %halo_rows.1 = (bf16[1024,256]{1,0:T(8,128)(2,1)}, bf16[1024,256]{1,0:T(8,128)(2,1)}) custom-call(s32[2048]{0:T(1024)S(1)} %bitcast.31, bf16[2048,200]{1,0:T(8,128)(2,1)S(1)} %copy.16.x), custom_call_target="tpu_custom_call" | custom-call | tf_op jit(solution)/shard_map/halo_rows/pallas_call | solution.py:486
  23.2 2.2 %collective-permute-start.1 = (bf16[1024,256]{1,0:T(8,128)(2,1)}, bf16[1024,256]{1,0:T(8,128)(2,1)}, u32[]{:S(2)}, u32[]{:S(2)}) collective-permute-start(bf16[1024,256]{1,0:T(8,128)(2,1)} %get-tuple-element.49), channel_id=1, source_target_pairs={{0,7},{1,0},{2,1},{3,2},{4,3},{5,4},{6,5},{7,6}} | collective-permute-start | bytes 1572872 | tf_op jit(solution)/shard_map/ppermute | solution.py:431
  26.2 1.1 broadcast_in_dim.62.w
  27.4 15.6 %one_own.1.y_own = f32[8192,128]{1,0:T(8,128)S(1)} custom-call(s32[12288]{0:T(1024)S(1)} %get-tuple-element.43.s4.to, s32[12288]{0:T(1024)S(1)} %get-tuple-element.78.d4.frm, s32[32]{0:T(128)S(1)} %get-tuple-element.93.cnt, bf16[2048,200]{1,0:T(8,128)(2,1)S(1)} %copy.16.x, bf16[200,512]{1,0:T(8,128)(2,1)S(1)} %convert_element_type.30.w1, ...), custom_call_target="tpu_custom_call" | custom-call | flops 199999995904 | bytes 8000000 | tf_op jit(solution)/shard_map/one_own/pallas_call | solution.py:501
  43.1 16.1 %one_halo.1 = (bf16[2048,256]{1,0:T(8,128)(2,1)}, bf16[2048,256]{1,0:T(8,128)(2,1)}, f32[2048,128]{1,0:T(8,128)S(1)}, bf16[1024,128]{1,0:T(8,128)(2,1)}, bf16[1024,128]{1,0:T(8,128)(2,1)}) custom-call(s32[12288]{0:T(1024)S(1)} %get-tuple-element.43.s4.to, s32[12288]{0:T(1024)S(1)} %get-tuple-element.78.d4.frm, f32[12288]{0:T(1024)S(1)} %reshape.170.w, ...), custom_call_target="tpu_custom_call" | custom-call | tf_op jit(solution)/shard_map/one_halo/pallas_call | solution.py:511
  59.2 1.4 collective-permute-start.7
  60.6 2.7 %collective-permute-start.3 = (bf16[1024,128]{1,0:T(8,128)(2,1)}, bf16[1024,128]{1,0:T(8,128)(2,1)}, u32[]{:S(2)}, u32[]{:S(2)}) collective-permute-start(bf16[1024,128]{1,0:T(8,128)(2,1)} %get-tuple-element.53), channel_id=1, source_target_pairs={{0,7},{1,0},{2,1},{3,2},{4,3},{5,4},{6,5},{7,6}} | collective-permute-start | bytes 786440 | tf_op jit(solution)/shard_map/ppermute | solution.py:431
  63.2 11.8 %two_own.1.z_own = f32[2048,128]{1,0:T(8,128)S(1)} custom-call(s32[12288]{0:T(1024)S(1)} %get-tuple-element.84.frm.s.to, s32[12288]{0:T(1024)S(1)} %get-tuple-element.77.to.d.frm, s32[32]{0:T(128)S(1)} %get-tuple-element.93.cnt, f32[2048,128]{1,0:T(8,128)S(1)} %get-tuple-element.51.table, f32[8192,128]{1,0:T(8,128)S(1)} %broadcast_in_dim.62.w), custom_call_target="tpu_custom_call" | custom-call | flops 199999995904 | bytes 8000000 | tf_op jit(solution)/shard_map/two_own/pallas_call | solution.py:533
  75.1 16.1 %collective-permute-done.2.t_prev = bf16[1024,128]{1,0:T(8,128)(2,1)} collective-permute-done((bf16[1024,128]{1,0:T(8,128)(2,1)}, bf16[1024,128]{1,0:T(8,128)(2,1)}, u32[]{:S(2)}, u32[]{:S(2)}) %collective-permute-start.2) | collective-permute-done | bytes 262176 | tf_op jit(solution)/shard_map/ppermute | solution.py:428
  91.5 17.6 %logits.1 = (f32[2048,128]{1,0:T(8,128)S(1)}, f32[1024,128]{1,0:T(8,128)}, f32[1024,128]{1,0:T(8,128)}, f32[8,128]{1,0:T(8,128)S(1)}) custom-call(s32[12288]{0:T(1024)S(1)} %get-tuple-element.84.frm.s.to, s32[12288]{0:T(1024)S(1)} %get-tuple-element.77.to.d.frm, f32[12288]{0:T(1024)S(1)} %reshape.170.w, s32[32]{0:T(128)S(1)} %get-tuple-element.75.cnt, ...), custom_call_target="tpu_custom_call" | custom-call | tf_op jit(solution)/shard_map/logits/pallas_call | solution.py:535
  109.0 1.3 collective-permute-start.4
  110.4 11.8 %two_back_own.1.own = f32[2048,128]{1,0:T(8,128)S(1)} custom-call(s32[12288]{0:T(1024)S(1)} %get-tuple-element.77.to.d.frm, s32[12288]{0:T(1024)S(1)} %get-tuple-element.84.frm.s.to, s32[32]{0:T(128)S(1)} %get-tuple-element.93.cnt, f32[2048,128]{1,0:T(8,128)S(1)} %get-tuple-element.56.table, f32[8192,128]{1,0:T(8,128)S(1)} %broadcast_in_dim.62.w), custom_call_target="tpu_custom_call" | custom-call | flops 199999995904 | bytes 8000000 | tf_op jit(solution)/shard_map/two_back_own/pallas_call | solution.py:548
  122.2 3.2 %collective-permute-start.8 = (bf16[2048,256]{1,0:T(8,128)(2,1)}, bf16[2048,256]{1,0:T(8,128)(2,1)}, u32[]{:S(2)}, u32[]{:S(2)}) collective-permute-start(bf16[2048,256]{1,0:T(8,128)(2,1)} %get-tuple-element.63.hid_b), channel_id=1, source_target_pairs={{0,7},{1,0},{2,1},{3,2},{4,3},{5,4},{6,5},{7,6}} | collective-permute-start | bytes 3145736 | tf_op jit(solution)/shard_map/ppermute | solution.py:431
  125.5 8.8 %hidden_grad.1 = (bf16[2048,128]{1,0:T(8,128)(2,1)}, f32[8192,128]{1,0:T(8,128)S(1)}, f32[512,128]{1,0:T(8,128)S(1)}) custom-call(s32[2048]{0:T(1024)S(1)} %bitcast.33, f32[2048,128]{1,0:T(8,128)S(1)} %two_back_own.1.own, f32[1024,128]{1,0:T(8,128)} %collective-permute-done.4.ret_next, f32[1024,128]{1,0:T(8,128)} %collective-permute-done.5.ret_prev, ...), custom_call_target="tpu_custom_call" | custom-call | tf_op jit(solution)/shard_map/hidden_grad/pallas_call | solution.py:549
  134.2 2.6 %collective-permute-start.6 = (bf16[2048,128]{1,0:T(8,128)(2,1)}, bf16[2048,128]{1,0:T(8,128)(2,1)}, u32[]{:S(2)}, u32[]{:S(2)}) collective-permute-start(bf16[2048,128]{1,0:T(8,128)(2,1)} %get-tuple-element.62), channel_id=1, source_target_pairs={{0,7},{1,0},{2,1},{3,2},{4,3},{5,4},{6,5},{7,6}} | collective-permute-start | bytes 1572872 | tf_op jit(solution)/shard_map/ppermute | solution.py:431
  136.9 13.9 %one_back_own.1.own = f32[8192,128]{1,0:T(8,128)S(1)} custom-call(s32[12288]{0:T(1024)S(1)} %get-tuple-element.78.d4.frm, s32[12288]{0:T(1024)S(1)} %get-tuple-element.43.s4.to, s32[32]{0:T(128)S(1)} %get-tuple-element.93.cnt, f32[8192,128]{1,0:T(8,128)S(1)} %get-tuple-element.61.table, f32[8192,128]{1,0:T(8,128)S(1)} %broadcast_in_dim.62.w), custom_call_target="tpu_custom_call" | custom-call | flops 199999995904 | bytes 8000000 | tf_op jit(solution)/shard_map/one_back_own/pallas_call | solution.py:559
  150.8 6.9 %collective-permute-done.6.tn = bf16[2048,128]{1,0:T(8,128)(2,1)} collective-permute-done((bf16[2048,128]{1,0:T(8,128)(2,1)}, bf16[2048,128]{1,0:T(8,128)(2,1)}, u32[]{:S(2)}, u32[]{:S(2)}) %collective-permute-start.6) | collective-permute-done | bytes 524320 | tf_op jit(solution)/shard_map/ppermute | solution.py:431
  157.7 3.4 %collective-permute-done.9.tp = bf16[2048,128]{1,0:T(8,128)(2,1)} collective-permute-done((bf16[2048,128]{1,0:T(8,128)(2,1)}, bf16[2048,128]{1,0:T(8,128)(2,1)}, u32[]{:S(2)}, u32[]{:S(2)}) %collective-permute-start.9) | collective-permute-done | bytes 524320 | tf_op jit(solution)/shard_map/ppermute | solution.py:428
  161.1 15.9 %table_grad.1.g1 = f32[200,512]{1,0:T(8,128)S(1)} custom-call(s32[2048]{0:T(1024)S(1)} %bitcast.34, s32[13312]{0:T(1024)S(1)} %bitcast.36, f32[12288]{0:T(1024)S(1)} %bitcast.38, s32[13312]{0:T(1024)S(1)} %bitcast.35, f32[12288]{0:T(1024)S(1)} %bitcast.37, f32[8192,128]{1,0:T(8,128)S(1)} %one_back_own.1.own, bf16[2048,128]{1,0:T(8,128)(2,1)} %collective-permute-done.6.tn, ...), custom_call_target="tpu_custom_call" | custom-call | tf_op jit(solution)/shard_map/table_grad/pallas_call | solution.py:569
  177.0 15.6 %reduce.18 = (f32[200,512]{1,0:T(8,128)S(1)}, f32[512,128]{1,0:T(8,128)S(1)}, f32[8,128]{1,0:T(8,128)S(1)}) custom-call(f32[200,512]{1,0:T(8,128)S(1)} %table_grad.1.g1, f32[512,128]{1,0:T(8,128)S(1)} %get-tuple-element.64.g2, f32[8,128]{1,0:T(8,128)S(1)} %get-tuple-element.65.loss, f32[8,128]{1,0:T(8,128)S(1)} %get-tuple-element.55.count), custom_call_target="tpu_custom_call" | custom-call | tf_op jit(solution)/shard_map/reduce/pallas_call | solution.py:580
  193.2 0.8 copy.19
  (64 shorter events, 6.4 us)
Async XLA Ops:
  0.6 24.9 %copy-start.5 = (s32[2048]{0:T(1024)S(1)}, s32[2048]{0:T(1024)}, u32[]{:S(2)}) copy-start(s32[2048]{0:T(1024)} %param.17) | copy-start | bytes 24580
  0.6 24.9 %copy-start.7 = (f32[512,107]{0,1:T(8,128)S(1)}, f32[512,107]{0,1:T(8,128)}, u32[]{:S(2)}) copy-start(f32[512,107]{0,1:T(8,128)} %param.11) | copy-start | bytes 657412
  0.7 24.9 %copy-start.9 = (s32[2048]{0:T(1024)S(1)}, s32[2048]{0:T(1024)}, u32[]{:S(2)}) copy-start(s32[2048]{0:T(1024)} %param.16) | copy-start | bytes 24580
  7.8 17.7 %copy-start.2 = (s32[1,8,2,128]{3,1,2,0:T(8,128)}, s32[1,8,2,128]{3,1,2,0:T(8,128)S(1)}, u32[]{:S(2)}) copy-start(s32[1,8,2,128]{3,1,2,0:T(8,128)S(1)} %copy.23) | copy-start | bytes 24580
  7.9 0.7 copy-start.4
  8.6 18.8 %copy-start.6 = (f32[200,512]{1,0:T(8,128)S(1)}, f32[200,512]{1,0:T(8,128)}, u32[]{:S(2)}) copy-start(f32[200,512]{1,0:T(8,128)} %param.10) | copy-start | bytes 1228804
  22.8 20.3 %collective-permute-start = (bf16[1024,256]{1,0:T(8,128)(2,1)}, bf16[1024,256]{1,0:T(8,128)(2,1)}, u32[]{:S(2)}, u32[]{:S(2)}) collective-permute-start(bf16[1024,256]{1,0:T(8,128)(2,1)} %get-tuple-element.48), channel_id=1, source_target_pairs={{0,1},{1,2},{2,3},{3,4},{4,5},{5,6},{6,7},{7,0}} | collective-permute-start | bytes 1572872 | tf_op jit(solution)/shard_map/ppermute | solution.py:428
  23.2 19.8 %collective-permute-start.1 = (bf16[1024,256]{1,0:T(8,128)(2,1)}, bf16[1024,256]{1,0:T(8,128)(2,1)}, u32[]{:S(2)}, u32[]{:S(2)}) collective-permute-start(bf16[1024,256]{1,0:T(8,128)(2,1)} %get-tuple-element.49), channel_id=1, source_target_pairs={{0,7},{1,0},{2,1},{3,2},{4,3},{5,4},{6,5},{7,6}} | collective-permute-start | bytes 1572872 | tf_op jit(solution)/shard_map/ppermute | solution.py:431
  26.2 99.2 %copy-start = (bf16[128,512]{1,0:T(8,128)(2,1)}, bf16[128,512]{1,0:T(8,128)(2,1)S(1)}, u32[]{:S(2)}) copy-start(bf16[128,512]{1,0:T(8,128)(2,1)S(1)} %pad.4.w2t) | copy-start | bytes 393220
  27.4 15.6 %copy-start.3 = (s32[1,8,2,128]{3,1,2,0:T(8,128)S(1)}, s32[1,8,2,128]{3,1,2,0:T(8,128)}, u32[]{:S(2)}) copy-start(s32[1,8,2,128]{3,1,2,0:T(8,128)} %copy-done.2) | copy-start | bytes 24580
  59.2 77.7 %collective-permute-start.7 = (bf16[2048,256]{1,0:T(8,128)(2,1)}, bf16[2048,256]{1,0:T(8,128)(2,1)}, u32[]{:S(2)}, u32[]{:S(2)}) collective-permute-start(bf16[2048,256]{1,0:T(8,128)(2,1)} %get-tuple-element.59.hid_a), channel_id=1, source_target_pairs={{0,7},{1,0},{2,1},{3,2},{4,3},{5,4},{6,5},{7,6}} | collective-permute-start | bytes 3145736 | tf_op jit(solution)/shard_map/ppermute | solution.py:431
  60.6 90.2 %collective-permute-start.10 = (bf16[2048,256]{1,0:T(8,128)(2,1)}, bf16[2048,256]{1,0:T(8,128)(2,1)}, u32[]{:S(2)}, u32[]{:S(2)}) collective-permute-start(bf16[2048,256]{1,0:T(8,128)(2,1)} %get-tuple-element.59.hid_a), channel_id=1, source_target_pairs={{0,1},{1,2},{2,3},{3,4},{4,5},{5,6},{6,7},{7,0}} | collective-permute-start | bytes 3145736 | tf_op jit(solution)/shard_map/ppermute | solution.py:428
  60.6 30.6 %collective-permute-start.2 = (bf16[1024,128]{1,0:T(8,128)(2,1)}, bf16[1024,128]{1,0:T(8,128)(2,1)}, u32[]{:S(2)}, u32[]{:S(2)}) collective-permute-start(bf16[1024,128]{1,0:T(8,128)(2,1)} %get-tuple-element.52), channel_id=1, source_target_pairs={{0,1},{1,2},{2,3},{3,4},{4,5},{5,6},{6,7},{7,0}} | collective-permute-start | bytes 786440 | tf_op jit(solution)/shard_map/ppermute | solution.py:428
  60.6 30.6 %collective-permute-start.3 = (bf16[1024,128]{1,0:T(8,128)(2,1)}, bf16[1024,128]{1,0:T(8,128)(2,1)}, u32[]{:S(2)}, u32[]{:S(2)}) collective-permute-start(bf16[1024,128]{1,0:T(8,128)(2,1)} %get-tuple-element.53), channel_id=1, source_target_pairs={{0,7},{1,0},{2,1},{3,2},{4,3},{5,4},{6,5},{7,6}} | collective-permute-start | bytes 786440 | tf_op jit(solution)/shard_map/ppermute | solution.py:431
  63.2 27.9 %copy-start.8 = (s32[2048]{0:T(1024)S(1)}, s32[2048]{0:T(1024)}, u32[]{:S(2)}) copy-start(s32[2048]{0:T(1024)} %compare_select_fusion) | copy-start | bytes 24580
  109.0 16.4 %collective-permute-start.4 = (f32[1024,128]{1,0:T(8,128)}, f32[1024,128]{1,0:T(8,128)}, u32[]{:S(2)}, u32[]{:S(2)}) collective-permute-start(f32[1024,128]{1,0:T(8,128)} %get-tuple-element.57), channel_id=1, source_target_pairs={{0,7},{1,0},{2,1},{3,2},{4,3},{5,4},{6,5},{7,6}} | collective-permute-start | bytes 1572872 | tf_op jit(solution)/shard_map/ppermute | solution.py:431
  110.4 15.1 %collective-permute-start.5 = (f32[1024,128]{1,0:T(8,128)}, f32[1024,128]{1,0:T(8,128)}, u32[]{:S(2)}, u32[]{:S(2)}) collective-permute-start(f32[1024,128]{1,0:T(8,128)} %get-tuple-element.58), channel_id=1, source_target_pairs={{0,1},{1,2},{2,3},{3,4},{4,5},{5,6},{6,7},{7,0}} | collective-permute-start | bytes 1572872 | tf_op jit(solution)/shard_map/ppermute | solution.py:428
  122.2 35.5 %collective-permute-start.8 = (bf16[2048,256]{1,0:T(8,128)(2,1)}, bf16[2048,256]{1,0:T(8,128)(2,1)}, u32[]{:S(2)}, u32[]{:S(2)}) collective-permute-start(bf16[2048,256]{1,0:T(8,128)(2,1)} %get-tuple-element.63.hid_b), channel_id=1, source_target_pairs={{0,7},{1,0},{2,1},{3,2},{4,3},{5,4},{6,5},{7,6}} | collective-permute-start | bytes 3145736 | tf_op jit(solution)/shard_map/ppermute | solution.py:431
  125.4 35.7 %collective-permute-start.11 = (bf16[2048,256]{1,0:T(8,128)(2,1)}, bf16[2048,256]{1,0:T(8,128)(2,1)}, u32[]{:S(2)}, u32[]{:S(2)}) collective-permute-start(bf16[2048,256]{1,0:T(8,128)(2,1)} %get-tuple-element.63.hid_b), channel_id=1, source_target_pairs={{0,1},{1,2},{2,3},{3,4},{4,5},{5,6},{6,7},{7,0}} | collective-permute-start | bytes 3145736 | tf_op jit(solution)/shard_map/ppermute | solution.py:428
  134.2 23.4 %collective-permute-start.6 = (bf16[2048,128]{1,0:T(8,128)(2,1)}, bf16[2048,128]{1,0:T(8,128)(2,1)}, u32[]{:S(2)}, u32[]{:S(2)}) collective-permute-start(bf16[2048,128]{1,0:T(8,128)(2,1)} %get-tuple-element.62), channel_id=1, source_target_pairs={{0,7},{1,0},{2,1},{3,2},{4,3},{5,4},{6,5},{7,6}} | collective-permute-start | bytes 1572872 | tf_op jit(solution)/shard_map/ppermute | solution.py:431
  136.9 24.2 %collective-permute-start.9 = (bf16[2048,128]{1,0:T(8,128)(2,1)}, bf16[2048,128]{1,0:T(8,128)(2,1)}, u32[]{:S(2)}, u32[]{:S(2)}) collective-permute-start(bf16[2048,128]{1,0:T(8,128)(2,1)} %get-tuple-element.62), channel_id=1, source_target_pairs={{0,1},{1,2},{2,3},{3,4},{4,5},{5,6},{6,7},{7,0}} | collective-permute-start | bytes 1572872 | tf_op jit(solution)/shard_map/ppermute | solution.py:428
  136.9 24.2 %copy-start.1 = (bf16[128,512]{1,0:T(8,128)(2,1)S(1)}, bf16[128,512]{1,0:T(8,128)(2,1)}, u32[]{:S(2)}) copy-start(bf16[128,512]{1,0:T(8,128)(2,1)} %copy-done) | copy-start | bytes 393220

commit v10 on v9

--- a/solution.py
+++ b/solution.py
@@ -43,6 +43,16 @@
             ref[pl.ds(i * 64, 64), :] = jnp.zeros((64, LANES), F32)
 
     loop(rows // 64, body)
+
+
+def start_rows(first, refs):
+    def body(i):
+        at = pl.ds(i * 64, 64)
+        refs[0][at, :] = first[at, :]
+        for ref in refs[1:]:
+            ref[at, :] = jnp.zeros((64, LANES), F32)
+
+    loop(refs[0].shape[0] // 64, body)
 
 
 def sum_rows(out, refs):
@@ -182,7 +192,7 @@
 
 
 def one_halo_kernel(s4, d4, w, cnt, ids, y_own, x_prev, x_next, w1, w2t, hid_a, hid_b, t2, to_next, to_prev, table, picked, *accs):
-    zero_rows(accs)
+    start_rows(y_own, accs)
     half = x_prev.shape[0]
 
     def put(i):
@@ -193,7 +203,7 @@
 
     loop(half // BLOCK, put)
     edge_pass(s4, d4, w, cnt, table, accs, 4, 16, True)
-    sum_rows(accs[0], (y_own,) + accs)
+    sum_rows(accs[0], accs)
 
     def act(i):
         h = jnp.maximum(unspread(accs[0], i * BLOCK, BLOCK, 4), 0.0).astype(BF16)
@@ -335,7 +345,7 @@
 
 
 def table_grad_kernel(rows, ids, cn, wn, cp, wp, own, tn, han, hbn, tp, hap, hbp, w2t, x, g1, table, *accs):
-    zero_rows(accs)
+    start_rows(own, accs)
     g1[...] = jnp.zeros_like(g1)
 
     def fill(dt, hid_a, hid_b):
@@ -352,8 +362,8 @@
     peer_pass(ids, cp, wp, rows, 1, table, accs)
 
     def fold(i):
-        total = unspread(own, i * BLOCK, BLOCK, 4)
-        for acc in accs:
+        total = unspread(accs[0], i * BLOCK, BLOCK, 4)
+        for acc in accs[1:]:
             total = total + unspread(acc, i * BLOCK, BLOCK, 4)
         g1[...] += lax.dot_general(x[rows_at(i), :], total.astype(BF16), CONTRACT_ROWS, preferred_element_type=F32)
 

time: 195 us -> 195 us (level)
  no operation moved by 1% of the time
where the time goes in v10:
time: 195 us; the launch traced here: 194 us
  Pallas kernels  140 us (72%)
  waiting for transfers between devices  26.5 us (14%)
  starting transfers between devices  13.9 us (7%)
  local copies, waits for them, and re-layouts  8.19 us (4%)
  other arithmetic  5.26 us (3%)
    ppermute x6, waiting for transfers between devices, shift_next(): return lax.ppermute(a, GRAPH_AXIS, to_next)  19.5 us
    pallas_call x1, Pallas kernels, device_step(): pl.pallas_call(functools.partial(logits_kernel, classes), out_shape=[sds(...  17.6 us
    pallas_call x1, Pallas kernels, device_step(): pl.pallas_call(one_halo_kernel, out_shape=[sds((n_loc, f_hid // 2), BF16)...  16 us
    pallas_call x1, Pallas kernels, device_step(): pl.pallas_call(functools.partial(table_grad_kernel, rows), out_shape=sds(...  15.8 us
    pallas_call x1, Pallas kernels, device_step(): pl.pallas_call(functools.partial(reduce_kernel, num_dev), out_shape=[sds(...  15.6 us
    pallas_call x1, Pallas kernels, device_step(): pl.pallas_call(one_own_kernel, out_shape=sds((quad, LANES), F32), in_spec...  15.6 us
    pallas_call x1, Pallas kernels, device_step(): pl.pallas_call(wide_own_kernel, out_shape=sds((quad, LANES), F32), in_spe...  13.9 us
    ppermute x6, starting transfers between devices, shift_prev(): return lax.ppermute(a, GRAPH_AXIS, to_prev)  13.4 us
  transfers between devices with their start and end apart: 12, of which 3 were waited for; matrix products, arithmetic and copies ran while one was open for 1% of the time, Pallas kernels for 41%

profile of v10, /device:TPU:0, one launch (start us, length us, event | category | flops | bytes accessed | tf_op | source)
XLA Modules:
  0.0 194.5 jit_solution(17677918106869452619)
XLA Ops:
  2.8 4.2 %select_reduce_fusion = (s32[32,384]{1,0:T(8,128)S(1)}, f32[32,384]{1,0:T(8,128)S(1)}) fusion(f32[32,256]{1,0:T(8,128)S(1)} %pad_maximum_fusion, s32[32,256]{1,0:T(8,128)S(1)} %fusion.3, s32[32,256]{1,0:T(8,128)S(1)} %fusion.6), kind=kLoop, calls=%fused_computation | loop fusion | flops 15704064 | bytes 196608 | tf_op jit(solution)/shard_map/reduce | solution.py:463
  8.6 8.0 %lists.1 = (f32[8,128]{1,0:T(8,128)S(1)}, s32[104,128]{1,0:T(8,128)S(1)}, s32[104,128]{1,0:T(8,128)S(1)}, f32[96,128]{1,0:T(8,128)S(1)}, f32[96,128]{1,0:T(8,128)S(1)}) custom-call(s32[16,128]{1,0:T(8,128)S(1)} %bitcast.39, s32[104,128]{1,0:T(8,128)S(1)} %bitcast.30, f32[96,128]{1,0:T(8,128)S(1)} %reshape_reshape.3.wgt), custom_call_target="tpu_custom_call" | custom-call | tf_op jit(solution)/shard_map/lists/pallas_call | solution.py:484
  16.6 1.4 copy.16.x
  18.0 4.7 %halo_rows.1 = (bf16[1024,256]{1,0:T(8,128)(2,1)}, bf16[1024,256]{1,0:T(8,128)(2,1)}) custom-call(s32[2048]{0:T(1024)S(1)} %bitcast.31, bf16[2048,200]{1,0:T(8,128)(2,1)S(1)} %copy.16.x), custom_call_target="tpu_custom_call" | custom-call | tf_op jit(solution)/shard_map/halo_rows/pallas_call | solution.py:496
  23.2 2.2 %collective-permute-start.1 = (bf16[1024,256]{1,0:T(8,128)(2,1)}, bf16[1024,256]{1,0:T(8,128)(2,1)}, u32[]{:S(2)}, u32[]{:S(2)}) collective-permute-start(bf16[1024,256]{1,0:T(8,128)(2,1)} %get-tuple-element.49), channel_id=1, source_target_pairs={{0,7},{1,0},{2,1},{3,2},{4,3},{5,4},{6,5},{7,6}} | collective-permute-start | bytes 1572872 | tf_op jit(solution)/shard_map/ppermute | solution.py:441
  26.2 1.1 broadcast_in_dim.62.w
  27.4 15.6 %one_own.1.y_own = f32[8192,128]{1,0:T(8,128)S(1)} custom-call(s32[12288]{0:T(1024)S(1)} %get-tuple-element.43.s4.to, s32[12288]{0:T(1024)S(1)} %get-tuple-element.78.d4.frm, s32[32]{0:T(128)S(1)} %get-tuple-element.93.cnt, bf16[2048,200]{1,0:T(8,128)(2,1)S(1)} %copy.16.x, bf16[200,512]{1,0:T(8,128)(2,1)S(1)} %convert_element_type.30.w1, ...), custom_call_target="tpu_custom_call" | custom-call | flops 199999995904 | bytes 8000000 | tf_op jit(solution)/shard_map/one_own/pallas_call | solution.py:511
  43.1 16.0 %one_halo.1 = (bf16[2048,256]{1,0:T(8,128)(2,1)}, bf16[2048,256]{1,0:T(8,128)(2,1)}, f32[2048,128]{1,0:T(8,128)S(1)}, bf16[1024,128]{1,0:T(8,128)(2,1)}, bf16[1024,128]{1,0:T(8,128)(2,1)}) custom-call(s32[12288]{0:T(1024)S(1)} %get-tuple-element.43.s4.to, s32[12288]{0:T(1024)S(1)} %get-tuple-element.78.d4.frm, f32[12288]{0:T(1024)S(1)} %reshape.170.w, ...), custom_call_target="tpu_custom_call" | custom-call | tf_op jit(solution)/shard_map/one_halo/pallas_call | solution.py:521
  59.1 1.4 collective-permute-start.7
  60.4 2.7 %collective-permute-start.3 = (bf16[1024,128]{1,0:T(8,128)(2,1)}, bf16[1024,128]{1,0:T(8,128)(2,1)}, u32[]{:S(2)}, u32[]{:S(2)}) collective-permute-start(bf16[1024,128]{1,0:T(8,128)(2,1)} %get-tuple-element.53), channel_id=1, source_target_pairs={{0,7},{1,0},{2,1},{3,2},{4,3},{5,4},{6,5},{7,6}} | collective-permute-start | bytes 786440 | tf_op jit(solution)/shard_map/ppermute | solution.py:441
  63.1 11.8 %two_own.1.z_own = f32[2048,128]{1,0:T(8,128)S(1)} custom-call(s32[12288]{0:T(1024)S(1)} %get-tuple-element.84.frm.s.to, s32[12288]{0:T(1024)S(1)} %get-tuple-element.77.to.d.frm, s32[32]{0:T(128)S(1)} %get-tuple-element.93.cnt, f32[2048,128]{1,0:T(8,128)S(1)} %get-tuple-element.51.table, f32[8192,128]{1,0:T(8,128)S(1)} %broadcast_in_dim.62.w), custom_call_target="tpu_custom_call" | custom-call | flops 199999995904 | bytes 8000000 | tf_op jit(solution)/shard_map/two_own/pallas_call | solution.py:543
  74.9 16.1 %collective-permute-done.2.t_prev = bf16[1024,128]{1,0:T(8,128)(2,1)} collective-permute-done((bf16[1024,128]{1,0:T(8,128)(2,1)}, bf16[1024,128]{1,0:T(8,128)(2,1)}, u32[]{:S(2)}, u32[]{:S(2)}) %collective-permute-start.2) | collective-permute-done | bytes 262176 | tf_op jit(solution)/shard_map/ppermute | solution.py:438
  91.4 17.6 %logits.1 = (f32[2048,128]{1,0:T(8,128)S(1)}, f32[1024,128]{1,0:T(8,128)}, f32[1024,128]{1,0:T(8,128)}, f32[8,128]{1,0:T(8,128)S(1)}) custom-call(s32[12288]{0:T(1024)S(1)} %get-tuple-element.84.frm.s.to, s32[12288]{0:T(1024)S(1)} %get-tuple-element.77.to.d.frm, f32[12288]{0:T(1024)S(1)} %reshape.170.w, s32[32]{0:T(128)S(1)} %get-tuple-element.75.cnt, ...), custom_call_target="tpu_custom_call" | custom-call | tf_op jit(solution)/shard_map/logits/pallas_call | solution.py:545
  108.9 1.3 collective-permute-start.4
  110.2 11.8 %two_back_own.1.own = f32[2048,128]{1,0:T(8,128)S(1)} custom-call(s32[12288]{0:T(1024)S(1)} %get-tuple-element.77.to.d.frm, s32[12288]{0:T(1024)S(1)} %get-tuple-element.84.frm.s.to, s32[32]{0:T(128)S(1)} %get-tuple-element.93.cnt, f32[2048,128]{1,0:T(8,128)S(1)} %get-tuple-element.56.table, f32[8192,128]{1,0:T(8,128)S(1)} %broadcast_in_dim.62.w), custom_call_target="tpu_custom_call" | custom-call | flops 199999995904 | bytes 8000000 | tf_op jit(solution)/shard_map/two_back_own/pallas_call | solution.py:558
  122.1 3.2 %collective-permute-start.8 = (bf16[2048,256]{1,0:T(8,128)(2,1)}, bf16[2048,256]{1,0:T(8,128)(2,1)}, u32[]{:S(2)}, u32[]{:S(2)}) collective-permute-start(bf16[2048,256]{1,0:T(8,128)(2,1)} %get-tuple-element.63.hid_b), channel_id=1, source_target_pairs={{0,7},{1,0},{2,1},{3,2},{4,3},{5,4},{6,5},{7,6}} | collective-permute-start | bytes 3145736 | tf_op jit(solution)/shard_map/ppermute | solution.py:441
  125.3 8.8 %hidden_grad.1 = (bf16[2048,128]{1,0:T(8,128)(2,1)}, f32[8192,128]{1,0:T(8,128)S(1)}, f32[512,128]{1,0:T(8,128)S(1)}) custom-call(s32[2048]{0:T(1024)S(1)} %bitcast.33, f32[2048,128]{1,0:T(8,128)S(1)} %two_back_own.1.own, f32[1024,128]{1,0:T(8,128)} %collective-permute-done.4.ret_next, f32[1024,128]{1,0:T(8,128)} %collective-permute-done.5.ret_prev, ...), custom_call_target="tpu_custom_call" | custom-call | tf_op jit(solution)/shard_map/hidden_grad/pallas_call | solution.py:559
  134.1 2.6 %collective-permute-start.6 = (bf16[2048,128]{1,0:T(8,128)(2,1)}, bf16[2048,128]{1,0:T(8,128)(2,1)}, u32[]{:S(2)}, u32[]{:S(2)}) collective-permute-start(bf16[2048,128]{1,0:T(8,128)(2,1)} %get-tuple-element.62), channel_id=1, source_target_pairs={{0,7},{1,0},{2,1},{3,2},{4,3},{5,4},{6,5},{7,6}} | collective-permute-start | bytes 1572872 | tf_op jit(solution)/shard_map/ppermute | solution.py:441
  136.7 13.9 %one_back_own.1.own = f32[8192,128]{1,0:T(8,128)S(1)} custom-call(s32[12288]{0:T(1024)S(1)} %get-tuple-element.78.d4.frm, s32[12288]{0:T(1024)S(1)} %get-tuple-element.43.s4.to, s32[32]{0:T(128)S(1)} %get-tuple-element.93.cnt, f32[8192,128]{1,0:T(8,128)S(1)} %get-tuple-element.61.table, f32[8192,128]{1,0:T(8,128)S(1)} %broadcast_in_dim.62.w), custom_call_target="tpu_custom_call" | custom-call | flops 199999995904 | bytes 8000000 | tf_op jit(solution)/shard_map/one_back_own/pallas_call | solution.py:569
  150.6 6.9 %collective-permute-done.6.tn = bf16[2048,128]{1,0:T(8,128)(2,1)} collective-permute-done((bf16[2048,128]{1,0:T(8,128)(2,1)}, bf16[2048,128]{1,0:T(8,128)(2,1)}, u32[]{:S(2)}, u32[]{:S(2)}) %collective-permute-start.6) | collective-permute-done | bytes 524320 | tf_op jit(solution)/shard_map/ppermute | solution.py:441
  157.6 3.4 %collective-permute-done.9.tp = bf16[2048,128]{1,0:T(8,128)(2,1)} collective-permute-done((bf16[2048,128]{1,0:T(8,128)(2,1)}, bf16[2048,128]{1,0:T(8,128)(2,1)}, u32[]{:S(2)}, u32[]{:S(2)}) %collective-permute-start.9) | collective-permute-done | bytes 524320 | tf_op jit(solution)/shard_map/ppermute | solution.py:438
  161.0 15.8 %table_grad.1.g1 = f32[200,512]{1,0:T(8,128)S(1)} custom-call(s32[2048]{0:T(1024)S(1)} %bitcast.34, s32[13312]{0:T(1024)S(1)} %bitcast.36, f32[12288]{0:T(1024)S(1)} %bitcast.38, s32[13312]{0:T(1024)S(1)} %bitcast.35, f32[12288]{0:T(1024)S(1)} %bitcast.37, f32[8192,128]{1,0:T(8,128)S(1)} %one_back_own.1.own, bf16[2048,128]{1,0:T(8,128)(2,1)} %collective-permute-done.6.tn, ...), custom_call_target="tpu_custom_call" | custom-call | tf_op jit(solution)/shard_map/table_grad/pallas_call | solution.py:579
  176.7 15.6 %reduce.18 = (f32[200,512]{1,0:T(8,128)S(1)}, f32[512,128]{1,0:T(8,128)S(1)}, f32[8,128]{1,0:T(8,128)S(1)}) custom-call(f32[200,512]{1,0:T(8,128)S(1)} %table_grad.1.g1, f32[512,128]{1,0:T(8,128)S(1)} %get-tuple-element.64.g2, f32[8,128]{1,0:T(8,128)S(1)} %get-tuple-element.65.loss, f32[8,128]{1,0:T(8,128)S(1)} %get-tuple-element.55.count), custom_call_target="tpu_custom_call" | custom-call | tf_op jit(solution)/shard_map/reduce/pallas_call | solution.py:590
  192.9 0.8 copy.19
  (64 shorter events, 6.4 us)
Async XLA Ops:
  0.6 24.9 %copy-start.5 = (s32[2048]{0:T(1024)S(1)}, s32[2048]{0:T(1024)}, u32[]{:S(2)}) copy-start(s32[2048]{0:T(1024)} %param.17) | copy-start | bytes 24580
  0.6 24.9 %copy-start.7 = (f32[512,107]{0,1:T(8,128)S(1)}, f32[512,107]{0,1:T(8,128)}, u32[]{:S(2)}) copy-start(f32[512,107]{0,1:T(8,128)} %param.11) | copy-start | bytes 657412
  0.7 24.9 %copy-start.9 = (s32[2048]{0:T(1024)S(1)}, s32[2048]{0:T(1024)}, u32[]{:S(2)}) copy-start(s32[2048]{0:T(1024)} %param.16) | copy-start | bytes 24580
  7.8 17.7 %copy-start.2 = (s32[1,8,2,128]{3,1,2,0:T(8,128)}, s32[1,8,2,128]{3,1,2,0:T(8,128)S(1)}, u32[]{:S(2)}) copy-start(s32[1,8,2,128]{3,1,2,0:T(8,128)S(1)} %copy.23) | copy-start | bytes 24580
  7.9 0.7 copy-start.4
  8.6 18.8 %copy-start.6 = (f32[200,512]{1,0:T(8,128)S(1)}, f32[200,512]{1,0:T(8,128)}, u32[]{:S(2)}) copy-start(f32[200,512]{1,0:T(8,128)} %param.10) | copy-start | bytes 1228804
  22.8 20.3 %collective-permute-start = (bf16[1024,256]{1,0:T(8,128)(2,1)}, bf16[1024,256]{1,0:T(8,128)(2,1)}, u32[]{:S(2)}, u32[]{:S(2)}) collective-permute-start(bf16[1024,256]{1,0:T(8,128)(2,1)} %get-tuple-element.48), channel_id=1, source_target_pairs={{0,1},{1,2},{2,3},{3,4},{4,5},{5,6},{6,7},{7,0}} | collective-permute-start | bytes 1572872 | tf_op jit(solution)/shard_map/ppermute | solution.py:438
  23.2 19.8 %collective-permute-start.1 = (bf16[1024,256]{1,0:T(8,128)(2,1)}, bf16[1024,256]{1,0:T(8,128)(2,1)}, u32[]{:S(2)}, u32[]{:S(2)}) collective-permute-start(bf16[1024,256]{1,0:T(8,128)(2,1)} %get-tuple-element.49), channel_id=1, source_target_pairs={{0,7},{1,0},{2,1},{3,2},{4,3},{5,4},{6,5},{7,6}} | collective-permute-start | bytes 1572872 | tf_op jit(solution)/shard_map/ppermute | solution.py:441
  26.2 99.1 %copy-start = (bf16[128,512]{1,0:T(8,128)(2,1)}, bf16[128,512]{1,0:T(8,128)(2,1)S(1)}, u32[]{:S(2)}) copy-start(bf16[128,512]{1,0:T(8,128)(2,1)S(1)} %pad.4.w2t) | copy-start | bytes 393220
  27.4 15.6 %copy-start.3 = (s32[1,8,2,128]{3,1,2,0:T(8,128)S(1)}, s32[1,8,2,128]{3,1,2,0:T(8,128)}, u32[]{:S(2)}) copy-start(s32[1,8,2,128]{3,1,2,0:T(8,128)} %copy-done.2) | copy-start | bytes 24580
  59.1 77.7 %collective-permute-start.7 = (bf16[2048,256]{1,0:T(8,128)(2,1)}, bf16[2048,256]{1,0:T(8,128)(2,1)}, u32[]{:S(2)}, u32[]{:S(2)}) collective-permute-start(bf16[2048,256]{1,0:T(8,128)(2,1)} %get-tuple-element.59.hid_a), channel_id=1, source_target_pairs={{0,7},{1,0},{2,1},{3,2},{4,3},{5,4},{6,5},{7,6}} | collective-permute-start | bytes 3145736 | tf_op jit(solution)/shard_map/ppermute | solution.py:441
  60.4 90.2 %collective-permute-start.10 = (bf16[2048,256]{1,0:T(8,128)(2,1)}, bf16[2048,256]{1,0:T(8,128)(2,1)}, u32[]{:S(2)}, u32[]{:S(2)}) collective-permute-start(bf16[2048,256]{1,0:T(8,128)(2,1)} %get-tuple-element.59.hid_a), channel_id=1, source_target_pairs={{0,1},{1,2},{2,3},{3,4},{4,5},{5,6},{6,7},{7,0}} | collective-permute-start | bytes 3145736 | tf_op jit(solution)/shard_map/ppermute | solution.py:438
  60.4 30.6 %collective-permute-start.2 = (bf16[1024,128]{1,0:T(8,128)(2,1)}, bf16[1024,128]{1,0:T(8,128)(2,1)}, u32[]{:S(2)}, u32[]{:S(2)}) collective-permute-start(bf16[1024,128]{1,0:T(8,128)(2,1)} %get-tuple-element.52), channel_id=1, source_target_pairs={{0,1},{1,2},{2,3},{3,4},{4,5},{5,6},{6,7},{7,0}} | collective-permute-start | bytes 786440 | tf_op jit(solution)/shard_map/ppermute | solution.py:438
  60.4 30.6 %collective-permute-start.3 = (bf16[1024,128]{1,0:T(8,128)(2,1)}, bf16[1024,128]{1,0:T(8,128)(2,1)}, u32[]{:S(2)}, u32[]{:S(2)}) collective-permute-start(bf16[1024,128]{1,0:T(8,128)(2,1)} %get-tuple-element.53), channel_id=1, source_target_pairs={{0,7},{1,0},{2,1},{3,2},{4,3},{5,4},{6,5},{7,6}} | collective-permute-start | bytes 786440 | tf_op jit(solution)/shard_map/ppermute | solution.py:441
  63.1 27.9 %copy-start.8 = (s32[2048]{0:T(1024)S(1)}, s32[2048]{0:T(1024)}, u32[]{:S(2)}) copy-start(s32[2048]{0:T(1024)} %compare_select_fusion) | copy-start | bytes 24580
  108.9 16.4 %collective-permute-start.4 = (f32[1024,128]{1,0:T(8,128)}, f32[1024,128]{1,0:T(8,128)}, u32[]{:S(2)}, u32[]{:S(2)}) collective-permute-start(f32[1024,128]{1,0:T(8,128)} %get-tuple-element.57), channel_id=1, source_target_pairs={{0,7},{1,0},{2,1},{3,2},{4,3},{5,4},{6,5},{7,6}} | collective-permute-start | bytes 1572872 | tf_op jit(solution)/shard_map/ppermute | solution.py:441
  110.2 15.1 %collective-permute-start.5 = (f32[1024,128]{1,0:T(8,128)}, f32[1024,128]{1,0:T(8,128)}, u32[]{:S(2)}, u32[]{:S(2)}) collective-permute-start(f32[1024,128]{1,0:T(8,128)} %get-tuple-element.58), channel_id=1, source_target_pairs={{0,1},{1,2},{2,3},{3,4},{4,5},{5,6},{6,7},{7,0}} | collective-permute-start | bytes 1572872 | tf_op jit(solution)/shard_map/ppermute | solution.py:438
  122.1 35.5 %collective-permute-start.8 = (bf16[2048,256]{1,0:T(8,128)(2,1)}, bf16[2048,256]{1,0:T(8,128)(2,1)}, u32[]{:S(2)}, u32[]{:S(2)}) collective-permute-start(bf16[2048,256]{1,0:T(8,128)(2,1)} %get-tuple-element.63.hid_b), channel_id=1, source_target_pairs={{0,7},{1,0},{2,1},{3,2},{4,3},{5,4},{6,5},{7,6}} | collective-permute-start | bytes 3145736 | tf_op jit(solution)/shard_map/ppermute | solution.py:441
  125.3 35.7 %collective-permute-start.11 = (bf16[2048,256]{1,0:T(8,128)(2,1)}, bf16[2048,256]{1,0:T(8,128)(2,1)}, u32[]{:S(2)}, u32[]{:S(2)}) collective-permute-start(bf16[2048,256]{1,0:T(8,128)(2,1)} %get-tuple-element.63.hid_b), channel_id=1, source_target_pairs={{0,1},{1,2},{2,3},{3,4},{4,5},{5,6},{6,7},{7,0}} | collective-permute-start | bytes 3145736 | tf_op jit(solution)/shard_map/ppermute | solution.py:438
  134.1 23.4 %collective-permute-start.6 = (bf16[2048,128]{1,0:T(8,128)(2,1)}, bf16[2048,128]{1,0:T(8,128)(2,1)}, u32[]{:S(2)}, u32[]{:S(2)}) collective-permute-start(bf16[2048,128]{1,0:T(8,128)(2,1)} %get-tuple-element.62), channel_id=1, source_target_pairs={{0,7},{1,0},{2,1},{3,2},{4,3},{5,4},{6,5},{7,6}} | collective-permute-start | bytes 1572872 | tf_op jit(solution)/shard_map/ppermute | solution.py:441
  136.7 24.2 %collective-permute-start.9 = (bf16[2048,128]{1,0:T(8,128)(2,1)}, bf16[2048,128]{1,0:T(8,128)(2,1)}, u32[]{:S(2)}, u32[]{:S(2)}) collective-permute-start(bf16[2048,128]{1,0:T(8,128)(2,1)} %get-tuple-element.62), channel_id=1, source_target_pairs={{0,1},{1,2},{2,3},{3,4},{4,5},{5,6},{6,7},{7,0}} | collective-permute-start | bytes 1572872 | tf_op jit(solution)/shard_map/ppermute | solution.py:438
  136.7 24.2 %copy-start.1 = (bf16[128,512]{1,0:T(8,128)(2,1)S(1)}, bf16[128,512]{1,0:T(8,128)(2,1)}, u32[]{:S(2)}) copy-start(bf16[128,512]{1,0:T(8,128)(2,1)} %copy-done) | copy-start | bytes 393220
